TPU v7x, 512 devices: a whole 4x4x16 slice. The times are simulated.
512 devices in a mesh: expert: 64 (over x, z), tensor: 8 (over y, core).
Axes of the slice: x: 4, y: 4, z: 16, core: 2. Of those that a mesh axis runs over, the one named last changes fastest.
Arguments:
- grad_out: bfloat16 [1024, 3584], P('expert'), may hold values from -1.5 to 1.5
- expert_ids: int32 [1024, 8], P('expert'), may hold values from 0 to 63, all different within a row; in each aligned block of 16 rows (0 to 15, 16 to 31, ...) at most 4 rows name the same one
- gate_values: float32 [1024, 8], P('expert'), may hold values from 0.05 to 0.6
- w_gate_up: bfloat16 [64, 2, 3584, 1024], P('expert', None, None, 'tensor'), may hold values from -0.09375 to 0.09375
- w_down: bfloat16 [64, 1024, 3584], P('expert', 'tensor'), may hold values from -0.1875 to 0.1875
- saved_routed: bfloat16 [64, 2, 256, 1024], P('expert', None, None, 'tensor'), may hold values from -6 to 6
- shared_gate_up: bfloat16 [2, 3584, 1024], P(None, 'expert', 'tensor'), may hold values from -0.09375 to 0.09375
- shared_down: bfloat16 [1024, 3584], P('tensor', 'expert'), may hold values from -0.1875 to 0.1875
- saved_shared: bfloat16 [2, 1024, 1024], P(None, 'expert', 'tensor'), may hold values from -6 to 6
Outputs:
- grad_in: bfloat16 [1024, 3584], P('expert', 'tensor')
- grad_gates: float32 [1024, 8], P('expert')
Inputs may be any that keep to these rules, and one draw needn't show every extreme that they name: `expert_ids`: each row names 8 different experts. Among the 16 rows of one index of expert (aligned blocks of rows), no expert is named by more than 4 rows, and in some block one expert is named by exactly 4 rows.
All inputs are finite; a program needn't handle non-finite values.
Results may differ from a plain program's by a relative error of at most 0.015.
Values may be sent and summed in bfloat16 or wider, within the bound.
No kernel may reach another device: no remote copies, remote signals or barrier semaphores. Data moves between devices by JAX's collectives and lax.ppermute only.
A program may use at most 64 MiB of HBM per device.

v0:
```python
import jax
import jax.numpy as jnp
from jax import lax
from jax.sharding import Mesh
from jax.sharding import PartitionSpec as P

EXPERT = ("expert_0", "expert_1")


def from_everyone(array, axis):
    peers = lax.axis_size(axis)
    return lax.all_to_all(
        jnp.broadcast_to(array[None], (peers, *array.shape)), axis, 0, 0, tiled=True
    )


def joined_along(blocks, dim):
    lengths = list(blocks.shape[1:])
    lengths[dim] *= blocks.shape[0]
    return jnp.moveaxis(blocks, 0, dim).reshape(lengths)


def collect(array, axis, dim):
    blocks = from_everyone(array, axis)
    return joined_along(blocks, dim)


def gather_in_order(array, axes, sequence):
    blocks = array[None]
    for k in sequence:
        blocks = lax.all_gather(blocks, axes[k], axis=0, tiled=True)
    block = [lax.axis_size(axes[k]) for k in reversed(sequence)]
    blocks = blocks.reshape(*block, *array.shape)
    turned = sorted(range(len(sequence)), key=lambda place: sequence[len(sequence) - 1 - place])
    return blocks.transpose(*turned, *range(len(sequence), blocks.ndim)).reshape(-1, *array.shape)


def whole_of(array, axes, sequence, dim):
    return joined_along(gather_in_order(array, axes, sequence), dim)


def in_blocks(array, dim, peers):
    before, after = (array.shape[:dim], array.shape[dim + 1 :])
    return jnp.moveaxis(array.reshape(*before, peers, -1, *after), dim, 0)


def sum_at_owner(array, axis, dim):
    peers = lax.axis_size(axis)
    blocks = lax.all_to_all(in_blocks(array, dim, peers), axis, 0, 0, tiled=True)
    return jnp.sum(blocks.astype(jnp.float32), axis=0)


def side_by_side(arrays, axis, split_dim, concat_dim, along):
    columns = [a.reshape(*a.shape[:along], -1) for a in arrays]
    both = jnp.concatenate(columns, axis=along)
    whole, at, finished = (
        lax.all_to_all(both, axis, split_axis=split_dim, concat_axis=concat_dim, tiled=True),
        0,
        [],
    )
    for a, column in zip(arrays, columns):
        piece = whole[..., at : at + column.shape[along]]
        finished.append(piece.reshape(*piece.shape[:along], *a.shape[along:]))
        at += column.shape[along]
    return tuple(finished)


def taken_together(array, axis):
    everything = from_everyone(array, axis)
    return jnp.sum(everything, axis=0)


def contract_last(left_side, right_side):
    return lax.dot_general(
        left_side, right_side, (((1,), (1,)), ((), ())), preferred_element_type=jnp.float32
    )


def swiglu_grads(back_grad, saved_gate, saved_up):
    pre_gate = saved_gate.astype(jnp.float32)
    pre_up = saved_up.astype(jnp.float32)
    sigmoid = jax.nn.sigmoid(pre_gate)
    grad_gate = (back_grad * pre_up * sigmoid * (1.0 + pre_gate * (1.0 - sigmoid))).astype(
        jnp.bfloat16
    )
    grad_up = (back_grad * pre_gate * sigmoid).astype(jnp.bfloat16)
    return (grad_gate, grad_up)


def gate_mixture(back_grad, saved_gate, saved_up):
    pre_gate = saved_gate.astype(jnp.float32)
    pre_up = saved_up.astype(jnp.float32)
    sigmoid = jax.nn.sigmoid(pre_gate)
    return back_grad * pre_gate * sigmoid * pre_up


def per_device(
    grad_out,
    expert_ids,
    gate_values,
    w_gate_up,
    w_down,
    saved_routed,
    shared_gate_up,
    shared_down,
    saved_shared,
):
    experts = lax.axis_size(EXPERT)
    tensors = lax.axis_size("tensor")
    tokens, features = grad_out.shape
    choose = expert_ids.shape[1]
    slot_count = saved_routed.shape[2]
    capacity = slot_count // experts
    flat_ids = expert_ids.reshape(-1)
    onehot = (flat_ids[:, None] == jnp.arange(experts, dtype=jnp.int32)[None, :]).astype(jnp.int32)
    earlier = jnp.cumsum(onehot, axis=0) - onehot
    position = jnp.sum(earlier * onehot, axis=1)
    slot_index = flat_ids * capacity + position
    pair_token = jnp.arange(tokens * choose, dtype=jnp.int32) // choose
    source_row = jnp.full((slot_count,), tokens, jnp.int32).at[slot_index].set(pair_token)
    padded = jnp.concatenate([grad_out, jnp.zeros((1, features), grad_out.dtype)], axis=0)
    send_rows = padded[source_row].reshape(experts, capacity, features)
    column_share = features // tensors
    column_part = lax.dynamic_slice_in_dim(
        send_rows, lax.axis_index("tensor") * column_share, column_share, 2
    )
    arrived_part = lax.all_to_all(column_part, EXPERT, split_axis=0, concat_axis=0, tiled=True)
    arrived = collect(arrived_part, "tensor", 2)
    slot_rows = arrived.reshape(slot_count, features)
    back_grad = contract_last(slot_rows, w_down[0])
    grad_gate, grad_up = swiglu_grads(back_grad, saved_routed[0, 0], saved_routed[0, 1])
    gate_mix = gate_mixture(back_grad, saved_routed[0, 0], saved_routed[0, 1])
    row_terms = contract_last(grad_gate, w_gate_up[0, 0]) + contract_last(grad_up, w_gate_up[0, 1])
    gate_terms = jnp.sum(gate_mix, axis=1).astype(jnp.bfloat16)
    shared_back = contract_last(grad_out, whole_of(shared_down, EXPERT, (0, 1), 1))
    shared_gate, shared_up = swiglu_grads(shared_back, saved_shared[0], saved_shared[1])
    weight_piece = whole_of(shared_gate_up, EXPERT, (0, 1), 1)
    shared_term = contract_last(shared_gate, weight_piece[0]) + contract_last(
        shared_up, weight_piece[1]
    )
    reduced = sum_at_owner(
        row_terms.reshape(experts, capacity, features).astype(jnp.bfloat16), "tensor", 2
    )
    returned, gate_back = tuple(
        (
            part.astype(jnp.float32)
            for part in side_by_side(
                (
                    reduced.astype(jnp.bfloat16),
                    gate_terms.astype(jnp.float32).reshape(experts, capacity).astype(jnp.bfloat16),
                ),
                EXPERT,
                0,
                0,
                2,
            )
        )
    )
    narrow_width = returned.shape[2]
    picked = returned.reshape(slot_count, narrow_width)[slot_index].reshape(
        tokens, choose, narrow_width
    )
    routed = jnp.einsum("tkd,tk->td", picked, gate_values)
    summed = routed + sum_at_owner(shared_term.astype(jnp.bfloat16), "tensor", 1)
    gate_pairs = (
        gate_back.reshape(slot_count)[slot_index].reshape(tokens, choose).astype(jnp.float32)
    )
    grad_gates = taken_together(gate_pairs, "tensor")
    return (summed.astype(jnp.bfloat16), grad_gates)


def solution(mesh):
    finer = Mesh(
        mesh.devices.reshape(4, 16, mesh.shape["tensor"]), ("expert_0", "expert_1", "tensor")
    )
    placed = (
        P(EXPERT, None),
        P(EXPERT, None),
        P(EXPERT, None),
        P(EXPERT, None, None, "tensor"),
        P(EXPERT, "tensor", None),
        P(EXPERT, None, None, "tensor"),
        P(None, EXPERT, "tensor"),
        P("tensor", EXPERT),
        P(None, EXPERT, "tensor"),
    )
    return jax.shard_map(
        per_device,
        mesh=finer,
        in_specs=placed,
        out_specs=(P(EXPERT, "tensor"), P(EXPERT, None)),
        check_vma=False,
    )
```

profile of v0, /device:TPU:1, one launch (start us, length us, event | category | flops | bytes accessed | tf_op | source)
XLA Modules:
  0.0 212.9 jit_solution(13023604714832037073)
XLA Ops:
  11.4 1.7 gather_fusion
  13.1 1.5 reshape.99
  15.8 38.0 %all_to_all.30 = bf16[64,4,448]{2,1,0:T(4,128)(2,1)S(1)} all-to-all(bf16[64,4,448]{2,1,0:T(4,128)(2,1)S(1)} %constant_dynamic-slice_fusion), channel_id=1, replica_groups=mesh['expert_0'=4,'expert_1'=16,'tensor'=8] {'expert_0','expert_1'}, dimensions={0} | all-to-all | bytes 458752 | tf_op jit(solution)/shard_map/all_to_all | solution.py:127
  53.7 1.9 broadcast_in_dim.32
  55.6 7.5 %all-to-all-start.1 = ((bf16[8,64,4,448]{3,2,1,0:T(4,128)(2,1)}), bf16[8,64,4,448]{3,2,1,0:T(4,128)(2,1)S(1)}, u32[]{:S(2)}, u32[]{:S(2)}) async-start(bf16[8,64,4,448]{3,2,1,0:T(4,128)(2,1)} %broadcast_in_dim.32), calls=%async_computation.1 | async-start | bytes 4194304 | tf_op jit(solution)/shard_map/all_to_all | solution.py:12
  63.1 10.5 %all-gather.1 = bf16[8,56,128]{2,1,0:T(8,128)(2,1)} all-gather(bf16[2,56,128]{2,1,0:T(8,128)(2,1)S(1)} %copy-done.4), channel_id=3, replica_groups=mesh['expert_0'=4,'expert_1'=16,'tensor'=8] {'expert_0'}, dimensions={0}, use_global_device_ids=true | all-gather | bytes 143360 | tf_op jit(solution)/shard_map/all_gather | solution.py:31
  73.9 9.0 %all-gather = bf16[512,56]{0,1:T(8,128)(2,1)S(1)} all-gather(bf16[128,56]{0,1:T(8,128)(2,1)S(1)} %copy-done.5), channel_id=2, replica_groups=mesh['expert_0'=4,'expert_1'=16,'tensor'=8] {'expert_0'}, dimensions={0}, use_global_device_ids=true | all-gather | bytes 71680 | tf_op jit(solution)/shard_map/all_gather | solution.py:31
  82.9 6.4 %all-to-all-done.1 = bf16[8,64,4,448]{3,2,1,0:T(4,128)(2,1)S(1)} async-done(((bf16[8,64,4,448]{3,2,1,0:T(4,128)(2,1)}), bf16[8,64,4,448]{3,2,1,0:T(4,128)(2,1)S(1)}, u32[]{:S(2)}, u32[]{:S(2)}) %all-to-all-start.1) | async-done | bytes 1835040 | tf_op jit(solution)/shard_map/all_to_all | solution.py:12
  89.3 3.6 %copy.52 = bf16[64,4,8,448]{3,2,1,0:T(8,128)(2,1)} copy(bf16[64,4,8,448]{3,1,0,2:T(4,128)(2,1)S(1)} %bitcast.103) | data formatting | bytes 3670016 | tf_op jit(solution)/shard_map/transpose | solution.py:20
  92.9 3.7 %reshape_reshape.3 = bf16[256,3584]{1,0:T(8,128)(2,1)S(1)} reshape(bf16[64,4,8,448]{3,2,1,0:T(8,128)(2,1)} %copy.52) | data formatting | bytes 3670016 | tf_op jit(solution)/shard_map/reshape;reshape | solution.py:129
  98.8 2.0 fusion
  100.8 3.9 %convert_element_type.94 = bf16[64,4,8,448]{3,2,1,0:T(8,128)(2,1)S(1)} reshape(bf16[256,3584]{1,0:T(8,128)(2,1)} %fusion) | data formatting | bytes 3670016 | tf_op jit(solution)/shard_map/convert_element_type | solution.py:142
  104.7 2.4 %copy.73 = bf16[64,4,8,448]{3,1,0,2:T(4,128)(2,1)} copy(bf16[64,4,8,448]{3,2,1,0:T(8,128)(2,1)S(1)} %convert_element_type.94) | data formatting | bytes 3670016 | tf_op jit(solution)/shard_map/convert_element_type | solution.py:142
  107.1 4.6 %all-to-all-start.2 = ((bf16[8,64,4,448]{3,2,1,0:T(4,128)(2,1)}), bf16[8,64,4,448]{3,2,1,0:T(4,128)(2,1)S(1)}, u32[]{:S(2)}, u32[]{:S(2)}) async-start(bf16[8,64,4,448]{3,2,1,0:T(4,128)(2,1)} %bitcast.102), calls=%async_computation.2 | async-start | bytes 4194304 | tf_op jit(solution)/shard_map/all_to_all | solution.py:49
  111.8 30.3 %all_gather.13 = bf16[64,128,56]{1,2,0:T(8,128)(2,1)S(1)} all-gather(bf16[4,128,56]{1,2,0:T(8,128)(2,1)S(1)} %copy_bitcast_fusion.2), channel_id=1, replica_groups=mesh['expert_0'=4,'expert_1'=16,'tensor'=8] {'expert_1'}, dimensions={0}, use_global_device_ids=true | all-gather | bytes 974848 | tf_op jit(solution)/shard_map/all_gather | solution.py:31
  142.7 1.6 copy.60
  146.6 8.2 %all-to-all-start.4 = ((bf16[8,16,448]{2,1,0:T(8,128)(2,1)}), bf16[8,16,448]{2,1,0:T(8,128)(2,1)S(1)}, u32[]{:S(2)}, u32[]{:S(2)}) async-start(bf16[8,16,448]{2,1,0:T(8,128)(2,1)} %bitcast.100), calls=%async_computation.4 | async-start | bytes 262144 | tf_op jit(solution)/shard_map/all_to_all | solution.py:49
  154.8 1.3 reduce_sum.52
  157.0 3.1 %all-to-all-done.4 = bf16[8,16,448]{2,1,0:T(8,128)(2,1)S(1)} async-done(((bf16[8,16,448]{2,1,0:T(8,128)(2,1)}), bf16[8,16,448]{2,1,0:T(8,128)(2,1)S(1)}, u32[]{:S(2)}, u32[]{:S(2)}) %all-to-all-start.4) | async-done | bytes 114720 | tf_op jit(solution)/shard_map/all_to_all | solution.py:49
  160.0 11.0 %all-to-all-start.3 = ((bf16[64,4,449]{2,1,0:T(4,128)(2,1)}), bf16[64,4,449]{2,1,0:T(4,128)(2,1)S(1)}, u32[]{:S(2)}, u32[]{:S(2)}) async-start(bf16[64,4,449]{2,1,0:T(4,128)(2,1)} %pad_maximum_fusion), calls=%async_computation.3 | async-start | bytes 524288 | tf_op jit(solution)/shard_map/all_to_all | solution.py:57
  171.2 18.9 %all-to-all-done.3 = bf16[64,4,449]{2,1,0:T(4,128)(2,1)S(1)} async-done(((bf16[64,4,449]{2,1,0:T(4,128)(2,1)}), bf16[64,4,449]{2,1,0:T(4,128)(2,1)S(1)}, u32[]{:S(2)}, u32[]{:S(2)}) %all-to-all-start.3) | async-done | bytes 229920 | tf_op jit(solution)/shard_map/all_to_all | solution.py:57
  191.5 1.3 gather_fusion.2
  193.6 6.1 %all-to-all-start.5 = ((f32[8,1,128]{2,1,0:T(1,128)}), f32[8,1,128]{2,1,0:T(1,128)S(1)}, u32[]{:S(2)}, u32[]{:S(2)}) async-start(f32[8,1,128]{2,1,0:T(1,128)} %reshape.153), calls=%async_computation.5 | async-start | bytes 8192 | tf_op jit(solution)/shard_map/all_to_all | solution.py:12
  200.4 3.8 %all-to-all-done.5 = f32[8,1,128]{2,1,0:T(1,128)S(1)} async-done(((f32[8,1,128]{2,1,0:T(1,128)}), f32[8,1,128]{2,1,0:T(1,128)S(1)}, u32[]{:S(2)}, u32[]{:S(2)}) %all-to-all-start.5) | async-done | bytes 4128 | tf_op jit(solution)/shard_map/all_to_all | solution.py:12
  (67 shorter events, 16.4 us)
Async XLA Ops:
  7.2 89.5 %copy-start = (bf16[1,128,3584]{2,1,0:T(8,128)(2,1)S(1)}, bf16[1,128,3584]{2,1,0:T(8,128)(2,1)}, u32[]{:S(2)}) copy-start(bf16[1,128,3584]{2,1,0:T(8,128)(2,1)} %param.13) | copy-start | bytes 2752516
  55.6 7.5 %copy-start.4 = (bf16[2,56,128]{2,1,0:T(8,128)(2,1)S(1)}, bf16[2,56,128]{2,1,0:T(8,128)(2,1)}, u32[]{:S(2)}) copy-start(bf16[2,56,128]{2,1,0:T(8,128)(2,1)} %param.15) | copy-start | bytes 86020
  55.6 18.0 %copy-start.3 = (bf16[1,2,256,128]{3,2,1,0:T(8,128)(2,1)S(1)}, bf16[1,2,256,128]{3,2,1,0:T(8,128)(2,1)}, u32[]{:S(2)}) copy-start(bf16[1,2,256,128]{3,2,1,0:T(8,128)(2,1)} %param.14) | copy-start | bytes 393220
  55.6 18.2 %copy-start.5 = (bf16[128,56]{0,1:T(8,128)(2,1)S(1)}, bf16[128,56]{0,1:T(8,128)(2,1)}, u32[]{:S(2)}) copy-start(bf16[128,56]{0,1:T(8,128)(2,1)} %param.16) | copy-start | bytes 43012
  55.6 33.7 %all-to-all-start.1 = ((bf16[8,64,4,448]{3,2,1,0:T(4,128)(2,1)}), bf16[8,64,4,448]{3,2,1,0:T(4,128)(2,1)S(1)}, u32[]{:S(2)}, u32[]{:S(2)}) async-start(bf16[8,64,4,448]{3,2,1,0:T(4,128)(2,1)} %broadcast_in_dim.32), calls=%async_computation.1 | async-start | bytes 4194304 | tf_op jit(solution)/shard_map/all_to_all | solution.py:12
  63.1 79.5 %all-gather.4.cloned.1.call-start = ((), (), s32[]{:S(2)}) async-start(), calls=%async_computation.6 | async-start | bytes 1949696 | tf_op jit(solution)/shard_map/all_gather | solution.py:31
  96.6 1.5 copy-start.1
  107.1 39.5 %all-to-all-start.2 = ((bf16[8,64,4,448]{3,2,1,0:T(4,128)(2,1)}), bf16[8,64,4,448]{3,2,1,0:T(4,128)(2,1)S(1)}, u32[]{:S(2)}, u32[]{:S(2)}) async-start(bf16[8,64,4,448]{3,2,1,0:T(4,128)(2,1)} %bitcast.102), calls=%async_computation.2 | async-start | bytes 4194304 | tf_op jit(solution)/shard_map/all_to_all | solution.py:49
  111.8 30.4 %copy-start.2 = (bf16[16,3584]{1,0:T(8,128)(2,1)S(1)}, bf16[16,3584]{1,0:T(8,128)(2,1)}, u32[]{:S(2)}) copy-start(bf16[16,3584]{1,0:T(8,128)(2,1)} %param.9) | copy-start | bytes 344068
  144.3 0.7 copy-start.6
  146.6 24.5 %copy-start.7 = (f32[16,8]{0,1:T(8,128)S(1)}, f32[16,8]{0,1:T(8,128)}, u32[]{:S(2)}) copy-start(f32[16,8]{0,1:T(8,128)} %param.11) | copy-start | bytes 1540
  146.6 13.4 %all-to-all-start.4 = ((bf16[8,16,448]{2,1,0:T(8,128)(2,1)}), bf16[8,16,448]{2,1,0:T(8,128)(2,1)S(1)}, u32[]{:S(2)}, u32[]{:S(2)}) async-start(bf16[8,16,448]{2,1,0:T(8,128)(2,1)} %bitcast.100), calls=%async_computation.4 | async-start | bytes 262144 | tf_op jit(solution)/shard_map/all_to_all | solution.py:49
  160.0 30.1 %all-to-all-start.3 = ((bf16[64,4,449]{2,1,0:T(4,128)(2,1)}), bf16[64,4,449]{2,1,0:T(4,128)(2,1)S(1)}, u32[]{:S(2)}, u32[]{:S(2)}) async-start(bf16[64,4,449]{2,1,0:T(4,128)(2,1)} %pad_maximum_fusion), calls=%async_computation.3 | async-start | bytes 524288 | tf_op jit(solution)/shard_map/all_to_all | solution.py:57
  193.6 10.6 %all-to-all-start.5 = ((f32[8,1,128]{2,1,0:T(1,128)}), f32[8,1,128]{2,1,0:T(1,128)S(1)}, u32[]{:S(2)}, u32[]{:S(2)}) async-start(f32[8,1,128]{2,1,0:T(1,128)} %reshape.153), calls=%async_computation.5 | async-start | bytes 8192 | tf_op jit(solution)/shard_map/all_to_all | solution.py:12
Sparse Core Ops, SparseCore 0:
  73.8 57.8 all-gather.3
where the time goes:
time: 214 us; the launch traced here: 213 us
  blocking collectives  87.7 us (41%)
  starting transfers between devices  37.4 us (17%)
  waiting for transfers between devices  32.2 us (15%)
  local copies, waits for them, and re-layouts  31.3 us (15%)
  between operations  14.3 us (7%)
  other arithmetic  5.44 us (3%)
  matrix products  4.46 us (2%)
    all_gather x3, blocking collectives, gather_in_order(): blocks = lax.all_gather(blocks, axes[k], axis=0, tiled=True)  49.8 us
    all_to_all x1, blocking collectives, per_device(): lax.all_to_all(column_part, EXPERT, split_axis=0, concat_axis=0, tiled=True)  38 us
    all_to_all x1, waiting for transfers between devices, side_by_side(): lax.all_to_all(both, axis, split_axis=split_dim, concat_axis=concat_dim,...  18.9 us
    all_to_all x2, starting transfers between devices, from_everyone(): lax.all_to_all(jnp.broadcast_to(array[None], (peers, *array.shape)), axis...  13.5 us
    all_to_all x2, starting transfers between devices, sum_at_owner(): lax.all_to_all(in_blocks(array, dim, peers), axis, 0, 0, tiled=True)  12.8 us
    all_to_all x1, starting transfers between devices, side_by_side(): lax.all_to_all(both, axis, split_axis=split_dim, concat_axis=concat_dim,...  11 us
    all_to_all x2, waiting for transfers between devices, from_everyone(): lax.all_to_all(jnp.broadcast_to(array[None], (peers, *array.shape)), axis...  10.2 us
    convert_element_type x2, local copies, waits for them, and re-layouts, per_device(): row_terms.reshape(experts, capacity, features).astype(jnp.bfloat16)  6.34 us
  transfers between devices with their start and end apart: 6, of which 4 were waited for; matrix products, arithmetic and copies ran while one was open for 11% of the time, Pallas kernels for 0%

commit v1 on v0

v1 whole, which is shorter than its diff:
```python
import jax
import jax.numpy as jnp
from jax import lax
from jax.sharding import Mesh
from jax.sharding import PartitionSpec as P

OWNER = ("x", "z")
PARTS = ("y", "core")
F32 = jnp.float32
BF16 = jnp.bfloat16


def exchange(array, axis):
    return lax.all_to_all(array, axis, 0, 0, tiled=True)


def from_everyone(array, axis):
    peers = lax.axis_size(axis)
    return exchange(jnp.broadcast_to(array[None], (peers, *array.shape)), axis)


def contract_last(left, right):
    return lax.dot_general(left, right, (((1,), (1,)), ((), ())), preferred_element_type=F32)


def swiglu_grads(back_grad, saved_gate, saved_up):
    pre_gate = saved_gate.astype(F32)
    pre_up = saved_up.astype(F32)
    sigmoid = jax.nn.sigmoid(pre_gate)
    grad_gate = (back_grad * pre_up * sigmoid * (1.0 + pre_gate * (1.0 - sigmoid))).astype(BF16)
    grad_up = (back_grad * pre_gate * sigmoid).astype(BF16)
    return grad_gate, grad_up


def per_device(
    grad_out,
    expert_ids,
    gate_values,
    w_gate_up,
    w_down,
    saved_routed,
    shared_gate_up,
    shared_down,
    saved_shared,
):
    experts = lax.axis_size(OWNER)
    ys = lax.axis_size("y")
    parts = lax.axis_size(PARTS)
    tokens, features = grad_out.shape
    choose = expert_ids.shape[1]
    slots = saved_routed.shape[2]
    hidden = w_down.shape[1]
    capacity = slots // experts
    share = features // parts
    core = lax.axis_index("core")
    part = lax.axis_index(PARTS)
    swap = [(0, 1), (1, 0)]

    slot = jnp.arange(slots, dtype=jnp.int32)
    hit = expert_ids.T[:, None, :] == (slot // capacity)[None, :, None]
    chosen = jnp.any(hit, axis=0)
    earlier = jnp.arange(tokens)[:, None] < jnp.arange(tokens)[None, :]
    before = jnp.dot(chosen.astype(BF16), earlier.astype(BF16), preferred_element_type=F32)
    source = chosen & (before.astype(jnp.int32) == (slot % capacity)[:, None])
    columns = lax.dynamic_slice_in_dim(grad_out, part * share, share, 1)
    send = jnp.dot(source.astype(BF16), columns, preferred_element_type=F32).astype(BF16)
    own_rows = exchange(send.reshape(experts, capacity, share), OWNER).reshape(slots, share)

    piece = jnp.concatenate([shared_gate_up, shared_down.T[None]], axis=0)
    pieces = from_everyone(from_everyone(piece, "z"), "x")
    pieces = pieces.reshape(experts, 3, -1, hidden)
    down_all = pieces[:, 2].reshape(features, hidden)
    gate_all = pieces[:, 0].reshape(features, hidden)
    up_all = pieces[:, 1].reshape(features, hidden)

    down = exchange(w_down[0].reshape(hidden, ys, 2 * share).transpose(1, 0, 2), "y")
    other_rows = lax.ppermute(own_rows, "core", swap)
    low = jnp.where(core == 0, own_rows, other_rows)
    high = jnp.where(core == 0, other_rows, own_rows)
    rows = jnp.concatenate([low, high], axis=1)
    back_part = lax.dot_general(
        down, rows, (((2,), (1,)), ((), ())), preferred_element_type=F32
    ).transpose(0, 2, 1)
    back_grad = jnp.sum(exchange(back_part.astype(BF16), "y").astype(F32), axis=0)

    pre_gate, pre_up = saved_routed[0, 0], saved_routed[0, 1]
    grad_gate, grad_up = swiglu_grads(back_grad, pre_gate, pre_up)
    sigmoid = jax.nn.sigmoid(pre_gate.astype(F32))
    gate_mix = back_grad * pre_gate.astype(F32) * sigmoid * pre_up.astype(F32)
    gate_terms = jnp.sum(gate_mix, axis=1, keepdims=True).astype(BF16)

    halves = w_gate_up[0].reshape(2, ys, 2, share, hidden)
    own_half = lax.dynamic_index_in_dim(halves, core, 2, keepdims=False)
    other_half = lax.ppermute(
        lax.dynamic_index_in_dim(halves, 1 - core, 2, keepdims=False), "core", swap
    )
    mine = jnp.concatenate([grad_gate, grad_up, jnp.pad(gate_terms, ((0, 0), (0, 127)))], axis=1)
    theirs = lax.ppermute(mine, "core", swap)

    def rows_from(grads, half):
        total = 0.0
        for g in range(2):
            total = total + lax.dot_general(
                grads[:, g * hidden : (g + 1) * hidden],
                half[g],
                (((1,), (2,)), ((), ())),
                preferred_element_type=F32,
            )
        return total

    row_part = (rows_from(mine, own_half) + rows_from(theirs, other_half)).transpose(1, 0, 2)
    gates = jnp.concatenate([gate_terms, theirs[:, 2 * hidden : 2 * hidden + 1]], axis=1)
    row_part = jnp.concatenate(
        [row_part.astype(BF16), jnp.broadcast_to(gates[None], (ys, slots, 2))], axis=2
    )
    summed = jnp.sum(exchange(row_part, "y").astype(F32), axis=0)
    gate_sum = jnp.sum(summed[:, share:], axis=1, keepdims=True)
    gate_high = gate_sum.astype(BF16)
    gate_low = (gate_sum - gate_high.astype(F32)).astype(BF16)
    finished = jnp.concatenate([summed[:, :share].astype(BF16), gate_high, gate_low], axis=1)
    returned = exchange(finished.reshape(experts, capacity, share + 2), OWNER)

    shared_back = jnp.dot(grad_out, down_all, preferred_element_type=F32)
    shared_gate, shared_up = swiglu_grads(shared_back, saved_shared[0], saved_shared[1])
    shared_term = contract_last(shared_gate, gate_all) + contract_last(shared_up, up_all)
    shared_parts = shared_term.astype(BF16).reshape(tokens, parts, share).transpose(1, 0, 2)
    shared_sum = jnp.sum(exchange(shared_parts, PARTS).astype(F32), axis=0)

    pick = (hit & source[None]).transpose(0, 2, 1).reshape(choose * tokens, slots)
    picked = jnp.dot(
        pick.astype(BF16), returned.reshape(slots, share + 2), preferred_element_type=F32
    ).reshape(choose, tokens, share + 2)
    routed = jnp.sum(picked[:, :, :share] * gate_values.T[:, :, None], axis=0)
    grad_gates = jnp.sum(picked[:, :, share:], axis=2).T
    return (routed + shared_sum).astype(BF16), grad_gates


def solution(mesh):
    finer = Mesh(mesh.devices.reshape(4, 16, 4, 2), ("x", "z", "y", "core"))
    placed = (
        P(OWNER, None),
        P(OWNER, None),
        P(OWNER, None),
        P(OWNER, None, None, PARTS),
        P(OWNER, PARTS, None),
        P(OWNER, None, None, PARTS),
        P(None, OWNER, PARTS),
        P(PARTS, OWNER),
        P(None, OWNER, PARTS),
    )
    return jax.shard_map(
        per_device,
        mesh=finer,
        in_specs=placed,
        out_specs=(P(OWNER, PARTS), P(OWNER, None)),
        check_vma=False,
    )
```

time: 214 us -> 225 us (1.051)
  waiting for transfers between devices: 32.2 us -> 96.5 us
  blocking collectives: 87.7 us -> 33.3 us
  starting transfers between devices: 37.4 us -> 64.4 us
  local copies, waits for them, and re-layouts: 31.3 us -> 13.9 us
  between operations: 14.3 us -> 1.03 us
  matrix products: 4.46 us -> 9.34 us
    all_to_all x5 -> x7, waiting for transfers between devices: 32.2 us -> 95.2 us  [exchange(): return lax.all_to_all(array, axis, 0, 0, tiled=True)]
    all_gather x3 -> x0, blocking collectives: 49.8 us -> none  [gather_in_order(): blocks = lax.all_gather(blocks, axes[k], axis=0, tiled=True)]
    ppermute x0 -> x3, starting transfers between devices: none -> 16.9 us  [the longest x1 6.19 us: per_device(): lax.ppermute(lax.dynamic_index_in_dim(halves, 1 - core, 2, keepdims=False...]
    all_to_all x5 -> x7, starting transfers between devices: 37.4 us -> 47.5 us  [exchange(): return lax.all_to_all(array, axis, 0, 0, tiled=True)]
    convert_element_type x4 -> x5, local copies, waits for them, and re-layouts: 6.69 us -> 0.59 us  [the longest x1 0.15 us: per_device(): gate_high = gate_sum.astype(BF16)]
    transpose x3 -> x0, local copies, waits for them, and re-layouts: 5.3 us -> none  [the longest x1 3.58 us: joined_along(): return jnp.moveaxis(blocks, 0, dim).reshape(lengths)]
    dot_general x7 -> x11, matrix products: 4.46 us -> 9.34 us  [the longest x4 5.72 us: rows_from(): lax.dot_general(grads[:, g * hidden:(g + 1) * hidden], half[g], (((1,), (...]
    all_to_all x1, blocking collectives: 38 us -> 33.3 us  [exchange(): return lax.all_to_all(array, axis, 0, 0, tiled=True)]
  transfers between devices with their start and end apart: 6 -> 10, of which waited for: 4 -> 7; matrix products, arithmetic and copies ran while one was open for 11% -> 5% of each run, Pallas kernels for 0% -> 0%
where the time goes in v1:
time: 225 us; the launch traced here: 224 us
  waiting for transfers between devices  96.5 us (43%)
  starting transfers between devices  64.4 us (29%)
  blocking collectives  33.3 us (15%)
  local copies, waits for them, and re-layouts  13.9 us (6%)
  matrix products  9.34 us (4%)
  other arithmetic  5.72 us (3%)
    all_to_all x7, waiting for transfers between devices, exchange(): return lax.all_to_all(array, axis, 0, 0, tiled=True)  95.2 us
    all_to_all x7, starting transfers between devices, exchange(): return lax.all_to_all(array, axis, 0, 0, tiled=True)  47.5 us
    all_to_all x1, blocking collectives, exchange(): return lax.all_to_all(array, axis, 0, 0, tiled=True)  33.3 us
    ppermute x1, starting transfers between devices, per_device(): lax.ppermute(lax.dynamic_index_in_dim(halves, 1 - core, 2, keepdims=False...  6.19 us
    dot_general x4, matrix products, rows_from(): lax.dot_general(grads[:, g * hidden:(g + 1) * hidden], half[g], (((1,), (...  5.72 us
    ppermute x1, starting transfers between devices, per_device(): theirs = lax.ppermute(mine, 'core', swap)  5.62 us
    ppermute x1, starting transfers between devices, per_device(): other_rows = lax.ppermute(own_rows, 'core', swap)  5.06 us
  transfers between devices with their start and end apart: 10, of which 7 were waited for; matrix products, arithmetic and copies ran while one was open for 5% of the time, Pallas kernels for 0%

profile of v1, /device:TPU:1, one launch (start us, length us, event | category | flops | bytes accessed | tf_op | source)
XLA Modules:
  0.0 224.1 jit_solution(17534629734014031280)
XLA Ops:
  3.8 19.1 %all-to-all-start = ((bf16[64,4,448]{2,1,0:T(4,128)(2,1)}), bf16[64,4,448]{2,1,0:T(4,128)(2,1)S(1)}, u32[]{:S(2)}, u32[]{:S(2)}) async-start(bf16[64,4,448]{2,1,0:T(4,128)(2,1)} %reshape.132), calls=%async_computation | async-start | bytes 524288 | tf_op jit(solution)/shard_map/all_to_all | solution.py:14
  22.9 1.6 copy.46
  24.5 1.3 copy.47
  25.7 16.2 %all-to-all-done = bf16[64,4,448]{2,1,0:T(4,128)(2,1)S(1)} async-done(((bf16[64,4,448]{2,1,0:T(4,128)(2,1)}), bf16[64,4,448]{2,1,0:T(4,128)(2,1)S(1)}, u32[]{:S(2)}, u32[]{:S(2)}) %all-to-all-start) | async-done | bytes 229408 | tf_op jit(solution)/shard_map/all_to_all | solution.py:14
  42.0 4.2 %all-to-all-start.1 = ((bf16[4,128,896]{2,1,0:T(8,128)(2,1)}), bf16[4,128,896]{2,1,0:T(8,128)(2,1)S(1)}, u32[]{:S(2)}, u32[]{:S(2)}) async-start(bf16[4,128,896]{2,1,0:T(8,128)(2,1)} %bitcast.4), calls=%async_computation.1 | async-start | bytes 1835008 | tf_op jit(solution)/shard_map/all_to_all | solution.py:14
  46.3 5.1 %collective-permute-start = (bf16[256,448]{1,0:T(8,128)(2,1)S(1)}, bf16[256,448]{1,0:T(8,128)(2,1)}, u32[]{:S(2)}, u32[]{:S(2)}) collective-permute-start(bf16[256,448]{1,0:T(8,128)(2,1)S(1)} %reshape.133), channel_id=1, source_target_pairs={{0,1},{1,0},{2,3},{3,2},{4,5},{5,4},{6,7},{7,6},{8,9},{9,8},{10,11... | collective-permute-start | bytes 688136 | tf_op jit(solution)/shard_map/ppermute | solution.py:77
  53.6 2.9 %all-to-all-done.1 = bf16[4,128,896]{2,1,0:T(8,128)(2,1)S(1)} async-done(((bf16[4,128,896]{2,1,0:T(8,128)(2,1)}), bf16[4,128,896]{2,1,0:T(8,128)(2,1)S(1)}, u32[]{:S(2)}, u32[]{:S(2)}) %all-to-all-start.1) | async-done | bytes 917536 | tf_op jit(solution)/shard_map/all_to_all | solution.py:14
  57.7 3.5 %all-to-all-start.2 = ((bf16[4,256,128]{2,1,0:T(8,128)(2,1)}), bf16[4,256,128]{2,1,0:T(8,128)(2,1)S(1)}, u32[]{:S(2)}, u32[]{:S(2)}) async-start(bf16[4,256,128]{2,1,0:T(8,128)(2,1)} %fusion.2), calls=%async_computation.2 | async-start | bytes 524288 | tf_op jit(solution)/shard_map/all_to_all | solution.py:14
  62.3 6.2 %collective-permute-start.2 = (bf16[2,4,448,128]{3,2,1,0:T(8,128)(2,1)}, bf16[2,4,448,128]{3,2,1,0:T(8,128)(2,1)S(1)}, u32[]{:S(2)}, u32[]{:S(2)}) collective-permute-start(bf16[2,4,448,128]{3,2,1,0:T(8,128)(2,1)} %dynamic-slice_bitcast_fusion), channel_id=1, source_target_pairs={{0,1},{1,0},{2,3},{3,2},{4,5},{5,4},{6,7},{7,6},{8,9},{9,8},{10,11... | collective-permute-start | bytes 2752520 | tf_op jit(solution)/shard_map/ppermute | solution.py:94
  68.9 5.6 %collective-permute-start.1 = (bf16[256,384]{1,0:T(8,128)(2,1)S(1)}, bf16[256,384]{1,0:T(8,128)(2,1)S(1)}, u32[]{:S(2)}, u32[]{:S(2)}) collective-permute-start(bf16[256,384]{1,0:T(8,128)(2,1)S(1)} %fusion.17), channel_id=1, source_target_pairs={{0,1},{1,0},{2,3},{3,2},{4,5},{5,4},{6,7},{7,6},{8,9},{9,8},{10,11... | collective-permute-start | bytes 589832 | tf_op jit(solution)/shard_map/ppermute | solution.py:98
  74.5 1.7 fusion.7
  76.2 1.6 fusion.6
  79.4 2.0 fusion.1
  82.5 3.5 %all-to-all-start.3 = ((bf16[4,256,450]{1,2,0:T(8,128)(2,1)}), bf16[4,256,450]{1,2,0:T(8,128)(2,1)S(1)}, u32[]{:S(2)}, u32[]{:S(2)}) async-start(bf16[4,256,450]{1,2,0:T(8,128)(2,1)} %pad_maximum_fusion), calls=%async_computation.3 | async-start | bytes 1867776 | tf_op jit(solution)/shard_map/all_to_all | solution.py:14
  86.0 13.9 %all-to-all-done.3 = bf16[4,256,450]{1,2,0:T(8,128)(2,1)S(1)} async-done(((bf16[4,256,450]{1,2,0:T(8,128)(2,1)}), bf16[4,256,450]{1,2,0:T(8,128)(2,1)S(1)}, u32[]{:S(2)}, u32[]{:S(2)}) %all-to-all-start.3) | async-done | bytes 921632 | tf_op jit(solution)/shard_map/all_to_all | solution.py:14
  100.9 5.5 %all-to-all-start.5 = ((bf16[16,3,56,128]{3,2,1,0:T(8,128)(2,1)}), bf16[16,3,56,128]{3,2,1,0:T(8,128)(2,1)S(1)}, u32[]{:S(2)}, u32[]{:S(2)}) async-start(bf16[16,3,56,128]{3,2,1,0:T(8,128)(2,1)} %broadcast_in_dim.10), calls=%async_computation.5 | async-start | bytes 1376256 | tf_op jit(solution)/shard_map/all_to_all | solution.py:14
  109.0 27.5 %all-to-all-done.5 = bf16[16,3,56,128]{3,2,1,0:T(8,128)(2,1)S(1)} async-done(((bf16[16,3,56,128]{3,2,1,0:T(8,128)(2,1)}), bf16[16,3,56,128]{3,2,1,0:T(8,128)(2,1)S(1)}, u32[]{:S(2)}, u32[]{:S(2)}) %all-to-all-start.5) | async-done | bytes 688160 | tf_op jit(solution)/shard_map/all_to_all | solution.py:14
  136.5 33.3 %all_to_all.40 = bf16[64,4,450]{2,1,0:T(4,128)(2,1)S(1)} all-to-all(bf16[64,4,450]{2,1,0:T(4,128)(2,1)S(1)} %pad_maximum_fusion.1), channel_id=1, replica_groups=mesh['x'=4,'z'=16,'y'=4,'core'=2] {'x','z'}, dimensions={0} | all-to-all | bytes 460800 | tf_op jit(solution)/shard_map/all_to_all | solution.py:14
  169.8 2.0 broadcast_in_dim.11
  171.7 4.7 %all-to-all-start.6 = ((bf16[4,16,3,56,128]{4,3,2,1,0:T(8,128)(2,1)}), bf16[4,16,3,56,128]{4,3,2,1,0:T(8,128)(2,1)}, u32[]{:S(2)}, u32[]{:S(2)}) async-start(bf16[4,16,3,56,128]{4,3,2,1,0:T(8,128)(2,1)} %broadcast_in_dim.11), calls=%async_computation.6 | async-start | bytes 5505024 | tf_op jit(solution)/shard_map/all_to_all | solution.py:14
  176.9 30.2 %all-to-all-done.6 = bf16[4,16,3,56,128]{4,3,2,1,0:T(8,128)(2,1)} async-done(((bf16[4,16,3,56,128]{4,3,2,1,0:T(8,128)(2,1)}), bf16[4,16,3,56,128]{4,3,2,1,0:T(8,128)(2,1)}, u32[]{:S(2)}, u32[]{:S(2)}) %all-to-all-start.6) | async-done | bytes 2752544 | tf_op jit(solution)/shard_map/all_to_all | solution.py:14
  207.1 2.3 %fusion.82 = (bf16[64,1,56,128]{3,2,1,0:T(8,128)(2,1)S(1)}, bf16[64,1,56,128]{3,2,1,0:T(8,128)(2,1)S(1)}, bf16[64,1,56,128]{3,2,1,0:T(8,128)(2,1)S(1)}) fusion(bf16[64,3,56,128]{3,2,1,0:T(8,128)(2,1)} %bitcast.26), kind=kLoop, calls=%fused_computation.126 | loop fusion | bytes 5505024 | tf_op jit(solution)/shard_map/slice | solution.py:74
  211.2 7.0 %all-to-all-start.7 = ((bf16[8,16,448]{2,1,0:T(8,128)(2,1)}), bf16[8,16,448]{2,1,0:T(8,128)(2,1)S(1)}, u32[]{:S(2)}, u32[]{:S(2)}) async-start(bf16[8,16,448]{2,1,0:T(8,128)(2,1)} %bitcast.137), calls=%async_computation.7 | async-start | bytes 262144 | tf_op jit(solution)/shard_map/all_to_all | solution.py:14
  218.9 4.5 %all-to-all-done.7 = bf16[8,16,448]{2,1,0:T(8,128)(2,1)S(1)} async-done(((bf16[8,16,448]{2,1,0:T(8,128)(2,1)}), bf16[8,16,448]{2,1,0:T(8,128)(2,1)S(1)}, u32[]{:S(2)}, u32[]{:S(2)}) %all-to-all-start.7) | async-done | bytes 114720 | tf_op jit(solution)/shard_map/all_to_all | solution.py:14
  (69 shorter events, 17.9 us)
Async XLA Ops:
  0.6 60.6 %copy-start = (bf16[1,2,3584,128]{3,2,1,0:T(8,128)(2,1)S(1)}, bf16[1,2,3584,128]{3,2,1,0:T(8,128)(2,1)}, u32[]{:S(2)}) copy-start(bf16[1,2,3584,128]{3,2,1,0:T(8,128)(2,1)} %param.12) | copy-start | bytes 5505028
  3.8 38.2 %all-to-all-start = ((bf16[64,4,448]{2,1,0:T(4,128)(2,1)}), bf16[64,4,448]{2,1,0:T(4,128)(2,1)S(1)}, u32[]{:S(2)}, u32[]{:S(2)}) async-start(bf16[64,4,448]{2,1,0:T(4,128)(2,1)} %reshape.132), calls=%async_computation | async-start | bytes 524288 | tf_op jit(solution)/shard_map/all_to_all | solution.py:14
  42.0 14.5 %all-to-all-start.1 = ((bf16[4,128,896]{2,1,0:T(8,128)(2,1)}), bf16[4,128,896]{2,1,0:T(8,128)(2,1)S(1)}, u32[]{:S(2)}, u32[]{:S(2)}) async-start(bf16[4,128,896]{2,1,0:T(8,128)(2,1)} %bitcast.4), calls=%async_computation.1 | async-start | bytes 1835008 | tf_op jit(solution)/shard_map/all_to_all | solution.py:14
  46.3 6.3 %collective-permute-start = (bf16[256,448]{1,0:T(8,128)(2,1)S(1)}, bf16[256,448]{1,0:T(8,128)(2,1)}, u32[]{:S(2)}, u32[]{:S(2)}) collective-permute-start(bf16[256,448]{1,0:T(8,128)(2,1)S(1)} %reshape.133), channel_id=1, source_target_pairs={{0,1},{1,0},{2,3},{3,2},{4,5},{5,4},{6,7},{7,6},{8,9},{9,8},{10,11... | collective-permute-start | bytes 688136 | tf_op jit(solution)/shard_map/ppermute | solution.py:77
  57.7 10.8 %copy-start.3 = (bf16[1,2,256,128]{3,2,1,0:T(8,128)(2,1)S(1)}, bf16[1,2,256,128]{3,2,1,0:T(8,128)(2,1)}, u32[]{:S(2)}) copy-start(bf16[1,2,256,128]{3,2,1,0:T(8,128)(2,1)} %param.14) | copy-start | bytes 393220
  57.7 10.8 %all-to-all-start.2 = ((bf16[4,256,128]{2,1,0:T(8,128)(2,1)}), bf16[4,256,128]{2,1,0:T(8,128)(2,1)S(1)}, u32[]{:S(2)}, u32[]{:S(2)}) async-start(bf16[4,256,128]{2,1,0:T(8,128)(2,1)} %fusion.2), calls=%async_computation.2 | async-start | bytes 524288 | tf_op jit(solution)/shard_map/all_to_all | solution.py:14
  62.3 15.7 %collective-permute-start.2 = (bf16[2,4,448,128]{3,2,1,0:T(8,128)(2,1)}, bf16[2,4,448,128]{3,2,1,0:T(8,128)(2,1)S(1)}, u32[]{:S(2)}, u32[]{:S(2)}) collective-permute-start(bf16[2,4,448,128]{3,2,1,0:T(8,128)(2,1)} %dynamic-slice_bitcast_fusion), channel_id=1, source_target_pairs={{0,1},{1,0},{2,3},{3,2},{4,5},{5,4},{6,7},{7,6},{8,9},{9,8},{10,11... | collective-permute-start | bytes 2752520 | tf_op jit(solution)/shard_map/ppermute | solution.py:94
  68.9 8.9 %collective-permute-start.1 = (bf16[256,384]{1,0:T(8,128)(2,1)S(1)}, bf16[256,384]{1,0:T(8,128)(2,1)S(1)}, u32[]{:S(2)}, u32[]{:S(2)}) collective-permute-start(bf16[256,384]{1,0:T(8,128)(2,1)S(1)} %fusion.17), channel_id=1, source_target_pairs={{0,1},{1,0},{2,3},{3,2},{4,5},{5,4},{6,7},{7,6},{8,9},{9,8},{10,11... | collective-permute-start | bytes 589832 | tf_op jit(solution)/shard_map/ppermute | solution.py:98
  77.9 1.5 copy-start.1
  81.5 4.5 %copy-start.5 = (bf16[2,56,128]{2,1,0:T(8,128)(2,1)S(1)}, bf16[2,56,128]{2,1,0:T(8,128)(2,1)}, u32[]{:S(2)}) copy-start(bf16[2,56,128]{2,1,0:T(8,128)(2,1)} %param.15) | copy-start | bytes 86020
  81.5 4.5 %copy-start.7 = (bf16[128,56]{0,1:T(8,128)(2,1)S(1)}, bf16[128,56]{0,1:T(8,128)(2,1)}, u32[]{:S(2)}) copy-start(bf16[128,56]{0,1:T(8,128)(2,1)} %param.16) | copy-start | bytes 43012
  82.5 17.4 %all-to-all-start.3 = ((bf16[4,256,450]{1,2,0:T(8,128)(2,1)}), bf16[4,256,450]{1,2,0:T(8,128)(2,1)S(1)}, u32[]{:S(2)}, u32[]{:S(2)}) async-start(bf16[4,256,450]{1,2,0:T(8,128)(2,1)} %pad_maximum_fusion), calls=%async_computation.3 | async-start | bytes 1867776 | tf_op jit(solution)/shard_map/all_to_all | solution.py:14
  100.9 35.6 %all-to-all-start.5 = ((bf16[16,3,56,128]{3,2,1,0:T(8,128)(2,1)}), bf16[16,3,56,128]{3,2,1,0:T(8,128)(2,1)S(1)}, u32[]{:S(2)}, u32[]{:S(2)}) async-start(bf16[16,3,56,128]{3,2,1,0:T(8,128)(2,1)} %broadcast_in_dim.10), calls=%async_computation.5 | async-start | bytes 1376256 | tf_op jit(solution)/shard_map/all_to_all | solution.py:14
  106.5 0.8 copy-start.2
  171.7 4.9 %copy-start.6 = (s32[16,8]{0,1:T(8,128)S(1)}, s32[16,8]{0,1:T(8,128)}, u32[]{:S(2)}) copy-start(s32[16,8]{0,1:T(8,128)} %param.10) | copy-start | bytes 1540
  171.7 5.1 %copy-start.9 = (f32[16,8]{0,1:T(8,128)S(1)}, f32[16,8]{0,1:T(8,128)}, u32[]{:S(2)}) copy-start(f32[16,8]{0,1:T(8,128)} %param.11) | copy-start | bytes 1540
  171.7 35.4 %all-to-all-start.6 = ((bf16[4,16,3,56,128]{4,3,2,1,0:T(8,128)(2,1)}), bf16[4,16,3,56,128]{4,3,2,1,0:T(8,128)(2,1)}, u32[]{:S(2)}, u32[]{:S(2)}) async-start(bf16[4,16,3,56,128]{4,3,2,1,0:T(8,128)(2,1)} %broadcast_in_dim.11), calls=%async_computation.6 | async-start | bytes 5505024 | tf_op jit(solution)/shard_map/all_to_all | solution.py:14
  207.1 2.3 %copy-start.4 = (bf16[16,3584]{1,0:T(8,128)(2,1)S(1)}, bf16[16,3584]{1,0:T(8,128)(2,1)}, u32[]{:S(2)}) copy-start(bf16[16,3584]{1,0:T(8,128)(2,1)} %param.9) | copy-start | bytes 344068
  207.1 2.5 %copy-start.8 = (bf16[2,16,128]{2,1,0:T(8,128)(2,1)S(1)}, bf16[2,16,128]{2,1,0:T(8,128)(2,1)}, u32[]{:S(2)}) copy-start(bf16[2,16,128]{2,1,0:T(8,128)(2,1)} %param.17) | copy-start | bytes 24580
  211.2 12.3 %all-to-all-start.7 = ((bf16[8,16,448]{2,1,0:T(8,128)(2,1)}), bf16[8,16,448]{2,1,0:T(8,128)(2,1)S(1)}, u32[]{:S(2)}, u32[]{:S(2)}) async-start(bf16[8,16,448]{2,1,0:T(8,128)(2,1)} %bitcast.137), calls=%async_computation.7 | async-start | bytes 262144 | tf_op jit(solution)/shard_map/all_to_all | solution.py:14

commit v2 on v1

v2 whole, which is shorter than its diff:
```python
import jax
import jax.numpy as jnp
from jax import lax
from jax.experimental import pallas as pl
from jax.experimental.pallas import tpu as pltpu
from jax.sharding import Mesh
from jax.sharding import PartitionSpec as P

OWNER = ("x", "z")
PARTS = ("y", "core")
F32 = jnp.float32
BF16 = jnp.bfloat16
LANES = 128


def exchange(array, axis):
    return lax.all_to_all(array, axis, 0, 0, tiled=True)


def from_everyone(array, axis):
    peers = lax.axis_size(axis)
    return exchange(jnp.broadcast_to(array[None], (peers, *array.shape)), axis)


def contract_last(left, right):
    return lax.dot_general(left, right, (((1,), (1,)), ((), ())), preferred_element_type=F32)


def swiglu_grads(back_grad, saved_gate, saved_up):
    pre_gate = saved_gate.astype(F32)
    pre_up = saved_up.astype(F32)
    sigmoid = jax.nn.sigmoid(pre_gate)
    grad_gate = (back_grad * pre_up * sigmoid * (1.0 + pre_gate * (1.0 - sigmoid))).astype(BF16)
    grad_up = (back_grad * pre_gate * sigmoid).astype(BF16)
    return grad_gate, grad_up


def kernel_call(body, out_shape, scalars, *arrays):
    smem = pl.BlockSpec(memory_space=pltpu.SMEM)
    vmem = pl.BlockSpec(memory_space=pltpu.VMEM)
    return pl.pallas_call(
        body,
        out_shape=out_shape,
        in_specs=[smem] + [vmem] * len(arrays),
        out_specs=vmem,
    )(scalars, *arrays)


def back_kernel(where, own, other, *refs):
    *weights, out = refs
    core, y = where[0], where[1]
    for r, weight in enumerate(weights):
        part = contract_last(own[...], weight[core]) + contract_last(other[...], weight[1 - core])
        out[(y + len(weights) - r) % len(weights)] = part.astype(BF16)


def gate_kernel(where, parts, saved, out):
    back_grad = jnp.sum(parts[...].astype(F32), axis=0)
    pre_gate = saved[0].astype(F32)
    pre_up = saved[1].astype(F32)
    sigmoid = jax.nn.sigmoid(pre_gate)
    grad_gate = back_grad * pre_up * sigmoid * (1.0 + pre_gate * (1.0 - sigmoid))
    grad_up = back_grad * pre_gate * sigmoid
    term = jnp.sum(grad_up * pre_up, axis=1, keepdims=True)
    lane = lax.broadcasted_iota(jnp.int32, (term.shape[0], LANES), 1)
    hidden = pre_gate.shape[1]
    out[:, :hidden] = grad_gate.astype(BF16)
    out[:, hidden : 2 * hidden] = grad_up.astype(BF16)
    out[:, 2 * hidden :] = jnp.where(lane == 0, term, 0.0).astype(BF16)


def row_kernel(where, mine, theirs, own, other, out):
    core = where[0]
    ys, share = other.shape[1], other.shape[2]
    spare = out.shape[2] - share
    hidden = own.shape[2]
    row = lax.broadcasted_iota(jnp.int32, (share + spare, LANES), 0)
    lane = lax.broadcasted_iota(jnp.int32, (share + spare, LANES), 1)
    blank = jnp.zeros((spare, 2 * hidden), BF16)

    def wide(gate, up, column):
        weights = jnp.concatenate([jnp.concatenate([gate, up], axis=1), blank], axis=0)
        passing = jnp.where((row == column) & (lane == 0), 1.0, 0.0).astype(BF16)
        return jnp.concatenate([weights, passing], axis=1)

    for y in range(ys):
        at = pl.ds(pl.multiple_of((2 * y + core) * share, 16), share)
        total = contract_last(mine[...], wide(own[0, at, :], own[1, at, :], share))
        total += contract_last(theirs[...], wide(other[0, y], other[1, y], share + 1))
        out[y] = total.astype(BF16)


def pack_kernel(where, parts, out):
    total = jnp.sum(parts[...].astype(F32), axis=0)
    slots, width = total.shape
    share = SHARE
    lane = lax.broadcasted_iota(jnp.int32, (slots, width), 1)
    gates = jnp.sum(jnp.where(lane >= share, total, 0.0), axis=1, keepdims=True)
    high = gates.astype(BF16).astype(F32)
    low = gates - high
    packed = jnp.where(lane == share, high, jnp.where(lane == share + 1, low, total))
    out[...] = packed.astype(BF16).reshape(out.shape)


SHARE = 448


def per_device(
    grad_out,
    expert_ids,
    gate_values,
    w_gate_up,
    w_down,
    saved_routed,
    shared_gate_up,
    shared_down,
    saved_shared,
):
    experts = lax.axis_size(OWNER)
    xs = lax.axis_size("x")
    zs = lax.axis_size("z")
    ys = lax.axis_size("y")
    parts = lax.axis_size(PARTS)
    tokens, features = grad_out.shape
    choose = expert_ids.shape[1]
    slots = saved_routed.shape[2]
    hidden = w_down.shape[1]
    capacity = slots // experts
    share = features // parts
    wide = -(-share // LANES) * LANES
    core = lax.axis_index("core")
    y = lax.axis_index("y")
    part = lax.axis_index(PARTS)
    swap = [(0, 1), (1, 0)]
    where = jnp.stack([core, y]).astype(jnp.int32)

    piece = jnp.concatenate([shared_gate_up, shared_down.T[None]], axis=0)
    column = from_everyone(piece, "x")
    pieces = lax.all_gather(column, "z", axis=0)

    slot = jnp.arange(slots, dtype=jnp.int32)
    hit = expert_ids.T[:, None, :] == (slot // capacity)[None, :, None]
    chosen = jnp.any(hit, axis=0)
    earlier = jnp.arange(tokens)[:, None] < jnp.arange(tokens)[None, :]
    before = jnp.dot(chosen.astype(BF16), earlier.astype(BF16), preferred_element_type=F32)
    source = chosen & (before.astype(jnp.int32) == (slot % capacity)[:, None])
    columns = lax.dynamic_slice_in_dim(grad_out, part * share, share, 1)
    send = jnp.dot(source.astype(BF16), columns, preferred_element_type=F32).astype(BF16)
    send = send.reshape(experts, capacity, share)
    own_rows = exchange(send, OWNER)
    own_rows = own_rows.reshape(slots, share)

    blocks = w_down[0].reshape(hidden, ys, 2, share).transpose(1, 2, 0, 3)
    downs = []
    for r in range(ys):
        block = lax.dynamic_index_in_dim(blocks, (y + r) % ys, 0, keepdims=False)
        if r > 0:
            block = lax.ppermute(block, "y", [(i, (i + r) % ys) for i in range(ys)])
        downs.append(block)
    other_rows = lax.ppermute(own_rows, "core", swap)
    back_part = kernel_call(
        back_kernel,
        jax.ShapeDtypeStruct((ys, slots, hidden), BF16),
        where,
        own_rows,
        other_rows,
        *downs,
    )
    back_parts = exchange(back_part, "y")
    mine = kernel_call(
        gate_kernel,
        jax.ShapeDtypeStruct((slots, 3 * LANES), BF16),
        where,
        back_parts,
        saved_routed[0],
    )

    halves = w_gate_up[0].reshape(2, ys, 2, share, hidden)
    other_half = lax.ppermute(
        lax.dynamic_index_in_dim(halves, 1 - core, 2, keepdims=False), "core", swap
    )
    theirs = lax.ppermute(mine, "core", swap)
    row_part = kernel_call(
        row_kernel,
        jax.ShapeDtypeStruct((ys, slots, wide), BF16),
        where,
        mine,
        theirs,
        w_gate_up[0],
        other_half,
    )
    row_parts = exchange(row_part, "y")
    finished = kernel_call(
        pack_kernel,
        jax.ShapeDtypeStruct((experts, capacity, wide), BF16),
        where,
        row_parts,
    )
    returned = exchange(finished, OWNER)

    turned = grad_out.reshape(tokens, xs, zs, -1).transpose(0, 2, 1, 3).reshape(tokens, -1)
    down_all = pieces[:, :, 2].reshape(features, hidden)
    gate_all = pieces[:, :, 0].reshape(features, hidden)
    up_all = pieces[:, :, 1].reshape(features, hidden)
    shared_back = jnp.dot(turned, down_all, preferred_element_type=F32)
    shared_gate, shared_up = swiglu_grads(shared_back, saved_shared[0], saved_shared[1])
    shared_term = contract_last(shared_gate, gate_all) + contract_last(shared_up, up_all)
    shared_term = (
        shared_term.astype(BF16)
        .reshape(tokens, zs, xs, -1)
        .transpose(0, 2, 1, 3)
        .reshape(tokens, features)
    )
    everyone = lax.all_gather(shared_term, PARTS, axis=0)
    ours = lax.dynamic_slice_in_dim(everyone, part * share, share, 2)
    shared_sum = jnp.sum(ours.astype(F32), axis=0)

    pick = (hit & source[None]).transpose(0, 2, 1).reshape(choose * tokens, slots)
    picked = jnp.dot(
        pick.astype(BF16), returned.reshape(slots, wide), preferred_element_type=F32
    ).reshape(choose, tokens, wide)
    routed = jnp.sum(picked[:, :, :share] * gate_values.T[:, :, None], axis=0)
    grad_gates = jnp.sum(picked[:, :, share : share + 2], axis=2).T
    return (routed + shared_sum).astype(BF16), grad_gates


def solution(mesh):
    finer = Mesh(mesh.devices.reshape(4, 16, 4, 2), ("x", "z", "y", "core"))
    placed = (
        P(OWNER, None),
        P(OWNER, None),
        P(OWNER, None),
        P(OWNER, None, None, PARTS),
        P(OWNER, PARTS, None),
        P(OWNER, None, None, PARTS),
        P(None, OWNER, PARTS),
        P(PARTS, OWNER),
        P(None, OWNER, PARTS),
    )

    return jax.shard_map(
        per_device,
        mesh=finer,
        in_specs=placed,
        out_specs=(P(OWNER, PARTS), P(OWNER, None)),
        check_vma=False,
    )
```

time: 225 us -> 174 us (0.77)
  waiting for transfers between devices: 96.5 us -> 22.4 us
  blocking collectives: 33.3 us -> 56.5 us
  between operations: 1.03 us -> 14.5 us
  starting transfers between devices: 64.4 us -> 52.6 us
  Pallas kernels: 0 us -> 10.9 us
  matrix products: 9.34 us -> 2.44 us
  local copies, waits for them, and re-layouts: 13.9 us -> 9.73 us
    all_to_all x7 -> x2, waiting for transfers between devices: 95.2 us -> 21.1 us  [exchange(): return lax.all_to_all(array, axis, 0, 0, tiled=True)]
    all_to_all x7 -> x2, starting transfers between devices: 47.5 us -> 28.2 us  [exchange(): return lax.all_to_all(array, axis, 0, 0, tiled=True)]
    all_gather x0 -> x1, blocking collectives: none -> 16.6 us  [per_device(): everyone = lax.all_gather(shared_term, PARTS, axis=0)]
    pallas_call x0 -> x4, Pallas kernels: none -> 10.9 us  [kernel_call(): pl.pallas_call(body, out_shape=out_shape, in_specs=[smem] + [vmem] * len(...]
    ppermute x0 -> x3, starting transfers between devices: none -> 10.7 us  [per_device(): block = lax.ppermute(block, 'y', [(i, (i + r) % ys) for i in range(ys)])]
    dot_general x7 -> x2, matrix products: 7.36 us -> 0.46 us  [the longest x1 0.23 us: per_device(): shared_back = jnp.dot(turned, down_all, preferred_element_type=F32)]
    all_to_all x1 -> x3, blocking collectives: 33.3 us -> 39.9 us  [exchange(): return lax.all_to_all(array, axis, 0, 0, tiled=True)]
    broadcast_in_dim x2 -> x1, local copies, waits for them, and re-layouts: 2.91 us -> 0.02 us  [from_everyone(): return exchange(jnp.broadcast_to(array[None], (peers, *array.shape)), axis)]
  transfers between devices with their start and end apart: 10 -> 9, of which waited for: 7 -> 3; matrix products, arithmetic and copies ran while one was open for 5% -> 5% of each run, Pallas kernels for 0% -> 6%
where the time goes in v2:
time: 174 us; the launch traced here: 173 us
  blocking collectives  56.5 us (32%)
  starting transfers between devices  52.6 us (30%)
  waiting for transfers between devices  22.4 us (13%)
  between operations  14.5 us (8%)
  Pallas kernels  10.9 us (6%)
  local copies, waits for them, and re-layouts  9.73 us (6%)
  other arithmetic  3.93 us (2%)
  matrix products  2.44 us (1%)
    all_to_all x3, blocking collectives, exchange(): return lax.all_to_all(array, axis, 0, 0, tiled=True)  39.9 us
    all_to_all x2, starting transfers between devices, exchange(): return lax.all_to_all(array, axis, 0, 0, tiled=True)  28.2 us
    all_to_all x2, waiting for transfers between devices, exchange(): return lax.all_to_all(array, axis, 0, 0, tiled=True)  21.1 us
    all_gather x1, blocking collectives, per_device(): everyone = lax.all_gather(shared_term, PARTS, axis=0)  16.6 us
    pallas_call x4, Pallas kernels, kernel_call(): pl.pallas_call(body, out_shape=out_shape, in_specs=[smem] + [vmem] * len(...  10.9 us
    ppermute x3, starting transfers between devices, per_device(): block = lax.ppermute(block, 'y', [(i, (i + r) % ys) for i in range(ys)])  10.7 us
    ppermute x1, starting transfers between devices, per_device(): other_rows = lax.ppermute(own_rows, 'core', swap)  6.48 us
    ppermute x1, starting transfers between devices, per_device(): lax.ppermute(lax.dynamic_index_in_dim(halves, 1 - core, 2, keepdims=False...  4.09 us
  transfers between devices with their start and end apart: 9, of which 3 were waited for; matrix products, arithmetic and copies ran while one was open for 5% of the time, Pallas kernels for 6%

profile of v2, /device:TPU:1, one launch (start us, length us, event | category | flops | bytes accessed | tf_op | source)
XLA Modules:
  0.0 173.1 jit_solution(8884860577569415018)
XLA Ops:
  7.2 0.9 pad_maximum_fusion
  8.2 9.8 %all_to_all.25 = bf16[4,3,56,128]{3,2,1,0:T(8,128)(2,1)} all-to-all(bf16[4,3,56,128]{3,2,1,0:T(8,128)(2,1)S(1)} %broadcast_in_dim.5), channel_id=1, replica_groups=mesh['x'=4,'z'=16,'y'=4,'core'=2] {'x'}, dimensions={0} | all-to-all | bytes 344064 | tf_op jit(solution)/shard_map/all_to_all | solution.py:17
  19.0 1.1 convolution_convert_fusion
  21.0 16.6 %all-to-all-start = ((bf16[64,4,448]{2,1,0:T(4,128)(2,1)}), bf16[64,4,448]{2,1,0:T(4,128)(2,1)S(1)}, u32[]{:S(2)}, u32[]{:S(2)}) async-start(bf16[64,4,448]{2,1,0:T(4,128)(2,1)} %reshape.73), calls=%async_computation | async-start | bytes 524288 | tf_op jit(solution)/shard_map/all_to_all | solution.py:17
  37.6 1.0 dynamic-slice_bitcast_fusion
  38.6 4.1 %collective-permute-start.5 = (bf16[2,4,448,128]{3,2,1,0:T(8,128)(2,1)}, bf16[2,4,448,128]{3,2,1,0:T(8,128)(2,1)S(1)}, u32[]{:S(2)}, u32[]{:S(2)}) collective-permute-start(bf16[2,4,448,128]{3,2,1,0:T(8,128)(2,1)} %dynamic-slice_bitcast_fusion), channel_id=1, source_target_pairs={{0,1},{1,0},{2,3},{3,2},{4,5},{5,4},{6,7},{7,6},{8,9},{9,8},{10,11... | collective-permute-start | bytes 2752520 | tf_op jit(solution)/shard_map/ppermute | solution.py:179
  43.7 3.2 %collective-permute-start.1 = (bf16[2,128,448]{2,1,0:T(8,128)(2,1)S(1)}, bf16[2,128,448]{2,1,0:T(8,128)(2,1)S(1)}, u32[]{:S(2)}, u32[]{:S(2)}) collective-permute-start(bf16[2,128,448]{2,1,0:T(8,128)(2,1)S(1)} %bitcast.76), channel_id=1, source_target_pairs={{0,2},{2,4},{4,6},{6,0},{1,3},{3,5},{5,7},{7,1},{8,10},{10,12},{12... | collective-permute-start | bytes 688136 | tf_op jit(solution)/shard_map/ppermute | solution.py:158
  47.0 4.5 %collective-permute-start.2 = (bf16[2,128,448]{2,1,0:T(8,128)(2,1)S(1)}, bf16[2,128,448]{2,1,0:T(8,128)(2,1)S(1)}, u32[]{:S(2)}, u32[]{:S(2)}) collective-permute-start(bf16[2,128,448]{2,1,0:T(8,128)(2,1)S(1)} %bitcast.77), channel_id=1, source_target_pairs={{0,4},{2,6},{4,0},{6,2},{1,5},{3,7},{5,1},{7,3},{8,12},{10,14},{12... | collective-permute-start | bytes 688136 | tf_op jit(solution)/shard_map/ppermute | solution.py:158
  51.7 3.0 %collective-permute-start.3 = (bf16[2,128,448]{2,1,0:T(8,128)(2,1)S(1)}, bf16[2,128,448]{2,1,0:T(8,128)(2,1)}, u32[]{:S(2)}, u32[]{:S(2)}) collective-permute-start(bf16[2,128,448]{2,1,0:T(8,128)(2,1)S(1)} %bitcast.78), channel_id=1, source_target_pairs={{0,6},{2,0},{4,2},{6,4},{1,7},{3,1},{5,3},{7,5},{8,14},{10,8},{12,... | collective-permute-start | bytes 688136 | tf_op jit(solution)/shard_map/ppermute | solution.py:158
  54.7 3.3 %all-to-all-done = bf16[64,4,448]{2,1,0:T(4,128)(2,1)S(1)} async-done(((bf16[64,4,448]{2,1,0:T(4,128)(2,1)}), bf16[64,4,448]{2,1,0:T(4,128)(2,1)S(1)}, u32[]{:S(2)}, u32[]{:S(2)}) %all-to-all-start) | async-done | bytes 229408 | tf_op jit(solution)/shard_map/all_to_all | solution.py:17
  58.2 6.5 %collective-permute-start = (bf16[256,448]{1,0:T(8,128)(2,1)S(1)}, bf16[256,448]{1,0:T(8,128)(2,1)S(1)}, u32[]{:S(2)}, u32[]{:S(2)}) collective-permute-start(bf16[256,448]{1,0:T(8,128)(2,1)S(1)} %reshape.74.own), channel_id=1, source_target_pairs={{0,1},{1,0},{2,3},{3,2},{4,5},{5,4},{6,7},{7,6},{8,9},{9,8},{10,11... | collective-permute-start | bytes 688136 | tf_op jit(solution)/shard_map/ppermute | solution.py:160
  64.7 0.8 copy.40
  67.1 2.8 %shard_map.104 = bf16[4,256,128]{2,1,0:T(8,128)(2,1)} custom-call(s32[2]{0:T(128)} %pad_add_fusion.where, bf16[256,448]{1,0:T(8,128)(2,1)} %copy-done.1, bf16[256,448]{1,0:T(8,128)(2,1)} %copy-done.6, bf16[2,128,448]{2,1,0:T(8,128)(2,1)} %bitcast.75, bf16[2,128,448]{2,1,0:T(8,128)(2,1)} %copy-done.4, bf16[2,128,448]{2,1,0:T(8,128)(2,1)} %copy-done.5, ...), custom_call_target="tpu_custom_call" | custom-call | tf_op jit(solution)/shard_map/pallas_call | solution.py:41
  69.9 10.9 %all_to_all.26.parts = bf16[4,256,128]{2,1,0:T(8,128)(2,1)} all-to-all(bf16[4,256,128]{2,1,0:T(8,128)(2,1)} %shard_map.104), channel_id=1, replica_groups=mesh['x'=4,'z'=16,'y'=4,'core'=2] {'y'}, dimensions={0} | all-to-all | bytes 524288 | tf_op jit(solution)/shard_map/all_to_all | solution.py:17
  80.7 1.9 %shard_map.105.mine = bf16[256,384]{1,0:T(8,128)(2,1)} custom-call(s32[2]{0:T(128)} %pad_add_fusion.where, bf16[4,256,128]{2,1,0:T(8,128)(2,1)} %all_to_all.26.parts, bf16[2,256,128]{2,1,0:T(8,128)(2,1)} %bitcast.79), custom_call_target="tpu_custom_call" | custom-call | tf_op jit(solution)/shard_map/pallas_call | solution.py:41
  82.6 3.0 %collective-permute-start.4 = (bf16[256,384]{1,0:T(8,128)(2,1)}, bf16[256,384]{1,0:T(8,128)(2,1)S(1)}, u32[]{:S(2)}, u32[]{:S(2)}) collective-permute-start(bf16[256,384]{1,0:T(8,128)(2,1)} %shard_map.105.mine), channel_id=1, source_target_pairs={{0,1},{1,0},{2,3},{3,2},{4,5},{5,4},{6,7},{7,6},{8,9},{9,8},{10,11... | collective-permute-start | bytes 589832 | tf_op jit(solution)/shard_map/ppermute | solution.py:182
  85.7 1.2 collective-permute-done.4.theirs
  87.6 4.2 %shard_map.106 = bf16[4,256,512]{2,1,0:T(8,128)(2,1)} custom-call(s32[2]{0:T(128)} %pad_add_fusion.where, bf16[256,384]{1,0:T(8,128)(2,1)} %shard_map.105.mine, bf16[256,384]{1,0:T(8,128)(2,1)} %copy-done.7, bf16[2,3584,128]{2,1,0:T(8,128)(2,1)} %bitcast.66, bf16[2,4,448,128]{3,2,1,0:T(8,128)(2,1)} %copy-done.2), custom_call_target="tpu_custom_call" | custom-call | tf_op jit(solution)/shard_map/pallas_call | solution.py:41
  91.8 19.3 %all_to_all.27.parts = bf16[4,256,512]{2,1,0:T(8,128)(2,1)} all-to-all(bf16[4,256,512]{2,1,0:T(8,128)(2,1)} %shard_map.106), channel_id=1, replica_groups=mesh['x'=4,'z'=16,'y'=4,'core'=2] {'y'}, dimensions={0} | all-to-all | bytes 2097152 | tf_op jit(solution)/shard_map/all_to_all | solution.py:17
  111.0 2.1 %shard_map.107 = bf16[64,4,512]{2,1,0:T(4,128)(2,1)} custom-call(s32[2]{0:T(128)} %pad_add_fusion.where, bf16[4,256,512]{2,1,0:T(8,128)(2,1)} %all_to_all.27.parts), custom_call_target="tpu_custom_call" | custom-call | tf_op jit(solution)/shard_map/pallas_call | solution.py:41
  113.2 11.6 %all-to-all-start.3 = ((bf16[64,4,512]{2,1,0:T(4,128)(2,1)}), bf16[64,4,512]{2,1,0:T(4,128)(2,1)S(1)}, u32[]{:S(2)}, u32[]{:S(2)}) async-start(bf16[64,4,512]{2,1,0:T(4,128)(2,1)} %shard_map.107), calls=%async_computation.3 | async-start | bytes 524288 | tf_op jit(solution)/shard_map/all_to_all | solution.py:17
  125.8 17.8 %all-to-all-done.3 = bf16[64,4,512]{2,1,0:T(4,128)(2,1)S(1)} async-done(((bf16[64,4,512]{2,1,0:T(4,128)(2,1)}), bf16[64,4,512]{2,1,0:T(4,128)(2,1)S(1)}, u32[]{:S(2)}, u32[]{:S(2)}) %all-to-all-start.3) | async-done | bytes 262176 | tf_op jit(solution)/shard_map/all_to_all | solution.py:17
  144.8 2.2 %fusion.36 = (bf16[16,4,1,56,128]{4,3,2,1,0:T(8,128)(2,1)S(1)}, bf16[16,4,1,56,128]{4,3,2,1,0:T(8,128)(2,1)S(1)}, bf16[16,4,1,56,128]{4,3,2,1,0:T(8,128)(2,1)S(1)}) fusion(bf16[16,4,3,56,128]{4,3,2,1,0:T(8,128)(2,1)} %bitcast.72), kind=kLoop, calls=%fused_computation.62 | loop fusion | bytes 5505024 | tf_op jit(solution)/shard_map/slice | solution.py:204
  148.9 16.6 %all_gather.11 = bf16[8,16,3584]{2,1,0:T(8,128)(2,1)S(1)} all-gather(bf16[1,16,3584]{2,1,0:T(8,128)(2,1)S(1)} %all_gather_reshape.3), channel_id=1, replica_groups=mesh['x'=4,'z'=16,'y'=4,'core'=2] {'y','core'}, dimensions={0}, use_global_device_ids=true | all-gather | bytes 1032192 | tf_op jit(solution)/shard_map/all_gather | solution.py:214
  (60 shorter events, 10.1 us)
Async XLA Ops:
  7.2 30.4 %copy-start = (bf16[1,2,3584,128]{3,2,1,0:T(8,128)(2,1)S(1)}, bf16[1,2,3584,128]{3,2,1,0:T(8,128)(2,1)}, u32[]{:S(2)}) copy-start(bf16[1,2,3584,128]{3,2,1,0:T(8,128)(2,1)} %param.12) | copy-start | bytes 5505028
  7.2 35.6 %copy-start.3 = (bf16[1,128,3584]{2,1,0:T(8,128)(2,1)S(1)}, bf16[1,128,3584]{2,1,0:T(8,128)(2,1)}, u32[]{:S(2)}) copy-start(bf16[1,128,3584]{2,1,0:T(8,128)(2,1)} %param.13) | copy-start | bytes 2752516
  7.2 137.6 %all-gather.3.cloned.1.call-start = ((), (), s32[]{:S(2)}) async-start(), calls=%async_computation.5 | async-start | bytes 2924544 | tf_op jit(solution)/shard_map/all_gather | solution.py:139
  21.0 37.0 %all-to-all-start = ((bf16[64,4,448]{2,1,0:T(4,128)(2,1)}), bf16[64,4,448]{2,1,0:T(4,128)(2,1)S(1)}, u32[]{:S(2)}, u32[]{:S(2)}) async-start(bf16[64,4,448]{2,1,0:T(4,128)(2,1)} %reshape.73), calls=%async_computation | async-start | bytes 524288 | tf_op jit(solution)/shard_map/all_to_all | solution.py:17
  38.6 47.0 %collective-permute-start.5 = (bf16[2,4,448,128]{3,2,1,0:T(8,128)(2,1)}, bf16[2,4,448,128]{3,2,1,0:T(8,128)(2,1)S(1)}, u32[]{:S(2)}, u32[]{:S(2)}) collective-permute-start(bf16[2,4,448,128]{3,2,1,0:T(8,128)(2,1)} %dynamic-slice_bitcast_fusion), channel_id=1, source_target_pairs={{0,1},{1,0},{2,3},{3,2},{4,5},{5,4},{6,7},{7,6},{8,9},{9,8},{10,11... | collective-permute-start | bytes 2752520 | tf_op jit(solution)/shard_map/ppermute | solution.py:179
  43.7 22.5 %collective-permute-start.1 = (bf16[2,128,448]{2,1,0:T(8,128)(2,1)S(1)}, bf16[2,128,448]{2,1,0:T(8,128)(2,1)S(1)}, u32[]{:S(2)}, u32[]{:S(2)}) collective-permute-start(bf16[2,128,448]{2,1,0:T(8,128)(2,1)S(1)} %bitcast.76), channel_id=1, source_target_pairs={{0,2},{2,4},{4,6},{6,0},{1,3},{3,5},{5,7},{7,1},{8,10},{10,12},{12... | collective-permute-start | bytes 688136 | tf_op jit(solution)/shard_map/ppermute | solution.py:158
  47.0 19.2 %collective-permute-start.2 = (bf16[2,128,448]{2,1,0:T(8,128)(2,1)S(1)}, bf16[2,128,448]{2,1,0:T(8,128)(2,1)S(1)}, u32[]{:S(2)}, u32[]{:S(2)}) collective-permute-start(bf16[2,128,448]{2,1,0:T(8,128)(2,1)S(1)} %bitcast.77), channel_id=1, source_target_pairs={{0,4},{2,6},{4,0},{6,2},{1,5},{3,7},{5,1},{7,3},{8,12},{10,14},{12... | collective-permute-start | bytes 688136 | tf_op jit(solution)/shard_map/ppermute | solution.py:158
  51.7 14.5 %collective-permute-start.3 = (bf16[2,128,448]{2,1,0:T(8,128)(2,1)S(1)}, bf16[2,128,448]{2,1,0:T(8,128)(2,1)}, u32[]{:S(2)}, u32[]{:S(2)}) collective-permute-start(bf16[2,128,448]{2,1,0:T(8,128)(2,1)S(1)} %bitcast.78), channel_id=1, source_target_pairs={{0,6},{2,0},{4,2},{6,4},{1,7},{3,1},{5,3},{7,5},{8,14},{10,8},{12,... | collective-permute-start | bytes 688136 | tf_op jit(solution)/shard_map/ppermute | solution.py:158
  58.2 8.1 %copy-start.1 = (bf16[256,448]{1,0:T(8,128)(2,1)}, bf16[256,448]{1,0:T(8,128)(2,1)S(1)}, u32[]{:S(2)}) copy-start(bf16[256,448]{1,0:T(8,128)(2,1)S(1)} %reshape.74.own) | copy-start | bytes 688132
  58.2 8.0 %collective-permute-start = (bf16[256,448]{1,0:T(8,128)(2,1)S(1)}, bf16[256,448]{1,0:T(8,128)(2,1)S(1)}, u32[]{:S(2)}, u32[]{:S(2)}) collective-permute-start(bf16[256,448]{1,0:T(8,128)(2,1)S(1)} %reshape.74.own), channel_id=1, source_target_pairs={{0,1},{1,0},{2,3},{3,2},{4,5},{5,4},{6,7},{7,6},{8,9},{9,8},{10,11... | collective-permute-start | bytes 688136 | tf_op jit(solution)/shard_map/ppermute | solution.py:160
  66.2 0.7 copy-start.4
  66.2 0.8 copy-start.5
  66.2 0.9 copy-start.6
  82.6 4.3 %collective-permute-start.4 = (bf16[256,384]{1,0:T(8,128)(2,1)}, bf16[256,384]{1,0:T(8,128)(2,1)S(1)}, u32[]{:S(2)}, u32[]{:S(2)}) collective-permute-start(bf16[256,384]{1,0:T(8,128)(2,1)} %shard_map.105.mine), channel_id=1, source_target_pairs={{0,1},{1,0},{2,3},{3,2},{4,5},{5,4},{6,7},{7,6},{8,9},{9,8},{10,11... | collective-permute-start | bytes 589832 | tf_op jit(solution)/shard_map/ppermute | solution.py:182
  85.6 1.3 copy-start.2
  86.9 0.7 copy-start.7
  91.8 33.0 %copy-start.8 = (bf16[16,3584]{1,0:T(8,128)(2,1)S(1)}, bf16[16,3584]{1,0:T(8,128)(2,1)}, u32[]{:S(2)}) copy-start(bf16[16,3584]{1,0:T(8,128)(2,1)} %param.9) | copy-start | bytes 344068
  91.8 51.9 %copy-start.9 = (s32[16,8]{0,1:T(8,128)S(1)}, s32[16,8]{0,1:T(8,128)}, u32[]{:S(2)}) copy-start(s32[16,8]{0,1:T(8,128)} %param.10) | copy-start | bytes 1540
  91.8 52.9 %copy-start.11 = (f32[16,8]{0,1:T(8,128)S(1)}, f32[16,8]{0,1:T(8,128)}, u32[]{:S(2)}) copy-start(f32[16,8]{0,1:T(8,128)} %param.11) | copy-start | bytes 1540
  113.2 30.4 %all-to-all-start.3 = ((bf16[64,4,512]{2,1,0:T(4,128)(2,1)}), bf16[64,4,512]{2,1,0:T(4,128)(2,1)S(1)}, u32[]{:S(2)}, u32[]{:S(2)}) async-start(bf16[64,4,512]{2,1,0:T(4,128)(2,1)} %shard_map.107), calls=%async_computation.3 | async-start | bytes 524288 | tf_op jit(solution)/shard_map/all_to_all | solution.py:17
  144.8 2.5 %copy-start.10 = (bf16[2,16,128]{2,1,0:T(8,128)(2,1)S(1)}, bf16[2,16,128]{2,1,0:T(8,128)(2,1)}, u32[]{:S(2)}) copy-start(bf16[2,16,128]{2,1,0:T(8,128)(2,1)} %param.17) | copy-start | bytes 24580
Sparse Core Ops, SparseCore 0:
  18.1 78.3 all-gather.2

commit v3 on v2

--- a/solution.py
+++ b/solution.py
@@ -42,8 +42,20 @@
         body,
         out_shape=out_shape,
         in_specs=[smem] + [vmem] * len(arrays),
-        out_specs=vmem,
+        out_specs=jax.tree.map(lambda _: vmem, out_shape),
+        compiler_params=pltpu.CompilerParams(vmem_limit_bytes=10 * 2**20),
     )(scalars, *arrays)
+
+
+def split_kernel(where, whole, *outs):
+    y = where[1]
+    _, features = whole.shape
+    width = features // len(outs)
+    for r, out in enumerate(outs):
+        at = pl.multiple_of(((y + r) % len(outs)) * width, LANES)
+        both = whole[:, pl.ds(at, width)]
+        out[0] = both[:, : width // 2]
+        out[1] = both[:, width // 2 :]
 
 
 def back_kernel(where, own, other, *refs):
@@ -150,13 +162,16 @@
     own_rows = exchange(send, OWNER)
     own_rows = own_rows.reshape(slots, share)
 
-    blocks = w_down[0].reshape(hidden, ys, 2, share).transpose(1, 2, 0, 3)
-    downs = []
-    for r in range(ys):
-        block = lax.dynamic_index_in_dim(blocks, (y + r) % ys, 0, keepdims=False)
-        if r > 0:
-            block = lax.ppermute(block, "y", [(i, (i + r) % ys) for i in range(ys)])
-        downs.append(block)
+    downs = kernel_call(
+        split_kernel,
+        [jax.ShapeDtypeStruct((2, hidden, share), BF16)] * ys,
+        where,
+        w_down[0],
+    )
+    downs = [downs[0]] + [
+        lax.ppermute(downs[r], "y", [(i, (i + r) % ys) for i in range(ys)])
+        for r in range(1, ys)
+    ]
     other_rows = lax.ppermute(own_rows, "core", swap)
     back_part = kernel_call(
         back_kernel,

time: 174 us -> 168 us (0.966)
  Pallas kernels: 10.9 us -> 7.32 us
  blocking collectives: 56.5 us -> 53.7 us
  starting transfers between devices: 52.6 us -> 55.2 us
    pallas_call x4 -> x5, Pallas kernels: 10.9 us -> 7.32 us  [kernel_call(): pl.pallas_call(body, out_shape=out_shape, in_specs=[smem] + [vmem] * len(...]
    all_to_all x3, blocking collectives: 39.9 us -> 37.1 us  [exchange(): return lax.all_to_all(array, axis, 0, 0, tiled=True)]
    all_to_all x2, starting transfers between devices: 28.2 us -> 30.2 us  [exchange(): return lax.all_to_all(array, axis, 0, 0, tiled=True)]
    all_to_all x2, waiting for transfers between devices: 21.1 us -> 19.4 us  [exchange(): return lax.all_to_all(array, axis, 0, 0, tiled=True)]
    unnamed x29 -> x14, local copies, waits for them, and re-layouts: 3.49 us -> 2.11 us
  transfers between devices with their start and end apart: 9 -> 9, of which waited for: 3 -> 4; matrix products, arithmetic and copies ran while one was open for 5% -> 4% of each run, Pallas kernels for 6% -> 4%
where the time goes in v3:
time: 168 us; the launch traced here: 167 us
  starting transfers between devices  55.2 us (33%)
  blocking collectives  53.7 us (32%)
  waiting for transfers between devices  21.6 us (13%)
  between operations  14.3 us (9%)
  local copies, waits for them, and re-layouts  9.24 us (6%)
  Pallas kernels  7.32 us (4%)
  other arithmetic  3.32 us (2%)
  matrix products  2.44 us (1%)
    all_to_all x3, blocking collectives, exchange(): return lax.all_to_all(array, axis, 0, 0, tiled=True)  37.1 us
    all_to_all x2, starting transfers between devices, exchange(): return lax.all_to_all(array, axis, 0, 0, tiled=True)  30.2 us
    all_to_all x2, waiting for transfers between devices, exchange(): return lax.all_to_all(array, axis, 0, 0, tiled=True)  19.4 us
    all_gather x1, blocking collectives, per_device(): everyone = lax.all_gather(shared_term, PARTS, axis=0)  16.6 us
    ppermute x3, starting transfers between devices, per_device(): lax.ppermute(downs[r], 'y', [(i, (i + r) % ys) for i in range(ys)])  10.7 us
    pallas_call x5, Pallas kernels, kernel_call(): pl.pallas_call(body, out_shape=out_shape, in_specs=[smem] + [vmem] * len(...  7.32 us
    ppermute x1, starting transfers between devices, per_device(): other_rows = lax.ppermute(own_rows, 'core', swap)  6.45 us
    ppermute x1, starting transfers between devices, per_device(): lax.ppermute(lax.dynamic_index_in_dim(halves, 1 - core, 2, keepdims=False...  4.1 us
  transfers between devices with their start and end apart: 9, of which 4 were waited for; matrix products, arithmetic and copies ran while one was open for 4% of the time, Pallas kernels for 4%

profile of v3, /device:TPU:1, one launch (start us, length us, event | category | flops | bytes accessed | tf_op | source)
XLA Modules:
  0.0 167.1 jit_solution(5421266407282558976)
XLA Ops:
  8.1 9.8 %all_to_all.25 = bf16[4,3,56,128]{3,2,1,0:T(8,128)(2,1)} all-to-all(bf16[4,3,56,128]{3,2,1,0:T(8,128)(2,1)S(1)} %broadcast_in_dim.5), channel_id=1, replica_groups=mesh['x'=4,'z'=16,'y'=4,'core'=2] {'x'}, dimensions={0} | all-to-all | bytes 344064 | tf_op jit(solution)/shard_map/all_to_all | solution.py:17
  18.9 1.1 convolution_convert_fusion
  20.9 16.9 %all-to-all-start = ((bf16[64,4,448]{2,1,0:T(4,128)(2,1)}), bf16[64,4,448]{2,1,0:T(4,128)(2,1)}, u32[]{:S(2)}, u32[]{:S(2)}) async-start(bf16[64,4,448]{2,1,0:T(4,128)(2,1)} %reshape.73), calls=%async_computation | async-start | bytes 524288 | tf_op jit(solution)/shard_map/all_to_all | solution.py:17
  38.8 4.1 %collective-permute-start.5 = (bf16[2,4,448,128]{3,2,1,0:T(8,128)(2,1)}, bf16[2,4,448,128]{3,2,1,0:T(8,128)(2,1)S(1)}, u32[]{:S(2)}, u32[]{:S(2)}) collective-permute-start(bf16[2,4,448,128]{3,2,1,0:T(8,128)(2,1)} %dynamic-slice_bitcast_fusion), channel_id=1, source_target_pairs={{0,1},{1,0},{2,3},{3,2},{4,5},{5,4},{6,7},{7,6},{8,9},{9,8},{10,11... | collective-permute-start | bytes 2752520 | tf_op jit(solution)/shard_map/ppermute | solution.py:194
  43.0 1.2 copy-done.1
  44.2 1.6 shard_map.104
  45.9 3.2 %collective-permute-start.1 = (bf16[2,128,448]{2,1,0:T(8,128)(2,1)}, bf16[2,128,448]{2,1,0:T(8,128)(2,1)S(1)}, u32[]{:S(2)}, u32[]{:S(2)}) collective-permute-start(bf16[2,128,448]{2,1,0:T(8,128)(2,1)} %get-tuple-element.7), channel_id=1, source_target_pairs={{0,2},{2,4},{4,6},{6,0},{1,3},{3,5},{5,7},{7,1},{8,10},{10,12},{12... | collective-permute-start | bytes 688136 | tf_op jit(solution)/shard_map/ppermute | solution.py:172
  49.1 4.5 %collective-permute-start.2 = (bf16[2,128,448]{2,1,0:T(8,128)(2,1)}, bf16[2,128,448]{2,1,0:T(8,128)(2,1)}, u32[]{:S(2)}, u32[]{:S(2)}) collective-permute-start(bf16[2,128,448]{2,1,0:T(8,128)(2,1)} %get-tuple-element.8), channel_id=1, source_target_pairs={{0,4},{2,6},{4,0},{6,2},{1,5},{3,7},{5,1},{7,3},{8,12},{10,14},{12... | collective-permute-start | bytes 688136 | tf_op jit(solution)/shard_map/ppermute | solution.py:172
  53.6 3.0 %collective-permute-start.3 = (bf16[2,128,448]{2,1,0:T(8,128)(2,1)}, bf16[2,128,448]{2,1,0:T(8,128)(2,1)}, u32[]{:S(2)}, u32[]{:S(2)}) collective-permute-start(bf16[2,128,448]{2,1,0:T(8,128)(2,1)} %get-tuple-element.9), channel_id=1, source_target_pairs={{0,6},{2,0},{4,2},{6,4},{1,7},{3,1},{5,3},{7,5},{8,14},{10,8},{12,... | collective-permute-start | bytes 688136 | tf_op jit(solution)/shard_map/ppermute | solution.py:172
  56.6 1.5 all-to-all-done
  58.1 1.1 reshape.74.own
  59.2 6.4 %collective-permute-start = (bf16[256,448]{1,0:T(8,128)(2,1)S(1)}, bf16[256,448]{1,0:T(8,128)(2,1)S(1)}, u32[]{:S(2)}, u32[]{:S(2)}) collective-permute-start(bf16[256,448]{1,0:T(8,128)(2,1)S(1)} %reshape.74.own), channel_id=1, source_target_pairs={{0,1},{1,0},{2,3},{3,2},{4,5},{5,4},{6,7},{7,6},{8,9},{9,8},{10,11... | collective-permute-start | bytes 688136 | tf_op jit(solution)/shard_map/ppermute | solution.py:175
  65.7 1.1 collective-permute-done.other
  66.8 1.8 %shard_map.105 = bf16[4,256,128]{2,1,0:T(8,128)(2,1)S(1)} custom-call(s32[2]{0:T(128)S(1)} %pad_add_fusion.where, bf16[256,448]{1,0:T(8,128)(2,1)S(1)} %reshape.74.own, bf16[256,448]{1,0:T(8,128)(2,1)S(1)} %collective-permute-done.other, bf16[2,128,448]{2,1,0:T(8,128)(2,1)S(1)} %get-tuple-element.6.refs_0_, ...), custom_call_target="tpu_custom_call" | custom-call | tf_op jit(solution)/shard_map/pallas_call | solution.py:41
  68.6 9.9 %all_to_all.26.parts = bf16[4,256,128]{2,1,0:T(8,128)(2,1)S(1)} all-to-all(bf16[4,256,128]{2,1,0:T(8,128)(2,1)S(1)} %shard_map.105), channel_id=1, replica_groups=mesh['x'=4,'z'=16,'y'=4,'core'=2] {'y'}, dimensions={0} | all-to-all | bytes 524288 | tf_op jit(solution)/shard_map/all_to_all | solution.py:17
  80.1 3.7 %collective-permute-start.4 = (bf16[256,384]{1,0:T(8,128)(2,1)S(1)}, bf16[256,384]{1,0:T(8,128)(2,1)S(1)}, u32[]{:S(2)}, u32[]{:S(2)}) collective-permute-start(bf16[256,384]{1,0:T(8,128)(2,1)S(1)} %shard_map.106.mine), channel_id=1, source_target_pairs={{0,1},{1,0},{2,3},{3,2},{4,5},{5,4},{6,7},{7,6},{8,9},{9,8},{10,11... | collective-permute-start | bytes 589832 | tf_op jit(solution)/shard_map/ppermute | solution.py:197
  83.8 1.0 collective-permute-done.4.theirs
  84.8 1.8 %shard_map.107 = bf16[4,256,512]{2,1,0:T(8,128)(2,1)S(1)} custom-call(s32[2]{0:T(128)S(1)} %pad_add_fusion.where, bf16[256,384]{1,0:T(8,128)(2,1)S(1)} %shard_map.106.mine, bf16[256,384]{1,0:T(8,128)(2,1)S(1)} %collective-permute-done.4.theirs, bf16[2,3584,128]{2,1,0:T(8,128)(2,1)S(1)} %bitcast.55, bf16[2,4,448,128]{3,2,1,0:T(8,128)(2,1)S(1)} %collective-permute-done.5.other), custom_call_target="tpu_custom_call" | custom-call | tf_op jit(solution)/shard_map/pallas_call | solution.py:41
  86.6 17.4 %all_to_all.27.parts = bf16[4,256,512]{2,1,0:T(8,128)(2,1)S(1)} all-to-all(bf16[4,256,512]{2,1,0:T(8,128)(2,1)S(1)} %shard_map.107), channel_id=1, replica_groups=mesh['x'=4,'z'=16,'y'=4,'core'=2] {'y'}, dimensions={0} | all-to-all | bytes 2097152 | tf_op jit(solution)/shard_map/all_to_all | solution.py:17
  104.0 1.4 shard_map.108
  105.4 13.4 %all-to-all-start.3 = ((bf16[64,4,512]{2,1,0:T(4,128)(2,1)}), bf16[64,4,512]{2,1,0:T(4,128)(2,1)S(1)}, u32[]{:S(2)}, u32[]{:S(2)}) async-start(bf16[64,4,512]{2,1,0:T(4,128)(2,1)} %shard_map.108), calls=%async_computation.3 | async-start | bytes 524288 | tf_op jit(solution)/shard_map/all_to_all | solution.py:17
  119.8 17.8 %all-to-all-done.3 = bf16[64,4,512]{2,1,0:T(4,128)(2,1)S(1)} async-done(((bf16[64,4,512]{2,1,0:T(4,128)(2,1)}), bf16[64,4,512]{2,1,0:T(4,128)(2,1)S(1)}, u32[]{:S(2)}, u32[]{:S(2)}) %all-to-all-start.3) | async-done | bytes 262176 | tf_op jit(solution)/shard_map/all_to_all | solution.py:17
  138.9 2.2 %fusion.36 = (bf16[16,4,1,56,128]{4,3,2,1,0:T(8,128)(2,1)S(1)}, bf16[16,4,1,56,128]{4,3,2,1,0:T(8,128)(2,1)S(1)}, bf16[16,4,1,56,128]{4,3,2,1,0:T(8,128)(2,1)S(1)}) fusion(bf16[16,4,3,56,128]{4,3,2,1,0:T(8,128)(2,1)} %bitcast.61), kind=kLoop, calls=%fused_computation.58 | loop fusion | bytes 5505024 | tf_op jit(solution)/shard_map/slice | solution.py:219
  142.9 16.6 %all_gather.11 = bf16[8,16,3584]{2,1,0:T(8,128)(2,1)S(1)} all-gather(bf16[1,16,3584]{2,1,0:T(8,128)(2,1)S(1)} %all_gather_reshape.3), channel_id=1, replica_groups=mesh['x'=4,'z'=16,'y'=4,'core'=2] {'y','core'}, dimensions={0}, use_global_device_ids=true | all-gather | bytes 1032192 | tf_op jit(solution)/shard_map/all_gather | solution.py:229
  (45 shorter events, 10.2 us)
Async XLA Ops:
  7.2 30.7 %copy-start = (bf16[1,2,3584,128]{3,2,1,0:T(8,128)(2,1)S(1)}, bf16[1,2,3584,128]{3,2,1,0:T(8,128)(2,1)}, u32[]{:S(2)}) copy-start(bf16[1,2,3584,128]{3,2,1,0:T(8,128)(2,1)} %param.12) | copy-start | bytes 5505028
  7.2 131.7 %all-gather.3.cloned.1.call-start = ((), (), s32[]{:S(2)}) async-start(), calls=%async_computation.5 | async-start | bytes 2924544 | tf_op jit(solution)/shard_map/all_gather | solution.py:151
  20.9 37.2 %all-to-all-start = ((bf16[64,4,448]{2,1,0:T(4,128)(2,1)}), bf16[64,4,448]{2,1,0:T(4,128)(2,1)}, u32[]{:S(2)}, u32[]{:S(2)}) async-start(bf16[64,4,448]{2,1,0:T(4,128)(2,1)} %reshape.73), calls=%async_computation | async-start | bytes 524288 | tf_op jit(solution)/shard_map/all_to_all | solution.py:17
  38.8 44.9 %collective-permute-start.5 = (bf16[2,4,448,128]{3,2,1,0:T(8,128)(2,1)}, bf16[2,4,448,128]{3,2,1,0:T(8,128)(2,1)S(1)}, u32[]{:S(2)}, u32[]{:S(2)}) collective-permute-start(bf16[2,4,448,128]{3,2,1,0:T(8,128)(2,1)} %dynamic-slice_bitcast_fusion), channel_id=1, source_target_pairs={{0,1},{1,0},{2,3},{3,2},{4,5},{5,4},{6,7},{7,6},{8,9},{9,8},{10,11... | collective-permute-start | bytes 2752520 | tf_op jit(solution)/shard_map/ppermute | solution.py:194
  43.0 1.2 copy-start.1
  45.9 19.8 %collective-permute-start.1 = (bf16[2,128,448]{2,1,0:T(8,128)(2,1)}, bf16[2,128,448]{2,1,0:T(8,128)(2,1)S(1)}, u32[]{:S(2)}, u32[]{:S(2)}) collective-permute-start(bf16[2,128,448]{2,1,0:T(8,128)(2,1)} %get-tuple-element.7), channel_id=1, source_target_pairs={{0,2},{2,4},{4,6},{6,0},{1,3},{3,5},{5,7},{7,1},{8,10},{10,12},{12... | collective-permute-start | bytes 688136 | tf_op jit(solution)/shard_map/ppermute | solution.py:172
  49.1 16.6 %collective-permute-start.2 = (bf16[2,128,448]{2,1,0:T(8,128)(2,1)}, bf16[2,128,448]{2,1,0:T(8,128)(2,1)}, u32[]{:S(2)}, u32[]{:S(2)}) collective-permute-start(bf16[2,128,448]{2,1,0:T(8,128)(2,1)} %get-tuple-element.8), channel_id=1, source_target_pairs={{0,4},{2,6},{4,0},{6,2},{1,5},{3,7},{5,1},{7,3},{8,12},{10,14},{12... | collective-permute-start | bytes 688136 | tf_op jit(solution)/shard_map/ppermute | solution.py:172
  53.6 12.1 %collective-permute-start.3 = (bf16[2,128,448]{2,1,0:T(8,128)(2,1)}, bf16[2,128,448]{2,1,0:T(8,128)(2,1)}, u32[]{:S(2)}, u32[]{:S(2)}) collective-permute-start(bf16[2,128,448]{2,1,0:T(8,128)(2,1)} %get-tuple-element.9), channel_id=1, source_target_pairs={{0,6},{2,0},{4,2},{6,4},{1,7},{3,1},{5,3},{7,5},{8,14},{10,8},{12,... | collective-permute-start | bytes 688136 | tf_op jit(solution)/shard_map/ppermute | solution.py:172
  59.2 7.6 %collective-permute-start = (bf16[256,448]{1,0:T(8,128)(2,1)S(1)}, bf16[256,448]{1,0:T(8,128)(2,1)S(1)}, u32[]{:S(2)}, u32[]{:S(2)}) collective-permute-start(bf16[256,448]{1,0:T(8,128)(2,1)S(1)} %reshape.74.own), channel_id=1, source_target_pairs={{0,1},{1,0},{2,3},{3,2},{4,5},{5,4},{6,7},{7,6},{8,9},{9,8},{10,11... | collective-permute-start | bytes 688136 | tf_op jit(solution)/shard_map/ppermute | solution.py:175
  78.5 0.9 copy-start.2
  80.1 4.7 %collective-permute-start.4 = (bf16[256,384]{1,0:T(8,128)(2,1)S(1)}, bf16[256,384]{1,0:T(8,128)(2,1)S(1)}, u32[]{:S(2)}, u32[]{:S(2)}) collective-permute-start(bf16[256,384]{1,0:T(8,128)(2,1)S(1)} %shard_map.106.mine), channel_id=1, source_target_pairs={{0,1},{1,0},{2,3},{3,2},{4,5},{5,4},{6,7},{7,6},{8,9},{9,8},{10,11... | collective-permute-start | bytes 589832 | tf_op jit(solution)/shard_map/ppermute | solution.py:197
  86.6 32.2 %copy-start.3 = (bf16[16,3584]{1,0:T(8,128)(2,1)S(1)}, bf16[16,3584]{1,0:T(8,128)(2,1)}, u32[]{:S(2)}) copy-start(bf16[16,3584]{1,0:T(8,128)(2,1)} %param.9) | copy-start | bytes 344068
  86.6 51.1 %copy-start.4 = (s32[16,8]{0,1:T(8,128)S(1)}, s32[16,8]{0,1:T(8,128)}, u32[]{:S(2)}) copy-start(s32[16,8]{0,1:T(8,128)} %param.10) | copy-start | bytes 1540
  86.6 52.1 %copy-start.6 = (f32[16,8]{0,1:T(8,128)S(1)}, f32[16,8]{0,1:T(8,128)}, u32[]{:S(2)}) copy-start(f32[16,8]{0,1:T(8,128)} %param.11) | copy-start | bytes 1540
  105.4 32.2 %all-to-all-start.3 = ((bf16[64,4,512]{2,1,0:T(4,128)(2,1)}), bf16[64,4,512]{2,1,0:T(4,128)(2,1)S(1)}, u32[]{:S(2)}, u32[]{:S(2)}) async-start(bf16[64,4,512]{2,1,0:T(4,128)(2,1)} %shard_map.108), calls=%async_computation.3 | async-start | bytes 524288 | tf_op jit(solution)/shard_map/all_to_all | solution.py:17
  138.8 2.5 %copy-start.5 = (bf16[2,16,128]{2,1,0:T(8,128)(2,1)S(1)}, bf16[2,16,128]{2,1,0:T(8,128)(2,1)}, u32[]{:S(2)}) copy-start(bf16[2,16,128]{2,1,0:T(8,128)(2,1)} %param.17) | copy-start | bytes 24580
Sparse Core Ops, SparseCore 0:
  18.1 77.7 all-gather.2

commit v4 on v3

v4 whole, which is shorter than its diff:
```python
import jax
import jax.numpy as jnp
from jax import lax
from jax.experimental import pallas as pl
from jax.experimental.pallas import tpu as pltpu
from jax.sharding import Mesh
from jax.sharding import PartitionSpec as P

OWNER = ("x", "z")
PARTS = ("y", "core")
F32 = jnp.float32
BF16 = jnp.bfloat16
LANES = 128


def exchange(array, axis):
    return lax.all_to_all(array, axis, 0, 0, tiled=True)


def contract_last(left, right):
    return lax.dot_general(left, right, (((1,), (1,)), ((), ())), preferred_element_type=F32)


def swiglu_grads(back_grad, saved_gate, saved_up):
    pre_gate = saved_gate.astype(F32)
    pre_up = saved_up.astype(F32)
    sigmoid = jax.nn.sigmoid(pre_gate)
    grad_gate = (back_grad * pre_up * sigmoid * (1.0 + pre_gate * (1.0 - sigmoid))).astype(BF16)
    grad_up = (back_grad * pre_gate * sigmoid).astype(BF16)
    return grad_gate, grad_up


def kernel_call(body, out_shape, scalars, *arrays):
    smem = pl.BlockSpec(memory_space=pltpu.SMEM)
    vmem = pl.BlockSpec(memory_space=pltpu.VMEM)
    return pl.pallas_call(
        body,
        out_shape=out_shape,
        in_specs=[smem] + [vmem] * len(arrays),
        out_specs=jax.tree.map(lambda _: vmem, out_shape),
        compiler_params=pltpu.CompilerParams(vmem_limit_bytes=10 * 2**20),
    )(scalars, *arrays)


def spread_kernel(where, pair, last, out):
    for peer in range(out.shape[0]):
        out[peer, :2] = pair[...]
        out[peer, 2] = last[...]


def route_kernel(where, ids, tokens, out):
    core, y = where[0], where[1]
    experts, half, width = out.shape
    count = tokens.shape[0]
    shape = (experts * half, count)
    row = lax.broadcasted_iota(jnp.int32, shape, 0)
    expert = row // half
    chosen = ids[0:1, :] == expert
    for k in range(1, ids.shape[0]):
        chosen = chosen | (ids[k : k + 1, :] == expert)
    chosen = jnp.where(chosen, 1.0, 0.0)
    first = lax.broadcasted_iota(jnp.int32, (count, count), 0)
    second = lax.broadcasted_iota(jnp.int32, (count, count), 1)
    earlier = jnp.where(first < second, 1.0, 0.0).astype(BF16)
    before = jnp.dot(chosen.astype(BF16), earlier, preferred_element_type=F32)
    place = (row % half + half * core).astype(F32)
    source = jnp.where(before == place, chosen, 0.0).astype(BF16)
    columns = tokens[:, pl.ds(pl.multiple_of(y * width, LANES), width)]
    rows = jnp.dot(source, columns, preferred_element_type=F32).astype(BF16)
    out[...] = rows.reshape(out.shape)


def shared_kernel(where, turned, pieces, saved, out):
    count = pieces.shape[0]
    back_grad = jnp.zeros(saved.shape[1:], F32)
    for z in range(count):
        back_grad += jnp.dot(turned[z], pieces[z, 2], preferred_element_type=F32)
    grads = jnp.concatenate(swiglu_grads(back_grad, saved[0], saved[1]), axis=1)
    for z in range(count):
        weights = jnp.concatenate([pieces[z, 0], pieces[z, 1]], axis=1)
        out[z] = contract_last(grads, weights).astype(BF16)


def split_kernel(where, whole, *outs):
    y = where[1]
    width = whole.shape[1] // len(outs)
    for r, out in enumerate(outs):
        at = pl.multiple_of(((y + r) % len(outs)) * width, LANES)
        out[...] = whole[:, pl.ds(at, width)]


def back_kernel(where, arrived, own, other, out):
    y = where[1]
    ys, hidden = own.shape[:2]
    rows = arrived[...].reshape(out.shape[1], own.shape[2])
    for r in range(ys):
        home = (y + ys - r) % ys
        out[home, :, :hidden] = contract_last(rows, own[r]).astype(BF16)
        out[home, :, hidden:] = contract_last(rows, other[r]).astype(BF16)


def gate_kernel(where, parts, own, other, grads, gates):
    core = where[0]
    back_grad = jnp.sum(parts[...].astype(F32), axis=0)
    rows, width = back_grad.shape
    slots = own.shape[1]
    row = lax.broadcasted_iota(jnp.int32, (rows, slots), 0)
    slot = lax.broadcasted_iota(jnp.int32, (rows, slots), 1)
    take = jnp.where(slot == (row // 2) * 4 + row % 2 + 2 * core, 1.0, 0.0).astype(BF16)

    def saved(g):
        mine = jnp.dot(take, own[g], preferred_element_type=F32)
        theirs = jnp.dot(take, other[g], preferred_element_type=F32)
        return jnp.concatenate([mine, theirs], axis=1)

    pre_gate, pre_up = saved(0), saved(1)
    sigmoid = jax.nn.sigmoid(pre_gate)
    grad_gate = back_grad * pre_up * sigmoid * (1.0 + pre_gate * (1.0 - sigmoid))
    grad_up = back_grad * pre_gate * sigmoid
    term = jnp.sum(grad_up * pre_up, axis=1, keepdims=True)
    grads[:, :width] = grad_gate.astype(BF16)
    grads[:, width:] = grad_up.astype(BF16)
    gates[...] = jnp.broadcast_to(term, (rows, rows)).T.astype(BF16)


def row_kernel(where, grads, gates, own, other, out):
    ys, width = out.shape[0], out.shape[2]
    rows = grads.shape[0]
    extra = out.shape[1] - rows
    for y in range(ys):
        at = slice(y * width, (y + 1) * width)
        weights = jnp.concatenate(
            [own[0, at, :], other[0, at, :], own[1, at, :], other[1, at, :]], axis=1
        )
        out[y, :rows, :] = contract_last(grads[...], weights).astype(BF16)
        out[y, rows:, :rows] = gates[:extra, :]
        out[y, rows:, rows:] = jnp.zeros((extra, width - rows), BF16)


def pack_kernel(where, parts, out):
    rows = out.shape[0] * out.shape[1]
    total = jnp.sum(parts[...].astype(F32), axis=0)
    gates = jnp.broadcast_to(total[rows : rows + 1, :rows], (rows, rows)).T
    high = gates.astype(BF16).astype(F32)
    lane = lax.broadcasted_iota(jnp.int32, (rows, rows), 1)
    spare = jnp.where(lane == 0, high, jnp.where(lane == 1, gates - high, 0.0))
    packed = jnp.concatenate([total[:rows], spare], axis=1)
    out[...] = packed.astype(BF16).reshape(out.shape)


def pick_kernel(where, ids, gate_values, returned, keep, give):
    core = where[0]
    count, choose = ids.shape
    half = returned.shape[1]
    rows = returned.shape[0] * half
    share = (returned.shape[2] - LANES) // 2
    row = lax.broadcasted_iota(jnp.int32, (count, rows), 1)
    expert = row // half
    hits = [jnp.where(ids[:, k : k + 1] == expert, 1.0, 0.0) for k in range(choose)]
    chosen = sum(hits[1:], hits[0])
    first = lax.broadcasted_iota(jnp.int32, (count, count), 1)
    second = lax.broadcasted_iota(jnp.int32, (count, count), 0)
    earlier = jnp.where(first < second, 1.0, 0.0).astype(BF16)
    before = jnp.dot(earlier, chosen.astype(BF16), preferred_element_type=F32)
    place = (row % half + half * core).astype(F32)
    source = jnp.where(before == place, chosen, 0.0)
    weight = sum(hits[k] * gate_values[:, k : k + 1] for k in range(choose)) * source
    high = weight.astype(BF16)
    low = (weight - high.astype(F32)).astype(BF16)
    values = returned[...].reshape(rows, returned.shape[2])
    routed = jnp.dot(high, values, preferred_element_type=F32)
    routed += jnp.dot(low, values, preferred_element_type=F32)
    tail = values[:, 2 * share :].astype(F32)
    gates = jnp.broadcast_to(tail[:, 0:1] + tail[:, 1:2], (rows, rows)).T[0:1, :]
    lane = lax.broadcasted_iota(jnp.int32, (count, LANES), 1)
    spare = jnp.zeros((count, LANES), F32)
    for k in range(choose):
        term = jnp.sum(hits[k] * source * gates, axis=1, keepdims=True)
        spare = jnp.where(lane == k, term, spare)
    left, right = routed[:, :share], routed[:, share : 2 * share]
    keep[:, :share] = jnp.where(core == 0, left, right)
    give[:, :share] = jnp.where(core == 0, right, left)
    keep[:, share:] = spare[:, : keep.shape[1] - share]
    give[:, share:] = spare[:, : keep.shape[1] - share]


def per_device(
    grad_out,
    expert_ids,
    gate_values,
    w_gate_up,
    w_down,
    saved_routed,
    shared_gate_up,
    shared_down,
    saved_shared,
):
    experts = lax.axis_size(OWNER)
    xs = lax.axis_size("x")
    zs = lax.axis_size("z")
    ys = lax.axis_size("y")
    parts = lax.axis_size(PARTS)
    tokens, features = grad_out.shape
    choose = expert_ids.shape[1]
    slots = saved_routed.shape[2]
    hidden = w_down.shape[1]
    capacity = slots // experts
    share = features // parts
    core = lax.axis_index("core")
    y = lax.axis_index("y")
    part = lax.axis_index(PARTS)
    swap = [(0, 1), (1, 0)]
    where = jnp.stack([core, y]).astype(jnp.int32)
    half = capacity // 2
    width = 2 * share
    rows = experts * half

    spread = kernel_call(
        spread_kernel,
        jax.ShapeDtypeStruct((xs, 3, *shared_gate_up.shape[1:]), BF16),
        where,
        shared_gate_up,
        shared_down.T,
    )
    column = exchange(spread, "x")
    column = column.transpose(1, 0, 2, 3).reshape(3, -1, hidden)
    pieces = lax.all_gather(column, "z", axis=0)

    send = kernel_call(
        route_kernel,
        jax.ShapeDtypeStruct((experts, half, width), BF16),
        where,
        expert_ids.T,
        grad_out,
    )
    arrived = exchange(send, OWNER)

    downs = kernel_call(
        split_kernel,
        [jax.ShapeDtypeStruct((hidden, width), BF16)] * ys,
        where,
        w_down[0],
    )
    downs = [downs[0]] + [
        lax.ppermute(downs[r], "y", [(i, (i + r) % ys) for i in range(ys)])
        for r in range(1, ys)
    ]
    own_down = jnp.stack(downs)
    other_down = lax.ppermute(own_down, "core", swap)
    other_saved = lax.ppermute(saved_routed[0], "core", swap)
    other_gate_up = lax.ppermute(w_gate_up[0], "core", swap)

    back_part = kernel_call(
        back_kernel,
        jax.ShapeDtypeStruct((ys, rows, 2 * hidden), BF16),
        where,
        arrived,
        own_down,
        other_down,
    )
    back_parts = exchange(back_part, "y")
    grads, gates = kernel_call(
        gate_kernel,
        [
            jax.ShapeDtypeStruct((rows, 4 * hidden), BF16),
            jax.ShapeDtypeStruct((rows, rows), BF16),
        ],
        where,
        back_parts,
        saved_routed[0],
        other_saved,
    )
    row_part = kernel_call(
        row_kernel,
        jax.ShapeDtypeStruct((ys, rows + 8, width), BF16),
        where,
        grads,
        gates,
        w_gate_up[0],
        other_gate_up,
    )
    row_parts = exchange(row_part, "y")
    finished = kernel_call(
        pack_kernel,
        jax.ShapeDtypeStruct((experts, half, width + LANES), BF16),
        where,
        row_parts,
    )
    returned = exchange(finished, OWNER)

    turned = grad_out.reshape(tokens, xs, zs, -1).transpose(2, 0, 1, 3)
    turned = turned.reshape(zs, tokens, -1)
    shared_term = kernel_call(
        shared_kernel,
        jax.ShapeDtypeStruct((zs, tokens, features // zs), BF16),
        where,
        turned,
        pieces,
        saved_shared,
    )
    shared_term = shared_term.reshape(zs, tokens, xs, -1).transpose(1, 2, 0, 3)
    shared_term = shared_term.reshape(tokens, features)
    everyone = lax.all_gather(shared_term, PARTS, axis=0)
    ours = lax.dynamic_slice_in_dim(everyone, part * share, share, 2)
    shared_sum = jnp.sum(ours.astype(F32), axis=0)

    keep, give = kernel_call(
        pick_kernel,
        [jax.ShapeDtypeStruct((tokens, share + 64), F32)] * 2,
        where,
        expert_ids,
        gate_values,
        returned,
    )
    taken = lax.ppermute(give, "core", swap)
    total = keep + taken
    grad_in = (total[:, :share] + shared_sum).astype(BF16)
    return grad_in, total[:, share : share + choose]


def solution(mesh):
    finer = Mesh(mesh.devices.reshape(4, 16, 4, 2), ("x", "z", "y", "core"))
    placed = (
        P(OWNER, None),
        P(OWNER, None),
        P(OWNER, None),
        P(OWNER, None, None, PARTS),
        P(OWNER, PARTS, None),
        P(OWNER, None, None, PARTS),
        P(None, OWNER, PARTS),
        P(PARTS, OWNER),
        P(None, OWNER, PARTS),
    )

    return jax.shard_map(
        per_device,
        mesh=finer,
        in_specs=placed,
        out_specs=(P(OWNER, PARTS), P(OWNER, None)),
        check_vma=False,
    )
```

time: 168 us -> 180 us (1.071)
  blocking collectives: 53.7 us -> 76.5 us
  starting transfers between devices: 55.2 us -> 37.6 us
  waiting for transfers between devices: 21.6 us -> 29.8 us
  Pallas kernels: 7.32 us -> 12.1 us
  matrix products: 2.44 us -> 0 us
  other arithmetic: 3.32 us -> 0.94 us
    all_to_all x3, blocking collectives: 37.1 us -> 62.7 us  [exchange(): return lax.all_to_all(array, axis, 0, 0, tiled=True)]
    all_to_all x2, starting transfers between devices: 30.2 us -> 10.2 us  [exchange(): return lax.all_to_all(array, axis, 0, 0, tiled=True)]
    ppermute x3, waiting for transfers between devices: 0.01 us -> 10.6 us  [per_device(): lax.ppermute(downs[r], 'y', [(i, (i + r) % ys) for i in range(ys)])]
    ppermute x3 -> x4, starting transfers between devices: 14.2 us -> 20.2 us  [the longest x1 7.62 us: per_device(): other_gate_up = lax.ppermute(w_gate_up[0], 'core', swap)]
    pallas_call x5 -> x9, Pallas kernels: 7.32 us -> 12.1 us  [kernel_call(): pl.pallas_call(body, out_shape=out_shape, in_specs=[smem] + [vmem] * len(...]
    ppermute x3, starting transfers between devices: 10.7 us -> 7.2 us  [per_device(): lax.ppermute(downs[r], 'y', [(i, (i + r) % ys) for i in range(ys)])]
    unnamed x14 -> x23, local copies, waits for them, and re-layouts: 2.11 us -> 5.25 us
    all_gather x1, blocking collectives: 16.6 us -> 13.8 us  [per_device(): everyone = lax.all_gather(shared_term, PARTS, axis=0)]
  transfers between devices with their start and end apart: 9 -> 10, of which waited for: 4 -> 6; matrix products, arithmetic and copies ran while one was open for 4% -> 1% of each run, Pallas kernels for 4% -> 5%
where the time goes in v4:
time: 180 us; the launch traced here: 179 us
  blocking collectives  76.5 us (42%)
  starting transfers between devices  37.6 us (21%)
  waiting for transfers between devices  29.8 us (17%)
  between operations  14.3 us (8%)
  Pallas kernels  12.1 us (7%)
  local copies, waits for them, and re-layouts  7.5 us (4%)
    all_to_all x3, blocking collectives, exchange(): return lax.all_to_all(array, axis, 0, 0, tiled=True)  62.7 us
    all_to_all x2, waiting for transfers between devices, exchange(): return lax.all_to_all(array, axis, 0, 0, tiled=True)  18.2 us
    all_gather x1, blocking collectives, per_device(): everyone = lax.all_gather(shared_term, PARTS, axis=0)  13.8 us
    pallas_call x9, Pallas kernels, kernel_call(): pl.pallas_call(body, out_shape=out_shape, in_specs=[smem] + [vmem] * len(...  12.1 us
    ppermute x3, waiting for transfers between devices, per_device(): lax.ppermute(downs[r], 'y', [(i, (i + r) % ys) for i in range(ys)])  10.6 us
    all_to_all x2, starting transfers between devices, exchange(): return lax.all_to_all(array, axis, 0, 0, tiled=True)  10.2 us
    ppermute x1, starting transfers between devices, per_device(): other_gate_up = lax.ppermute(w_gate_up[0], 'core', swap)  7.62 us
    ppermute x3, starting transfers between devices, per_device(): lax.ppermute(downs[r], 'y', [(i, (i + r) % ys) for i in range(ys)])  7.2 us
  transfers between devices with their start and end apart: 10, of which 6 were waited for; matrix products, arithmetic and copies ran while one was open for 1% of the time, Pallas kernels for 5%

profile of v4, /device:TPU:1, one launch (start us, length us, event | category | flops | bytes accessed | tf_op | source)
XLA Modules:
  0.0 178.7 jit_solution(7764086370652009967)
XLA Ops:
  9.3 9.8 %all_to_all.25 = bf16[4,3,56,128]{3,2,1,0:T(8,128)(2,1)S(1)} all-to-all(bf16[4,3,56,128]{3,2,1,0:T(8,128)(2,1)S(1)} %shard_map.111), channel_id=1, replica_groups=mesh['x'=4,'z'=16,'y'=4,'core'=2] {'x'}, dimensions={0} | all-to-all | bytes 344064 | tf_op jit(solution)/shard_map/all_to_all | solution.py:17
  19.9 7.6 %collective-permute-start.5 = (bf16[2,3584,128]{2,1,0:T(8,128)(2,1)}, bf16[2,3584,128]{2,1,0:T(8,128)(2,1)}, u32[]{:S(2)}, u32[]{:S(2)}) collective-permute-start(bf16[2,3584,128]{2,1,0:T(8,128)(2,1)} %bitcast.21), channel_id=1, source_target_pairs={{0,1},{1,0},{2,3},{3,2},{4,5},{5,4},{6,7},{7,6},{8,9},{9,8},{10,11... | collective-permute-start | bytes 5505032 | tf_op jit(solution)/shard_map/ppermute | solution.py:251
  27.5 1.2 copy-done.2
  29.3 1.9 %collective-permute-start.2 = (bf16[128,896]{1,0:T(8,128)(2,1)S(1)}, bf16[128,896]{1,0:T(8,128)(2,1)S(1)}, u32[]{:S(2)}, u32[]{:S(2)}) collective-permute-start(bf16[128,896]{1,0:T(8,128)(2,1)S(1)} %get-tuple-element.13), channel_id=1, source_target_pairs={{0,6},{2,0},{4,2},{6,4},{1,7},{3,1},{5,3},{7,5},{8,14},{10,8},{12,... | collective-permute-start | bytes 688136 | tf_op jit(solution)/shard_map/ppermute | solution.py:245
  31.2 1.9 %collective-permute-start.1 = (bf16[128,896]{1,0:T(8,128)(2,1)S(1)}, bf16[128,896]{1,0:T(8,128)(2,1)S(1)}, u32[]{:S(2)}, u32[]{:S(2)}) collective-permute-start(bf16[128,896]{1,0:T(8,128)(2,1)S(1)} %get-tuple-element.12), channel_id=1, source_target_pairs={{0,4},{2,6},{4,0},{6,2},{1,5},{3,7},{5,1},{7,3},{8,12},{10,14},{12... | collective-permute-start | bytes 688136 | tf_op jit(solution)/shard_map/ppermute | solution.py:245
  33.2 3.4 %collective-permute-start = (bf16[128,896]{1,0:T(8,128)(2,1)S(1)}, bf16[128,896]{1,0:T(8,128)(2,1)S(1)}, u32[]{:S(2)}, u32[]{:S(2)}) collective-permute-start(bf16[128,896]{1,0:T(8,128)(2,1)S(1)} %get-tuple-element.11), channel_id=1, source_target_pairs={{0,2},{2,4},{4,6},{6,0},{1,3},{3,5},{5,7},{7,1},{8,10},{10,12},{12... | collective-permute-start | bytes 688136 | tf_op jit(solution)/shard_map/ppermute | solution.py:245
  36.5 1.8 %collective-permute-done.2 = bf16[128,896]{1,0:T(8,128)(2,1)S(1)} collective-permute-done((bf16[128,896]{1,0:T(8,128)(2,1)S(1)}, bf16[128,896]{1,0:T(8,128)(2,1)S(1)}, u32[]{:S(2)}, u32[]{:S(2)}) %collective-permute-start.2) | collective-permute-done | bytes 229408 | tf_op jit(solution)/shard_map/ppermute | solution.py:245
  38.3 3.4 %collective-permute-done.1 = bf16[128,896]{1,0:T(8,128)(2,1)S(1)} collective-permute-done((bf16[128,896]{1,0:T(8,128)(2,1)S(1)}, bf16[128,896]{1,0:T(8,128)(2,1)S(1)}, u32[]{:S(2)}, u32[]{:S(2)}) %collective-permute-start.1) | collective-permute-done | bytes 229408 | tf_op jit(solution)/shard_map/ppermute | solution.py:245
  41.8 5.3 %collective-permute-done = bf16[128,896]{1,0:T(8,128)(2,1)S(1)} collective-permute-done((bf16[128,896]{1,0:T(8,128)(2,1)S(1)}, bf16[128,896]{1,0:T(8,128)(2,1)S(1)}, u32[]{:S(2)}, u32[]{:S(2)}) %collective-permute-start) | collective-permute-done | bytes 229408 | tf_op jit(solution)/shard_map/ppermute | solution.py:245
  47.3 2.5 %collective-permute-start.3 = (bf16[4,128,896]{2,1,0:T(8,128)(2,1)S(1)}, bf16[4,128,896]{2,1,0:T(8,128)(2,1)S(1)}, u32[]{:S(2)}, u32[]{:S(2)}) collective-permute-start(bf16[4,128,896]{2,1,0:T(8,128)(2,1)S(1)} %pad_maximum_fusion.own), channel_id=1, source_target_pairs={{0,1},{1,0},{2,3},{3,2},{4,5},{5,4},{6,7},{7,6},{8,9},{9,8},{10,11... | collective-permute-start | bytes 2752520 | tf_op jit(solution)/shard_map/ppermute | solution.py:249
  50.7 36.7 %all_to_all.26.arrived = bf16[64,2,896]{2,1,0:T(2,128)(2,1)S(1)} all-to-all(bf16[64,2,896]{2,1,0:T(2,128)(2,1)S(1)} %shard_map.104), channel_id=1, replica_groups=mesh['x'=4,'z'=16,'y'=4,'core'=2] {'x','z'}, dimensions={0} | all-to-all | bytes 458752 | tf_op jit(solution)/shard_map/all_to_all | solution.py:17
  87.4 2.0 %shard_map.106 = bf16[4,128,256]{2,1,0:T(8,128)(2,1)} custom-call(s32[2]{0:T(128)S(1)} %pad_add_fusion.where, bf16[64,2,896]{2,1,0:T(2,128)(2,1)S(1)} %all_to_all.26.arrived, bf16[4,128,896]{2,1,0:T(8,128)(2,1)S(1)} %pad_maximum_fusion.own, bf16[4,128,896]{2,1,0:T(8,128)(2,1)S(1)} %collective-permute-done.3.other), custom_call_target="tpu_custom_call" | custom-call | tf_op jit(solution)/shard_map/pallas_call | solution.py:36
  89.4 3.4 %all-to-all-start.1 = ((bf16[4,128,256]{2,1,0:T(8,128)(2,1)}), bf16[4,128,256]{2,1,0:T(8,128)(2,1)S(1)}, u32[]{:S(2)}, u32[]{:S(2)}) async-start(bf16[4,128,256]{2,1,0:T(8,128)(2,1)} %shard_map.106), calls=%async_computation.1 | async-start | bytes 524288 | tf_op jit(solution)/shard_map/all_to_all | solution.py:17
  92.9 4.0 %collective-permute-start.4 = (bf16[2,256,128]{2,1,0:T(8,128)(2,1)S(1)}, bf16[2,256,128]{2,1,0:T(8,128)(2,1)S(1)}, u32[]{:S(2)}, u32[]{:S(2)}) collective-permute-start(bf16[2,256,128]{2,1,0:T(8,128)(2,1)S(1)} %bitcast.25), channel_id=1, source_target_pairs={{0,1},{1,0},{2,3},{3,2},{4,5},{5,4},{6,7},{7,6},{8,9},{9,8},{10,11... | collective-permute-start | bytes 393224 | tf_op jit(solution)/shard_map/ppermute | solution.py:250
  99.3 2.8 %shard_map.108 = bf16[4,136,896]{2,1,0:T(8,128)(2,1)S(1)} custom-call(s32[2]{0:T(128)S(1)} %pad_add_fusion.where, bf16[128,512]{1,0:T(8,128)(2,1)S(1)} %get-tuple-element.14.grads, bf16[128,128]{1,0:T(8,128)(2,1)S(1)} %get-tuple-element.15.gates, bf16[2,3584,128]{2,1,0:T(8,128)(2,1)S(1)} %bitcast.22, bf16[2,3584,128]{2,1,0:T(8,128)(2,1)} %collective-permute-done.5.other), custom_call_target="tpu_custom_call" | custom-call | tf_op jit(solution)/shard_map/pallas_call | solution.py:36
  102.1 16.2 %all_to_all.27.parts = bf16[4,136,896]{2,1,0:T(8,128)(2,1)S(1)} all-to-all(bf16[4,136,896]{2,1,0:T(8,128)(2,1)S(1)} %shard_map.108), channel_id=1, replica_groups=mesh['x'=4,'z'=16,'y'=4,'core'=2] {'y'}, dimensions={0} | all-to-all | bytes 1949696 | tf_op jit(solution)/shard_map/all_to_all | solution.py:17
  118.2 1.4 shard_map.109
  119.7 6.8 %all-to-all-start.3 = ((bf16[64,2,1024]{2,1,0:T(2,128)(2,1)}), bf16[64,2,1024]{2,1,0:T(2,128)(2,1)S(1)}, u32[]{:S(2)}, u32[]{:S(2)}) async-start(bf16[64,2,1024]{2,1,0:T(2,128)(2,1)} %shard_map.109), calls=%async_computation.3 | async-start | bytes 524288 | tf_op jit(solution)/shard_map/all_to_all | solution.py:17
  126.6 17.7 %all-to-all-done.3.returned = bf16[64,2,1024]{2,1,0:T(2,128)(2,1)S(1)} async-done(((bf16[64,2,1024]{2,1,0:T(2,128)(2,1)}), bf16[64,2,1024]{2,1,0:T(2,128)(2,1)S(1)}, u32[]{:S(2)}, u32[]{:S(2)}) %all-to-all-start.3) | async-done | bytes 262176 | tf_op jit(solution)/shard_map/all_to_all | solution.py:17
  144.3 1.0 shard_map.110
  145.3 6.0 %collective-permute-start.6 = (f32[16,512]{1,0:T(8,128)S(1)}, f32[16,512]{1,0:T(8,128)S(1)}, u32[]{:S(2)}, u32[]{:S(2)}) collective-permute-start(f32[16,512]{1,0:T(8,128)S(1)} %get-tuple-element.17), channel_id=1, source_target_pairs={{0,1},{1,0},{2,3},{3,2},{4,5},{5,4},{6,7},{7,6},{8,9},{9,8},{10,11... | collective-permute-start | bytes 98312 | tf_op jit(solution)/shard_map/ppermute | solution.py:315
  153.0 1.8 copy-done
  154.8 1.9 %shard_map.112 = bf16[16,16,224]{2,1,0:T(8,128)(2,1)S(1)} custom-call(s32[2]{0:T(128)S(1)} %pad_add_fusion.where, bf16[16,16,224]{2,1,0:T(8,128)(2,1)S(1)} %reshape.14.turned, bf16[16,3,224,128]{3,2,1,0:T(8,128)(2,1)S(1)} %copy-done, bf16[2,16,128]{2,1,0:T(8,128)(2,1)S(1)} %copy-done.8), custom_call_target="tpu_custom_call" | custom-call | tf_op jit(solution)/shard_map/pallas_call | solution.py:36
  157.4 13.8 %all_gather.7 = bf16[8,16,3584]{2,1,0:T(8,128)(2,1)S(1)} all-gather(bf16[1,16,3584]{2,1,0:T(8,128)(2,1)S(1)} %all_gather_reshape.7), channel_id=1, replica_groups=mesh['x'=4,'z'=16,'y'=4,'core'=2] {'y','core'}, dimensions={0}, use_global_device_ids=true | all-gather | bytes 1032192 | tf_op jit(solution)/shard_map/all_gather | solution.py:303
  (46 shorter events, 10.0 us)
Async XLA Ops:
  7.2 145.8 %all-gather.2.cloned.1.call-start = ((), (), s32[]{:S(2)}) async-start(), calls=%async_computation.5 | async-start | bytes 2924544 | tf_op jit(solution)/shard_map/all_gather | solution.py:227
  7.3 0.7 copy-start.5
  8.0 0.7 copy-start.7
  9.3 40.4 %copy-start.3 = (bf16[16,3584]{1,0:T(8,128)(2,1)S(1)}, bf16[16,3584]{1,0:T(8,128)(2,1)}, u32[]{:S(2)}) copy-start(bf16[16,3584]{1,0:T(8,128)(2,1)} %tokens.1) | copy-start | bytes 344068
  9.3 40.4 %copy-start.6 = (s32[16,8]{0,1:T(8,128)S(1)}, s32[16,8]{0,1:T(8,128)}, u32[]{:S(2)}) copy-start(s32[16,8]{0,1:T(8,128)} %param.10) | copy-start | bytes 1540
  19.9 79.4 %collective-permute-start.5 = (bf16[2,3584,128]{2,1,0:T(8,128)(2,1)}, bf16[2,3584,128]{2,1,0:T(8,128)(2,1)}, u32[]{:S(2)}, u32[]{:S(2)}) collective-permute-start(bf16[2,3584,128]{2,1,0:T(8,128)(2,1)} %bitcast.21), channel_id=1, source_target_pairs={{0,1},{1,0},{2,3},{3,2},{4,5},{5,4},{6,7},{7,6},{8,9},{9,8},{10,11... | collective-permute-start | bytes 5505032 | tf_op jit(solution)/shard_map/ppermute | solution.py:251
  27.5 1.2 copy-start.2
  29.3 9.0 %collective-permute-start.2 = (bf16[128,896]{1,0:T(8,128)(2,1)S(1)}, bf16[128,896]{1,0:T(8,128)(2,1)S(1)}, u32[]{:S(2)}, u32[]{:S(2)}) collective-permute-start(bf16[128,896]{1,0:T(8,128)(2,1)S(1)} %get-tuple-element.13), channel_id=1, source_target_pairs={{0,6},{2,0},{4,2},{6,4},{1,7},{3,1},{5,3},{7,5},{8,14},{10,8},{12,... | collective-permute-start | bytes 688136 | tf_op jit(solution)/shard_map/ppermute | solution.py:245
  31.2 10.6 %collective-permute-start.1 = (bf16[128,896]{1,0:T(8,128)(2,1)S(1)}, bf16[128,896]{1,0:T(8,128)(2,1)S(1)}, u32[]{:S(2)}, u32[]{:S(2)}) collective-permute-start(bf16[128,896]{1,0:T(8,128)(2,1)S(1)} %get-tuple-element.12), channel_id=1, source_target_pairs={{0,4},{2,6},{4,0},{6,2},{1,5},{3,7},{5,1},{7,3},{8,12},{10,14},{12... | collective-permute-start | bytes 688136 | tf_op jit(solution)/shard_map/ppermute | solution.py:245
  33.2 13.9 %collective-permute-start = (bf16[128,896]{1,0:T(8,128)(2,1)S(1)}, bf16[128,896]{1,0:T(8,128)(2,1)S(1)}, u32[]{:S(2)}, u32[]{:S(2)}) collective-permute-start(bf16[128,896]{1,0:T(8,128)(2,1)S(1)} %get-tuple-element.11), channel_id=1, source_target_pairs={{0,2},{2,4},{4,6},{6,0},{1,3},{3,5},{5,7},{7,1},{8,10},{10,12},{12... | collective-permute-start | bytes 688136 | tf_op jit(solution)/shard_map/ppermute | solution.py:245
  47.2 45.6 %copy-start.4 = (bf16[1,2,256,128]{3,2,1,0:T(8,128)(2,1)S(1)}, bf16[1,2,256,128]{3,2,1,0:T(8,128)(2,1)}, u32[]{:S(2)}) copy-start(bf16[1,2,256,128]{3,2,1,0:T(8,128)(2,1)} %param.14) | copy-start | bytes 393220
  47.3 40.2 %collective-permute-start.3 = (bf16[4,128,896]{2,1,0:T(8,128)(2,1)S(1)}, bf16[4,128,896]{2,1,0:T(8,128)(2,1)S(1)}, u32[]{:S(2)}, u32[]{:S(2)}) collective-permute-start(bf16[4,128,896]{2,1,0:T(8,128)(2,1)S(1)} %pad_maximum_fusion.own), channel_id=1, source_target_pairs={{0,1},{1,0},{2,3},{3,2},{4,5},{5,4},{6,7},{7,6},{8,9},{9,8},{10,11... | collective-permute-start | bytes 2752520 | tf_op jit(solution)/shard_map/ppermute | solution.py:249
  50.7 48.6 %copy-start.1 = (bf16[1,2,3584,128]{3,2,1,0:T(8,128)(2,1)S(1)}, bf16[1,2,3584,128]{3,2,1,0:T(8,128)(2,1)}, u32[]{:S(2)}) copy-start(bf16[1,2,3584,128]{3,2,1,0:T(8,128)(2,1)} %param.12) | copy-start | bytes 5505028
  89.4 8.9 %all-to-all-start.1 = ((bf16[4,128,256]{2,1,0:T(8,128)(2,1)}), bf16[4,128,256]{2,1,0:T(8,128)(2,1)S(1)}, u32[]{:S(2)}, u32[]{:S(2)}) async-start(bf16[4,128,256]{2,1,0:T(8,128)(2,1)} %shard_map.106), calls=%async_computation.1 | async-start | bytes 524288 | tf_op jit(solution)/shard_map/all_to_all | solution.py:17
  92.9 5.0 %collective-permute-start.4 = (bf16[2,256,128]{2,1,0:T(8,128)(2,1)S(1)}, bf16[2,256,128]{2,1,0:T(8,128)(2,1)S(1)}, u32[]{:S(2)}, u32[]{:S(2)}) collective-permute-start(bf16[2,256,128]{2,1,0:T(8,128)(2,1)S(1)} %bitcast.25), channel_id=1, source_target_pairs={{0,1},{1,0},{2,3},{3,2},{4,5},{5,4},{6,7},{7,6},{8,9},{9,8},{10,11... | collective-permute-start | bytes 393224 | tf_op jit(solution)/shard_map/ppermute | solution.py:250
  102.1 24.5 %copy-start.9 = (f32[16,8]{0,1:T(8,128)S(1)}, f32[16,8]{0,1:T(8,128)}, u32[]{:S(2)}) copy-start(f32[16,8]{0,1:T(8,128)} %param.11) | copy-start | bytes 1540
  118.2 34.7 %copy-start.8 = (bf16[2,16,128]{2,1,0:T(8,128)(2,1)S(1)}, bf16[2,16,128]{2,1,0:T(8,128)(2,1)}, u32[]{:S(2)}) copy-start(bf16[2,16,128]{2,1,0:T(8,128)(2,1)} %saved.1) | copy-start | bytes 24580
  119.7 24.6 %all-to-all-start.3 = ((bf16[64,2,1024]{2,1,0:T(2,128)(2,1)}), bf16[64,2,1024]{2,1,0:T(2,128)(2,1)S(1)}, u32[]{:S(2)}, u32[]{:S(2)}) async-start(bf16[64,2,1024]{2,1,0:T(2,128)(2,1)} %shard_map.109), calls=%async_computation.3 | async-start | bytes 524288 | tf_op jit(solution)/shard_map/all_to_all | solution.py:17
  145.3 6.9 %collective-permute-start.6 = (f32[16,512]{1,0:T(8,128)S(1)}, f32[16,512]{1,0:T(8,128)S(1)}, u32[]{:S(2)}, u32[]{:S(2)}) collective-permute-start(f32[16,512]{1,0:T(8,128)S(1)} %get-tuple-element.17), channel_id=1, source_target_pairs={{0,1},{1,0},{2,3},{3,2},{4,5},{5,4},{6,7},{7,6},{8,9},{9,8},{10,11... | collective-permute-start | bytes 98312 | tf_op jit(solution)/shard_map/ppermute | solution.py:315
  153.0 1.8 copy-start
Sparse Core Ops, SparseCore 0:
  20.0 77.3 all-gather.1

commit v5 on v3

--- a/solution.py
+++ b/solution.py
@@ -15,11 +15,6 @@
 
 def exchange(array, axis):
     return lax.all_to_all(array, axis, 0, 0, tiled=True)
-
-
-def from_everyone(array, axis):
-    peers = lax.axis_size(axis)
-    return exchange(jnp.broadcast_to(array[None], (peers, *array.shape)), axis)
 
 
 def contract_last(left, right):
@@ -47,6 +42,59 @@
     )(scalars, *arrays)
 
 
+def route_kernel(where, ids, tokens, out):
+    core, y = where[0], where[1]
+    experts, capacity, share = out.shape
+    count = tokens.shape[0]
+    shape = (experts * capacity, count)
+    slot = lax.broadcasted_iota(jnp.int32, shape, 0)
+    expert = slot // capacity
+    chosen = ids[0:1, :] == expert
+    for k in range(1, ids.shape[0]):
+        chosen = chosen | (ids[k : k + 1, :] == expert)
+    chosen = jnp.where(chosen, 1.0, 0.0)
+    first = lax.broadcasted_iota(jnp.int32, (count, count), 0)
+    second = lax.broadcasted_iota(jnp.int32, (count, count), 1)
+    earlier = jnp.where(first < second, 1.0, 0.0).astype(BF16)
+    before = jnp.dot(chosen.astype(BF16), earlier, preferred_element_type=F32)
+    place = (slot % capacity).astype(F32)
+    source = jnp.where(before == place, chosen, 0.0).astype(BF16)
+    both = tokens[:, pl.ds(pl.multiple_of(y * 2 * share, LANES), 2 * share)]
+    columns = jnp.where(core == 0, both[:, :share], both[:, share:])
+    rows = jnp.dot(source, columns, preferred_element_type=F32).astype(BF16)
+    out[...] = rows.reshape(out.shape)
+
+
+def shared_kernel(where, turned, pieces, saved, mine, theirs, terms):
+    core = where[0]
+    count, half = pieces.shape[0], mine.shape[0]
+    back_grad = jnp.zeros(saved.shape[1:], F32)
+    for z in range(count):
+        back_grad += jnp.dot(turned[z], pieces[z, 2], preferred_element_type=F32)
+    grads = jnp.concatenate(swiglu_grads(back_grad, saved[0], saved[1]), axis=1)
+    for z in range(count):
+        weights = jnp.concatenate([pieces[z, 0], pieces[z, 1]], axis=1)
+        terms[z] = contract_last(grads, weights).astype(BF16)
+    mine[...] = terms[pl.ds(half * core, half)]
+    theirs[...] = terms[pl.ds(half * (1 - core), half)]
+
+
+def fold_kernel(where, mine, taken, *outs):
+    y = where[1]
+    count = mine.shape[0]
+    ys = len(outs)
+    piece = mine.shape[2] // ys
+    for z in range(count):
+        total = (mine[z].astype(F32) + taken[z].astype(F32)).astype(BF16)
+        parts = [total[:, x * piece : (x + 1) * piece] for x in range(ys)]
+        for r, out in enumerate(outs):
+            home = (y + r) % ys
+            chosen = parts[ys - 1]
+            for x in range(ys - 1):
+                chosen = jnp.where(home == x, parts[x], chosen)
+            out[:, z * piece : (z + 1) * piece] = chosen
+
+
 def split_kernel(where, whole, *outs):
     y = where[1]
     _, features = whole.shape
@@ -61,8 +109,10 @@
 def back_kernel(where, own, other, *refs):
     *weights, out = refs
     core, y = where[0], where[1]
+    mine = own[...].reshape(out.shape[1], own.shape[2])
+    theirs = other[...].reshape(mine.shape)
     for r, weight in enumerate(weights):
-        part = contract_last(own[...], weight[core]) + contract_last(other[...], weight[1 - core])
+        part = contract_last(mine, weight[core]) + contract_last(theirs, weight[1 - core])
         out[(y + len(weights) - r) % len(weights)] = part.astype(BF16)
 
 
@@ -142,25 +192,22 @@
     wide = -(-share // LANES) * LANES
     core = lax.axis_index("core")
     y = lax.axis_index("y")
-    part = lax.axis_index(PARTS)
     swap = [(0, 1), (1, 0)]
     where = jnp.stack([core, y]).astype(jnp.int32)
 
     piece = jnp.concatenate([shared_gate_up, shared_down.T[None]], axis=0)
-    column = from_everyone(piece, "x")
+    column = exchange(jnp.broadcast_to(piece[None], (xs, *piece.shape)), "x")
+    column = column.transpose(1, 0, 2, 3).reshape(3, -1, hidden)
     pieces = lax.all_gather(column, "z", axis=0)
 
-    slot = jnp.arange(slots, dtype=jnp.int32)
-    hit = expert_ids.T[:, None, :] == (slot // capacity)[None, :, None]
-    chosen = jnp.any(hit, axis=0)
-    earlier = jnp.arange(tokens)[:, None] < jnp.arange(tokens)[None, :]
-    before = jnp.dot(chosen.astype(BF16), earlier.astype(BF16), preferred_element_type=F32)
-    source = chosen & (before.astype(jnp.int32) == (slot % capacity)[:, None])
-    columns = lax.dynamic_slice_in_dim(grad_out, part * share, share, 1)
-    send = jnp.dot(source.astype(BF16), columns, preferred_element_type=F32).astype(BF16)
-    send = send.reshape(experts, capacity, share)
+    send = kernel_call(
+        route_kernel,
+        jax.ShapeDtypeStruct((experts, capacity, share), BF16),
+        where,
+        expert_ids.T,
+        grad_out,
+    )
     own_rows = exchange(send, OWNER)
-    own_rows = own_rows.reshape(slots, share)
 
     downs = kernel_call(
         split_kernel,
@@ -213,23 +260,38 @@
     )
     returned = exchange(finished, OWNER)
 
-    turned = grad_out.reshape(tokens, xs, zs, -1).transpose(0, 2, 1, 3).reshape(tokens, -1)
-    down_all = pieces[:, :, 2].reshape(features, hidden)
-    gate_all = pieces[:, :, 0].reshape(features, hidden)
-    up_all = pieces[:, :, 1].reshape(features, hidden)
-    shared_back = jnp.dot(turned, down_all, preferred_element_type=F32)
-    shared_gate, shared_up = swiglu_grads(shared_back, saved_shared[0], saved_shared[1])
-    shared_term = contract_last(shared_gate, gate_all) + contract_last(shared_up, up_all)
-    shared_term = (
-        shared_term.astype(BF16)
-        .reshape(tokens, zs, xs, -1)
-        .transpose(0, 2, 1, 3)
-        .reshape(tokens, features)
-    )
-    everyone = lax.all_gather(shared_term, PARTS, axis=0)
-    ours = lax.dynamic_slice_in_dim(everyone, part * share, share, 2)
-    shared_sum = jnp.sum(ours.astype(F32), axis=0)
-
+    turned = grad_out.reshape(tokens, xs, zs, -1).transpose(2, 0, 1, 3)
+    turned = turned.reshape(zs, tokens, -1)
+    half = jax.ShapeDtypeStruct((zs // 2, tokens, features // zs), BF16)
+    shared_mine, shared_theirs = pl.pallas_call(
+        shared_kernel,
+        out_shape=[half, half],
+        in_specs=[pl.BlockSpec(memory_space=pltpu.SMEM)]
+        + [pl.BlockSpec(memory_space=pltpu.VMEM)] * 3,
+        out_specs=[pl.BlockSpec(memory_space=pltpu.VMEM)] * 2,
+        scratch_shapes=[pltpu.VMEM((zs, *half.shape[1:]), BF16)],
+        compiler_params=pltpu.CompilerParams(vmem_limit_bytes=10 * 2**20),
+    )(where, turned, pieces, saved_shared)
+    shared_taken = lax.ppermute(shared_theirs, "core", swap)
+    folded = kernel_call(
+        fold_kernel,
+        [jax.ShapeDtypeStruct((tokens, share), BF16)] * ys,
+        where,
+        shared_mine,
+        shared_taken,
+    )
+    folded = [folded[0]] + [
+        lax.ppermute(folded[r], "y", [(i, (i + r) % ys) for i in range(ys)])
+        for r in range(1, ys)
+    ]
+    shared_sum = sum(block.astype(F32) for block in folded)
+
+    slot = jnp.arange(slots, dtype=jnp.int32)
+    hit = expert_ids.T[:, None, :] == (slot // capacity)[None, :, None]
+    chosen = jnp.any(hit, axis=0)
+    earlier = jnp.arange(tokens)[:, None] < jnp.arange(tokens)[None, :]
+    before = jnp.dot(chosen.astype(BF16), earlier.astype(BF16), preferred_element_type=F32)
+    source = chosen & (before.astype(jnp.int32) == (slot % capacity)[:, None])
     pick = (hit & source[None]).transpose(0, 2, 1).reshape(choose * tokens, slots)
     picked = jnp.dot(
         pick.astype(BF16), returned.reshape(slots, wide), preferred_element_type=F32

time: 168 us -> 167 us (level)
  blocking collectives: 53.7 us -> 37 us
  starting transfers between devices: 55.2 us -> 69.1 us
  Pallas kernels: 7.32 us -> 11.7 us
  waiting for transfers between devices: 21.6 us -> 23.8 us
  local copies, waits for them, and re-layouts: 9.24 us -> 7.1 us
  matrix products: 2.44 us -> 0.42 us
    all_gather x1 -> x0, blocking collectives: 16.6 us -> none  [per_device(): everyone = lax.all_gather(shared_term, PARTS, axis=0)]
    ppermute x0 -> x4, starting transfers between devices: none -> 13.5 us  [the longest x3 8.42 us: per_device(): lax.ppermute(folded[r], 'y', [(i, (i + r) % ys) for i in range(ys)])]
    reshape x7 -> x3, local copies, waits for them, and re-layouts: 3.33 us -> 0.79 us  [the longest x2 0.61 us: per_device(): turned = grad_out.reshape(tokens, xs, zs, -1).transpose(2, 0, 1, 3)]
    pallas_call x5 -> x7, Pallas kernels: 7.32 us -> 9.78 us  [kernel_call(): pl.pallas_call(body, out_shape=out_shape, in_specs=[smem] + [vmem] * len(...]
    unnamed x14 -> x20, local copies, waits for them, and re-layouts: 2.11 us -> 4.56 us
    slice x1 -> x0, local copies, waits for them, and re-layouts: 2.23 us -> none  [per_device(): up_all = pieces[:, :, 1].reshape(features, hidden)]
    dot_general x4 -> x0, matrix products: 2.02 us -> none  [the longest x1 1.08 us: per_device(): jnp.dot(source.astype(BF16), columns, preferred_element_type=F32)]
    ppermute x0 -> x4, waiting for transfers between devices: none -> 1.96 us  [the longest x3 1.18 us: per_device(): lax.ppermute(folded[r], 'y', [(i, (i + r) % ys) for i in range(ys)])]
  transfers between devices with their start and end apart: 9 -> 13, of which waited for: 4 -> 6; matrix products, arithmetic and copies ran while one was open for 4% -> 2% of each run, Pallas kernels for 4% -> 5%
where the time goes in v5:
time: 167 us; the launch traced here: 166 us
  starting transfers between devices  69.1 us (41%)
  blocking collectives  37 us (22%)
  waiting for transfers between devices  23.8 us (14%)
  between operations  14.4 us (9%)
  Pallas kernels  11.7 us (7%)
  local copies, waits for them, and re-layouts  7.1 us (4%)
  other arithmetic  2.53 us (2%)
    all_to_all x3, blocking collectives, exchange(): return lax.all_to_all(array, axis, 0, 0, tiled=True)  37 us
    all_to_all x2, starting transfers between devices, exchange(): return lax.all_to_all(array, axis, 0, 0, tiled=True)  30.5 us
    all_to_all x2, waiting for transfers between devices, exchange(): return lax.all_to_all(array, axis, 0, 0, tiled=True)  19.7 us
    ppermute x3, starting transfers between devices, per_device(): lax.ppermute(downs[r], 'y', [(i, (i + r) % ys) for i in range(ys)])  10.7 us
    pallas_call x7, Pallas kernels, kernel_call(): pl.pallas_call(body, out_shape=out_shape, in_specs=[smem] + [vmem] * len(...  9.78 us
    ppermute x3, starting transfers between devices, per_device(): lax.ppermute(folded[r], 'y', [(i, (i + r) % ys) for i in range(ys)])  8.42 us
    ppermute x1, starting transfers between devices, per_device(): other_rows = lax.ppermute(own_rows, 'core', swap)  6.52 us
    ppermute x1, starting transfers between devices, per_device(): shared_taken = lax.ppermute(shared_theirs, 'core', swap)  5.06 us
  transfers between devices with their start and end apart: 13, of which 6 were waited for; matrix products, arithmetic and copies ran while one was open for 2% of the time, Pallas kernels for 5%

profile of v5, /device:TPU:1, one launch (start us, length us, event | category | flops | bytes accessed | tf_op | source)
XLA Modules:
  0.0 166.0 jit_solution(10597271650411290787)
XLA Ops:
  8.1 9.7 %all_to_all.25 = bf16[4,3,56,128]{3,2,1,0:T(8,128)(2,1)S(1)} all-to-all(bf16[4,3,56,128]{3,2,1,0:T(8,128)(2,1)S(1)} %broadcast_in_dim.5), channel_id=1, replica_groups=mesh['x'=4,'z'=16,'y'=4,'core'=2] {'x'}, dimensions={0} | all-to-all | bytes 344064 | tf_op jit(solution)/shard_map/all_to_all | solution.py:17
  20.2 1.6 shard_map.104
  21.8 16.6 %all-to-all-start = ((bf16[64,4,448]{2,1,0:T(4,128)(2,1)}), bf16[64,4,448]{2,1,0:T(4,128)(2,1)S(1)}, u32[]{:S(2)}, u32[]{:S(2)}) async-start(bf16[64,4,448]{2,1,0:T(4,128)(2,1)} %shard_map.104), calls=%async_computation | async-start | bytes 524288 | tf_op jit(solution)/shard_map/all_to_all | solution.py:17
  39.4 4.1 %collective-permute-start.5 = (bf16[2,4,448,128]{3,2,1,0:T(8,128)(2,1)}, bf16[2,4,448,128]{3,2,1,0:T(8,128)(2,1)S(1)}, u32[]{:S(2)}, u32[]{:S(2)}) collective-permute-start(bf16[2,4,448,128]{3,2,1,0:T(8,128)(2,1)} %dynamic-slice_bitcast_fusion), channel_id=1, source_target_pairs={{0,1},{1,0},{2,3},{3,2},{4,5},{5,4},{6,7},{7,6},{8,9},{9,8},{10,11... | collective-permute-start | bytes 2752520 | tf_op jit(solution)/shard_map/ppermute | solution.py:241
  44.7 1.6 shard_map.105
  46.3 3.2 %collective-permute-start.1 = (bf16[2,128,448]{2,1,0:T(8,128)(2,1)}, bf16[2,128,448]{2,1,0:T(8,128)(2,1)S(1)}, u32[]{:S(2)}, u32[]{:S(2)}) collective-permute-start(bf16[2,128,448]{2,1,0:T(8,128)(2,1)} %get-tuple-element.13), channel_id=1, source_target_pairs={{0,2},{2,4},{4,6},{6,0},{1,3},{3,5},{5,7},{7,1},{8,10},{10,12},{12... | collective-permute-start | bytes 688136 | tf_op jit(solution)/shard_map/ppermute | solution.py:219
  49.5 4.5 %collective-permute-start.2 = (bf16[2,128,448]{2,1,0:T(8,128)(2,1)}, bf16[2,128,448]{2,1,0:T(8,128)(2,1)}, u32[]{:S(2)}, u32[]{:S(2)}) collective-permute-start(bf16[2,128,448]{2,1,0:T(8,128)(2,1)} %get-tuple-element.14), channel_id=1, source_target_pairs={{0,4},{2,6},{4,0},{6,2},{1,5},{3,7},{5,1},{7,3},{8,12},{10,14},{12... | collective-permute-start | bytes 688136 | tf_op jit(solution)/shard_map/ppermute | solution.py:219
  54.1 3.0 %collective-permute-start.3 = (bf16[2,128,448]{2,1,0:T(8,128)(2,1)}, bf16[2,128,448]{2,1,0:T(8,128)(2,1)}, u32[]{:S(2)}, u32[]{:S(2)}) collective-permute-start(bf16[2,128,448]{2,1,0:T(8,128)(2,1)} %get-tuple-element.15), channel_id=1, source_target_pairs={{0,6},{2,0},{4,2},{6,4},{1,7},{3,1},{5,3},{7,5},{8,14},{10,8},{12,... | collective-permute-start | bytes 688136 | tf_op jit(solution)/shard_map/ppermute | solution.py:219
  57.1 2.0 %all-to-all-done.own = bf16[64,4,448]{2,1,0:T(4,128)(2,1)S(1)} async-done(((bf16[64,4,448]{2,1,0:T(4,128)(2,1)}), bf16[64,4,448]{2,1,0:T(4,128)(2,1)S(1)}, u32[]{:S(2)}, u32[]{:S(2)}) %all-to-all-start) | async-done | bytes 229408 | tf_op jit(solution)/shard_map/all_to_all | solution.py:17
  59.1 6.5 %collective-permute-start = (bf16[64,4,448]{2,1,0:T(4,128)(2,1)S(1)}, bf16[64,4,448]{2,1,0:T(4,128)(2,1)S(1)}, u32[]{:S(2)}, u32[]{:S(2)}) collective-permute-start(bf16[64,4,448]{2,1,0:T(4,128)(2,1)S(1)} %all-to-all-done.own), channel_id=1, source_target_pairs={{0,1},{1,0},{2,3},{3,2},{4,5},{5,4},{6,7},{7,6},{8,9},{9,8},{10,11... | collective-permute-start | bytes 688136 | tf_op jit(solution)/shard_map/ppermute | solution.py:222
  66.8 1.8 %shard_map.106 = bf16[4,256,128]{2,1,0:T(8,128)(2,1)S(1)} custom-call(s32[2]{0:T(128)S(1)} %pad_add_fusion.where, bf16[64,4,448]{2,1,0:T(4,128)(2,1)S(1)} %all-to-all-done.own, bf16[64,4,448]{2,1,0:T(4,128)(2,1)S(1)} %collective-permute-done.other, bf16[2,128,448]{2,1,0:T(8,128)(2,1)S(1)} %get-tuple-element.12.refs_0_, ...), custom_call_target="tpu_custom_call" | custom-call | tf_op jit(solution)/shard_map/pallas_call | solution.py:36
  68.5 9.9 %all_to_all.26.parts = bf16[4,256,128]{2,1,0:T(8,128)(2,1)S(1)} all-to-all(bf16[4,256,128]{2,1,0:T(8,128)(2,1)S(1)} %shard_map.106), channel_id=1, replica_groups=mesh['x'=4,'z'=16,'y'=4,'core'=2] {'y'}, dimensions={0} | all-to-all | bytes 524288 | tf_op jit(solution)/shard_map/all_to_all | solution.py:17
  79.2 3.7 %collective-permute-start.4 = (bf16[256,384]{1,0:T(8,128)(2,1)S(1)}, bf16[256,384]{1,0:T(8,128)(2,1)S(1)}, u32[]{:S(2)}, u32[]{:S(2)}) collective-permute-start(bf16[256,384]{1,0:T(8,128)(2,1)S(1)} %shard_map.107.mine), channel_id=1, source_target_pairs={{0,1},{1,0},{2,3},{3,2},{4,5},{5,4},{6,7},{7,6},{8,9},{9,8},{10,11... | collective-permute-start | bytes 589832 | tf_op jit(solution)/shard_map/ppermute | solution.py:244
  83.9 1.8 %shard_map.108 = bf16[4,256,512]{2,1,0:T(8,128)(2,1)S(1)} custom-call(s32[2]{0:T(128)S(1)} %pad_add_fusion.where, bf16[256,384]{1,0:T(8,128)(2,1)S(1)} %shard_map.107.mine, bf16[256,384]{1,0:T(8,128)(2,1)S(1)} %collective-permute-done.4.theirs, bf16[2,3584,128]{2,1,0:T(8,128)(2,1)S(1)} %bitcast.27, bf16[2,4,448,128]{3,2,1,0:T(8,128)(2,1)S(1)} %collective-permute-done.5.other), custom_call_target="tpu_custom_call" | custom-call | tf_op jit(solution)/shard_map/pallas_call | solution.py:36
  85.7 17.4 %all_to_all.27.parts = bf16[4,256,512]{2,1,0:T(8,128)(2,1)S(1)} all-to-all(bf16[4,256,512]{2,1,0:T(8,128)(2,1)S(1)} %shard_map.108), channel_id=1, replica_groups=mesh['x'=4,'z'=16,'y'=4,'core'=2] {'y'}, dimensions={0} | all-to-all | bytes 2097152 | tf_op jit(solution)/shard_map/all_to_all | solution.py:17
  103.1 1.4 shard_map.109
  104.5 13.9 %all-to-all-start.3 = ((bf16[64,4,512]{2,1,0:T(4,128)(2,1)}), bf16[64,4,512]{2,1,0:T(4,128)(2,1)S(1)}, u32[]{:S(2)}, u32[]{:S(2)}) async-start(bf16[64,4,512]{2,1,0:T(4,128)(2,1)} %shard_map.109), calls=%async_computation.3 | async-start | bytes 524288 | tf_op jit(solution)/shard_map/all_to_all | solution.py:17
  119.6 17.7 %all-to-all-done.3 = bf16[64,4,512]{2,1,0:T(4,128)(2,1)S(1)} async-done(((bf16[64,4,512]{2,1,0:T(4,128)(2,1)}), bf16[64,4,512]{2,1,0:T(4,128)(2,1)S(1)}, u32[]{:S(2)}, u32[]{:S(2)}) %all-to-all-start.3) | async-done | bytes 262176 | tf_op jit(solution)/shard_map/all_to_all | solution.py:17
  137.7 1.8 %copy-done.1 = bf16[16,3,224,128]{3,2,1,0:T(8,128)(2,1)S(1)} copy-done((bf16[16,3,224,128]{3,2,1,0:T(8,128)(2,1)S(1)}, bf16[16,3,224,128]{3,2,1,0:T(8,128)(2,1)}, u32[]{:S(2)}) %copy-start.1) | copy-done | bytes 2752536
  139.4 1.9 %shard_map.110 = (bf16[8,16,224]{2,1,0:T(8,128)(2,1)S(1)}, bf16[8,16,224]{2,1,0:T(8,128)(2,1)S(1)}) custom-call(s32[2]{0:T(128)S(1)} %pad_add_fusion.where, bf16[16,16,224]{2,1,0:T(8,128)(2,1)S(1)} %reshape.62.turned, bf16[16,3,224,128]{3,2,1,0:T(8,128)(2,1)S(1)} %copy-done.1, bf16[2,16,128]{2,1,0:T(8,128)(2,1)S(1)} %copy-done.8), custom_call_target="tpu_custom_call" | custom-call | tf_op jit(solution)/shard_map/pallas_call | solution.py:266
  141.3 5.1 %collective-permute-start.6 = (bf16[8,16,224]{2,1,0:T(8,128)(2,1)S(1)}, bf16[8,16,224]{2,1,0:T(8,128)(2,1)S(1)}, u32[]{:S(2)}, u32[]{:S(2)}) collective-permute-start(bf16[8,16,224]{2,1,0:T(8,128)(2,1)S(1)} %get-tuple-element.17), channel_id=1, source_target_pairs={{0,1},{1,0},{2,3},{3,2},{4,5},{5,4},{6,7},{7,6},{8,9},{9,8},{10,11... | collective-permute-start | bytes 172040 | tf_op jit(solution)/shard_map/ppermute | solution.py:275
  148.2 2.2 %collective-permute-start.7 = (bf16[16,448]{1,0:T(8,128)(2,1)S(1)}, bf16[16,448]{1,0:T(8,128)(2,1)S(1)}, u32[]{:S(2)}, u32[]{:S(2)}) collective-permute-start(bf16[16,448]{1,0:T(8,128)(2,1)S(1)} %get-tuple-element.19), channel_id=1, source_target_pairs={{0,2},{2,4},{4,6},{6,0},{1,3},{3,5},{5,7},{7,1},{8,10},{10,12},{12... | collective-permute-start | bytes 43016 | tf_op jit(solution)/shard_map/ppermute | solution.py:284
  150.4 3.7 %collective-permute-start.8 = (bf16[16,448]{1,0:T(8,128)(2,1)S(1)}, bf16[16,448]{1,0:T(8,128)(2,1)S(1)}, u32[]{:S(2)}, u32[]{:S(2)}) collective-permute-start(bf16[16,448]{1,0:T(8,128)(2,1)S(1)} %get-tuple-element.20), channel_id=1, source_target_pairs={{0,4},{2,6},{4,0},{6,2},{1,5},{3,7},{5,1},{7,3},{8,12},{10,14},{12... | collective-permute-start | bytes 43016 | tf_op jit(solution)/shard_map/ppermute | solution.py:284
  154.1 2.5 %collective-permute-start.9 = (bf16[16,448]{1,0:T(8,128)(2,1)S(1)}, bf16[16,448]{1,0:T(8,128)(2,1)S(1)}, u32[]{:S(2)}, u32[]{:S(2)}) collective-permute-start(bf16[16,448]{1,0:T(8,128)(2,1)S(1)} %get-tuple-element.21), channel_id=1, source_target_pairs={{0,6},{2,0},{4,2},{6,4},{1,7},{3,1},{5,3},{7,5},{8,14},{10,8},{12,... | collective-permute-start | bytes 43016 | tf_op jit(solution)/shard_map/ppermute | solution.py:284
  (51 shorter events, 14.1 us)
Async XLA Ops:
  7.2 31.3 %copy-start = (bf16[1,2,3584,128]{3,2,1,0:T(8,128)(2,1)S(1)}, bf16[1,2,3584,128]{3,2,1,0:T(8,128)(2,1)}, u32[]{:S(2)}) copy-start(bf16[1,2,3584,128]{3,2,1,0:T(8,128)(2,1)} %param.12) | copy-start | bytes 5505028
  7.2 130.5 %all-gather.2.cloned.1.call-start = ((), (), s32[]{:S(2)}) async-start(), calls=%async_computation.5 | async-start | bytes 2924544 | tf_op jit(solution)/shard_map/all_gather | solution.py:201
  18.6 0.9 copy-start.3
  19.5 0.7 copy-start.6
  21.8 37.3 %all-to-all-start = ((bf16[64,4,448]{2,1,0:T(4,128)(2,1)}), bf16[64,4,448]{2,1,0:T(4,128)(2,1)S(1)}, u32[]{:S(2)}, u32[]{:S(2)}) async-start(bf16[64,4,448]{2,1,0:T(4,128)(2,1)} %shard_map.104), calls=%async_computation | async-start | bytes 524288 | tf_op jit(solution)/shard_map/all_to_all | solution.py:17
  39.4 43.5 %collective-permute-start.5 = (bf16[2,4,448,128]{3,2,1,0:T(8,128)(2,1)}, bf16[2,4,448,128]{3,2,1,0:T(8,128)(2,1)S(1)}, u32[]{:S(2)}, u32[]{:S(2)}) collective-permute-start(bf16[2,4,448,128]{3,2,1,0:T(8,128)(2,1)} %dynamic-slice_bitcast_fusion), channel_id=1, source_target_pairs={{0,1},{1,0},{2,3},{3,2},{4,5},{5,4},{6,7},{7,6},{8,9},{9,8},{10,11... | collective-permute-start | bytes 2752520 | tf_op jit(solution)/shard_map/ppermute | solution.py:241
  43.5 1.2 copy-start.2
  46.3 19.3 %collective-permute-start.1 = (bf16[2,128,448]{2,1,0:T(8,128)(2,1)}, bf16[2,128,448]{2,1,0:T(8,128)(2,1)S(1)}, u32[]{:S(2)}, u32[]{:S(2)}) collective-permute-start(bf16[2,128,448]{2,1,0:T(8,128)(2,1)} %get-tuple-element.13), channel_id=1, source_target_pairs={{0,2},{2,4},{4,6},{6,0},{1,3},{3,5},{5,7},{7,1},{8,10},{10,12},{12... | collective-permute-start | bytes 688136 | tf_op jit(solution)/shard_map/ppermute | solution.py:219
  49.5 16.1 %collective-permute-start.2 = (bf16[2,128,448]{2,1,0:T(8,128)(2,1)}, bf16[2,128,448]{2,1,0:T(8,128)(2,1)}, u32[]{:S(2)}, u32[]{:S(2)}) collective-permute-start(bf16[2,128,448]{2,1,0:T(8,128)(2,1)} %get-tuple-element.14), channel_id=1, source_target_pairs={{0,4},{2,6},{4,0},{6,2},{1,5},{3,7},{5,1},{7,3},{8,12},{10,14},{12... | collective-permute-start | bytes 688136 | tf_op jit(solution)/shard_map/ppermute | solution.py:219
  54.1 11.5 %collective-permute-start.3 = (bf16[2,128,448]{2,1,0:T(8,128)(2,1)}, bf16[2,128,448]{2,1,0:T(8,128)(2,1)}, u32[]{:S(2)}, u32[]{:S(2)}) collective-permute-start(bf16[2,128,448]{2,1,0:T(8,128)(2,1)} %get-tuple-element.15), channel_id=1, source_target_pairs={{0,6},{2,0},{4,2},{6,4},{1,7},{3,1},{5,3},{7,5},{8,14},{10,8},{12,... | collective-permute-start | bytes 688136 | tf_op jit(solution)/shard_map/ppermute | solution.py:219
  59.1 19.4 %copy-start.5 = (bf16[1,2,256,128]{3,2,1,0:T(8,128)(2,1)S(1)}, bf16[1,2,256,128]{3,2,1,0:T(8,128)(2,1)}, u32[]{:S(2)}) copy-start(bf16[1,2,256,128]{3,2,1,0:T(8,128)(2,1)} %param.14) | copy-start | bytes 393220
  59.1 7.7 %collective-permute-start = (bf16[64,4,448]{2,1,0:T(4,128)(2,1)S(1)}, bf16[64,4,448]{2,1,0:T(4,128)(2,1)S(1)}, u32[]{:S(2)}, u32[]{:S(2)}) collective-permute-start(bf16[64,4,448]{2,1,0:T(4,128)(2,1)S(1)} %all-to-all-done.own), channel_id=1, source_target_pairs={{0,1},{1,0},{2,3},{3,2},{4,5},{5,4},{6,7},{7,6},{8,9},{9,8},{10,11... | collective-permute-start | bytes 688136 | tf_op jit(solution)/shard_map/ppermute | solution.py:222
  79.2 4.8 %collective-permute-start.4 = (bf16[256,384]{1,0:T(8,128)(2,1)S(1)}, bf16[256,384]{1,0:T(8,128)(2,1)S(1)}, u32[]{:S(2)}, u32[]{:S(2)}) collective-permute-start(bf16[256,384]{1,0:T(8,128)(2,1)S(1)} %shard_map.107.mine), channel_id=1, source_target_pairs={{0,1},{1,0},{2,3},{3,2},{4,5},{5,4},{6,7},{7,6},{8,9},{9,8},{10,11... | collective-permute-start | bytes 589832 | tf_op jit(solution)/shard_map/ppermute | solution.py:244
  85.7 32.8 %copy-start.4 = (bf16[16,3584]{1,0:T(8,128)(2,1)S(1)}, bf16[16,3584]{1,0:T(8,128)(2,1)}, u32[]{:S(2)}) copy-start(bf16[16,3584]{1,0:T(8,128)(2,1)} %tokens.1) | copy-start | bytes 344068
  103.1 16.2 %copy-start.7 = (s32[16,8]{0,1:T(8,128)S(1)}, s32[16,8]{0,1:T(8,128)}, u32[]{:S(2)}) copy-start(s32[16,8]{0,1:T(8,128)} %param.10) | copy-start | bytes 1540
  103.1 34.5 %copy-start.8 = (bf16[2,16,128]{2,1,0:T(8,128)(2,1)S(1)}, bf16[2,16,128]{2,1,0:T(8,128)(2,1)}, u32[]{:S(2)}) copy-start(bf16[2,16,128]{2,1,0:T(8,128)(2,1)} %saved.1) | copy-start | bytes 24580
  104.5 32.8 %all-to-all-start.3 = ((bf16[64,4,512]{2,1,0:T(4,128)(2,1)}), bf16[64,4,512]{2,1,0:T(4,128)(2,1)S(1)}, u32[]{:S(2)}, u32[]{:S(2)}) async-start(bf16[64,4,512]{2,1,0:T(4,128)(2,1)} %shard_map.109), calls=%async_computation.3 | async-start | bytes 524288 | tf_op jit(solution)/shard_map/all_to_all | solution.py:17
  137.4 9.0 %copy-start.9 = (f32[16,8]{0,1:T(8,128)S(1)}, f32[16,8]{0,1:T(8,128)}, u32[]{:S(2)}) copy-start(f32[16,8]{0,1:T(8,128)} %param.11) | copy-start | bytes 1540
  137.6 1.8 %copy-start.1 = (bf16[16,3,224,128]{3,2,1,0:T(8,128)(2,1)S(1)}, bf16[16,3,224,128]{3,2,1,0:T(8,128)(2,1)}, u32[]{:S(2)}) copy-start(bf16[16,3,224,128]{3,2,1,0:T(8,128)(2,1)} %all-gather.2.cloned.1.call-done.pieces) | copy-start | bytes 8257540
  141.3 5.9 %collective-permute-start.6 = (bf16[8,16,224]{2,1,0:T(8,128)(2,1)S(1)}, bf16[8,16,224]{2,1,0:T(8,128)(2,1)S(1)}, u32[]{:S(2)}, u32[]{:S(2)}) collective-permute-start(bf16[8,16,224]{2,1,0:T(8,128)(2,1)S(1)} %get-tuple-element.17), channel_id=1, source_target_pairs={{0,1},{1,0},{2,3},{3,2},{4,5},{5,4},{6,7},{7,6},{8,9},{9,8},{10,11... | collective-permute-start | bytes 172040 | tf_op jit(solution)/shard_map/ppermute | solution.py:275
  148.2 9.2 %collective-permute-start.7 = (bf16[16,448]{1,0:T(8,128)(2,1)S(1)}, bf16[16,448]{1,0:T(8,128)(2,1)S(1)}, u32[]{:S(2)}, u32[]{:S(2)}) collective-permute-start(bf16[16,448]{1,0:T(8,128)(2,1)S(1)} %get-tuple-element.19), channel_id=1, source_target_pairs={{0,2},{2,4},{4,6},{6,0},{1,3},{3,5},{5,7},{7,1},{8,10},{10,12},{12... | collective-permute-start | bytes 43016 | tf_op jit(solution)/shard_map/ppermute | solution.py:284
  150.4 7.0 %collective-permute-start.8 = (bf16[16,448]{1,0:T(8,128)(2,1)S(1)}, bf16[16,448]{1,0:T(8,128)(2,1)S(1)}, u32[]{:S(2)}, u32[]{:S(2)}) collective-permute-start(bf16[16,448]{1,0:T(8,128)(2,1)S(1)} %get-tuple-element.20), channel_id=1, source_target_pairs={{0,4},{2,6},{4,0},{6,2},{1,5},{3,7},{5,1},{7,3},{8,12},{10,14},{12... | collective-permute-start | bytes 43016 | tf_op jit(solution)/shard_map/ppermute | solution.py:284
  154.1 4.5 %collective-permute-start.9 = (bf16[16,448]{1,0:T(8,128)(2,1)S(1)}, bf16[16,448]{1,0:T(8,128)(2,1)S(1)}, u32[]{:S(2)}, u32[]{:S(2)}) collective-permute-start(bf16[16,448]{1,0:T(8,128)(2,1)S(1)} %get-tuple-element.21), channel_id=1, source_target_pairs={{0,6},{2,0},{4,2},{6,4},{1,7},{3,1},{5,3},{7,5},{8,14},{10,8},{12,... | collective-permute-start | bytes 43016 | tf_op jit(solution)/shard_map/ppermute | solution.py:284
Sparse Core Ops, SparseCore 0:
  18.6 77.9 all-gather.1

commit v6 on v5

--- a/solution.py
+++ b/solution.py
@@ -134,37 +134,52 @@
 def row_kernel(where, mine, theirs, own, other, out):
     core = where[0]
     ys, share = other.shape[1], other.shape[2]
-    spare = out.shape[2] - share
-    hidden = own.shape[2]
-    row = lax.broadcasted_iota(jnp.int32, (share + spare, LANES), 0)
-    lane = lax.broadcasted_iota(jnp.int32, (share + spare, LANES), 1)
-    blank = jnp.zeros((spare, 2 * hidden), BF16)
-
-    def wide(gate, up, column):
-        weights = jnp.concatenate([jnp.concatenate([gate, up], axis=1), blank], axis=0)
-        passing = jnp.where((row == column) & (lane == 0), 1.0, 0.0).astype(BF16)
-        return jnp.concatenate([weights, passing], axis=1)
-
+    slots = mine.shape[0]
+    half = slots // 2
+    width = 2 * own.shape[2]
+    cut = share // LANES * LANES
+    blank = jnp.zeros((LANES - share % LANES, width), BF16)
+
+    def turned(grads):
+        column = grads[:, width : width + 1].astype(F32)
+        return jnp.broadcast_to(column, (slots, LANES)).T[0:8, :]
+
+    row = lax.broadcasted_iota(jnp.int32, (8, slots), 0)
+    gates = jnp.where(row == 0, turned(mine), jnp.where(row == 1, turned(theirs), 0.0))
     for y in range(ys):
         at = pl.ds(pl.multiple_of((2 * y + core) * share, 16), share)
-        total = contract_last(mine[...], wide(own[0, at, :], own[1, at, :], share))
-        total += contract_last(theirs[...], wide(other[0, y], other[1, y], share + 1))
-        out[y] = total.astype(BF16)
+        ours = jnp.concatenate([own[0, at, :], own[1, at, :]], axis=1)
+        others = jnp.concatenate([other[0, y], other[1, y]], axis=1)
+
+        def block(rows, before, after):
+            left = contract_last(mine[rows, :width], jnp.concatenate(before + [ours] + after, 0))
+            right = jnp.concatenate(before + [others] + after, 0)
+            return left + contract_last(theirs[rows, :width], right)
+
+        first = block(slice(0, half), [], [blank])
+        second = block(slice(half, slots), [blank], [])
+        out[y, :half, :cut] = first[:, :cut].astype(BF16)
+        out[y, :half, cut : cut + LANES] = (first[:, cut:] + second[:, :LANES]).astype(BF16)
+        out[y, :half, cut + LANES :] = second[:, LANES:].astype(BF16)
+        out[y, half:, :slots] = gates.astype(BF16)
+        out[y, half:, slots:] = jnp.zeros((8, out.shape[2] - slots), BF16)
 
 
 def pack_kernel(where, parts, out):
     total = jnp.sum(parts[...].astype(F32), axis=0)
-    slots, width = total.shape
-    share = SHARE
-    lane = lax.broadcasted_iota(jnp.int32, (slots, width), 1)
-    gates = jnp.sum(jnp.where(lane >= share, total, 0.0), axis=1, keepdims=True)
+    wide = out.shape[2]
+    half = out.shape[0] * out.shape[1] // 2
+    share = total.shape[1] // 2
+    terms = total[half : half + 1, : 2 * half] + total[half + 1 : half + 2, : 2 * half]
+    gates = jnp.broadcast_to(terms, (LANES, 2 * half)).T[:, 0:1]
     high = gates.astype(BF16).astype(F32)
-    low = gates - high
-    packed = jnp.where(lane == share, high, jnp.where(lane == share + 1, low, total))
+    first = total[:half, :wide]
+    second = pltpu.roll(total[:half, 2 * share - wide :], share, 1)
+    rows = jnp.concatenate([first, second], axis=0)
+    lane = lax.broadcasted_iota(jnp.int32, rows.shape, 1)
+    spare = jnp.where(lane == share, high, jnp.where(lane == share + 1, gates - high, 0.0))
+    packed = jnp.where(lane < share, rows, spare)
     out[...] = packed.astype(BF16).reshape(out.shape)
-
-
-SHARE = 448
 
 
 def per_device(
@@ -244,7 +259,7 @@
     theirs = lax.ppermute(mine, "core", swap)
     row_part = kernel_call(
         row_kernel,
-        jax.ShapeDtypeStruct((ys, slots, wide), BF16),
+        jax.ShapeDtypeStruct((ys, slots // 2 + 8, 2 * share), BF16),
         where,
         mine,
         theirs,

time: 167 us -> 166 us (level)
  transfers between devices with their start and end apart: 13 -> 13, of which waited for: 6 -> 6; matrix products, arithmetic and copies ran while one was open for 2% -> 2% of each run, Pallas kernels for 5% -> 6%
where the time goes in v6:
time: 166 us; the launch traced here: 164 us
  starting transfers between devices  68.6 us (41%)
  blocking collectives  36.1 us (22%)
  waiting for transfers between devices  24.3 us (15%)
  between operations  14.4 us (9%)
  Pallas kernels  12 us (7%)
  local copies, waits for them, and re-layouts  5.93 us (4%)
  other arithmetic  2.53 us (2%)
    all_to_all x3, blocking collectives, exchange(): return lax.all_to_all(array, axis, 0, 0, tiled=True)  36.1 us
    all_to_all x2, starting transfers between devices, exchange(): return lax.all_to_all(array, axis, 0, 0, tiled=True)  29.5 us
    all_to_all x2, waiting for transfers between devices, exchange(): return lax.all_to_all(array, axis, 0, 0, tiled=True)  20.5 us
    ppermute x3, starting transfers between devices, per_device(): lax.ppermute(downs[r], 'y', [(i, (i + r) % ys) for i in range(ys)])  10.7 us
    pallas_call x7, Pallas kernels, kernel_call(): pl.pallas_call(body, out_shape=out_shape, in_specs=[smem] + [vmem] * len(...  10.1 us
    ppermute x3, starting transfers between devices, per_device(): lax.ppermute(folded[r], 'y', [(i, (i + r) % ys) for i in range(ys)])  8.78 us
    ppermute x1, starting transfers between devices, per_device(): other_rows = lax.ppermute(own_rows, 'core', swap)  6.38 us
    ppermute x1, starting transfers between devices, per_device(): shared_taken = lax.ppermute(shared_theirs, 'core', swap)  5.26 us
  transfers between devices with their start and end apart: 13, of which 6 were waited for; matrix products, arithmetic and copies ran while one was open for 2% of the time, Pallas kernels for 6%

profile of v6, /device:TPU:1, one launch (start us, length us, event | category | flops | bytes accessed | tf_op | source)
XLA Modules:
  0.0 164.2 jit_solution(1325953164387921605)
XLA Ops:
  8.2 9.8 %all_to_all.25 = bf16[4,3,56,128]{3,2,1,0:T(8,128)(2,1)S(1)} all-to-all(bf16[4,3,56,128]{3,2,1,0:T(8,128)(2,1)S(1)} %broadcast_in_dim.5), channel_id=1, replica_groups=mesh['x'=4,'z'=16,'y'=4,'core'=2] {'x'}, dimensions={0} | all-to-all | bytes 344064 | tf_op jit(solution)/shard_map/all_to_all | solution.py:17
  20.3 1.6 shard_map.104
  22.0 16.6 %all-to-all-start = ((bf16[64,4,448]{2,1,0:T(4,128)(2,1)}), bf16[64,4,448]{2,1,0:T(4,128)(2,1)S(1)}, u32[]{:S(2)}, u32[]{:S(2)}) async-start(bf16[64,4,448]{2,1,0:T(4,128)(2,1)} %shard_map.104), calls=%async_computation | async-start | bytes 524288 | tf_op jit(solution)/shard_map/all_to_all | solution.py:17
  39.6 4.2 %collective-permute-start.5 = (bf16[2,4,448,128]{3,2,1,0:T(8,128)(2,1)}, bf16[2,4,448,128]{3,2,1,0:T(8,128)(2,1)}, u32[]{:S(2)}, u32[]{:S(2)}) collective-permute-start(bf16[2,4,448,128]{3,2,1,0:T(8,128)(2,1)} %dynamic-slice_bitcast_fusion), channel_id=1, source_target_pairs={{0,1},{1,0},{2,3},{3,2},{4,5},{5,4},{6,7},{7,6},{8,9},{9,8},{10,11... | collective-permute-start | bytes 2752520 | tf_op jit(solution)/shard_map/ppermute | solution.py:256
  43.8 1.7 %shard_map.105 = (bf16[2,128,448]{2,1,0:T(8,128)(2,1)S(1)}, bf16[2,128,448]{2,1,0:T(8,128)(2,1)}, bf16[2,128,448]{2,1,0:T(8,128)(2,1)}, bf16[2,128,448]{2,1,0:T(8,128)(2,1)}) custom-call(s32[2]{0:T(128)S(1)} %pad_add_fusion.where, bf16[128,3584]{1,0:T(8,128)(2,1)S(1)} %bitcast.28), custom_call_target="tpu_custom_call" | custom-call | tf_op jit(solution)/shard_map/pallas_call | solution.py:36
  45.5 3.2 %collective-permute-start.1 = (bf16[2,128,448]{2,1,0:T(8,128)(2,1)}, bf16[2,128,448]{2,1,0:T(8,128)(2,1)S(1)}, u32[]{:S(2)}, u32[]{:S(2)}) collective-permute-start(bf16[2,128,448]{2,1,0:T(8,128)(2,1)} %get-tuple-element.13), channel_id=1, source_target_pairs={{0,2},{2,4},{4,6},{6,0},{1,3},{3,5},{5,7},{7,1},{8,10},{10,12},{12... | collective-permute-start | bytes 688136 | tf_op jit(solution)/shard_map/ppermute | solution.py:234
  48.7 4.5 %collective-permute-start.2 = (bf16[2,128,448]{2,1,0:T(8,128)(2,1)}, bf16[2,128,448]{2,1,0:T(8,128)(2,1)S(1)}, u32[]{:S(2)}, u32[]{:S(2)}) collective-permute-start(bf16[2,128,448]{2,1,0:T(8,128)(2,1)} %get-tuple-element.14), channel_id=1, source_target_pairs={{0,4},{2,6},{4,0},{6,2},{1,5},{3,7},{5,1},{7,3},{8,12},{10,14},{12... | collective-permute-start | bytes 688136 | tf_op jit(solution)/shard_map/ppermute | solution.py:234
  53.2 3.0 %collective-permute-start.3 = (bf16[2,128,448]{2,1,0:T(8,128)(2,1)}, bf16[2,128,448]{2,1,0:T(8,128)(2,1)S(1)}, u32[]{:S(2)}, u32[]{:S(2)}) collective-permute-start(bf16[2,128,448]{2,1,0:T(8,128)(2,1)} %get-tuple-element.15), channel_id=1, source_target_pairs={{0,6},{2,0},{4,2},{6,4},{1,7},{3,1},{5,3},{7,5},{8,14},{10,8},{12,... | collective-permute-start | bytes 688136 | tf_op jit(solution)/shard_map/ppermute | solution.py:234
  56.2 3.0 %all-to-all-done.own = bf16[64,4,448]{2,1,0:T(4,128)(2,1)S(1)} async-done(((bf16[64,4,448]{2,1,0:T(4,128)(2,1)}), bf16[64,4,448]{2,1,0:T(4,128)(2,1)S(1)}, u32[]{:S(2)}, u32[]{:S(2)}) %all-to-all-start) | async-done | bytes 229408 | tf_op jit(solution)/shard_map/all_to_all | solution.py:17
  59.3 6.4 %collective-permute-start = (bf16[64,4,448]{2,1,0:T(4,128)(2,1)S(1)}, bf16[64,4,448]{2,1,0:T(4,128)(2,1)S(1)}, u32[]{:S(2)}, u32[]{:S(2)}) collective-permute-start(bf16[64,4,448]{2,1,0:T(4,128)(2,1)S(1)} %all-to-all-done.own), channel_id=1, source_target_pairs={{0,1},{1,0},{2,3},{3,2},{4,5},{5,4},{6,7},{7,6},{8,9},{9,8},{10,11... | collective-permute-start | bytes 688136 | tf_op jit(solution)/shard_map/ppermute | solution.py:237
  66.8 1.2 shard_map.106
  68.1 10.0 %all_to_all.26.parts = bf16[4,256,128]{2,1,0:T(8,128)(2,1)S(1)} all-to-all(bf16[4,256,128]{2,1,0:T(8,128)(2,1)S(1)} %shard_map.106), channel_id=1, replica_groups=mesh['x'=4,'z'=16,'y'=4,'core'=2] {'y'}, dimensions={0} | all-to-all | bytes 524288 | tf_op jit(solution)/shard_map/all_to_all | solution.py:17
  78.8 3.7 %collective-permute-start.4 = (bf16[256,384]{1,0:T(8,128)(2,1)S(1)}, bf16[256,384]{1,0:T(8,128)(2,1)S(1)}, u32[]{:S(2)}, u32[]{:S(2)}) collective-permute-start(bf16[256,384]{1,0:T(8,128)(2,1)S(1)} %shard_map.107.mine), channel_id=1, source_target_pairs={{0,1},{1,0},{2,3},{3,2},{4,5},{5,4},{6,7},{7,6},{8,9},{9,8},{10,11... | collective-permute-start | bytes 589832 | tf_op jit(solution)/shard_map/ppermute | solution.py:259
  83.5 2.5 %shard_map.108 = bf16[4,136,896]{2,1,0:T(8,128)(2,1)S(1)} custom-call(s32[2]{0:T(128)S(1)} %pad_add_fusion.where, bf16[256,384]{1,0:T(8,128)(2,1)S(1)} %shard_map.107.mine, bf16[256,384]{1,0:T(8,128)(2,1)S(1)} %collective-permute-done.4.theirs, bf16[2,3584,128]{2,1,0:T(8,128)(2,1)S(1)} %bitcast.27, bf16[2,4,448,128]{3,2,1,0:T(8,128)(2,1)} %collective-permute-done.5.other), custom_call_target="tpu_custom_call" | custom-call | tf_op jit(solution)/shard_map/pallas_call | solution.py:36
  86.0 16.3 %all_to_all.27.parts = bf16[4,136,896]{2,1,0:T(8,128)(2,1)S(1)} all-to-all(bf16[4,136,896]{2,1,0:T(8,128)(2,1)S(1)} %shard_map.108), channel_id=1, replica_groups=mesh['x'=4,'z'=16,'y'=4,'core'=2] {'y'}, dimensions={0} | all-to-all | bytes 1949696 | tf_op jit(solution)/shard_map/all_to_all | solution.py:17
  102.3 1.5 shard_map.109
  103.8 12.9 %all-to-all-start.3 = ((bf16[64,4,512]{2,1,0:T(4,128)(2,1)}), bf16[64,4,512]{2,1,0:T(4,128)(2,1)S(1)}, u32[]{:S(2)}, u32[]{:S(2)}) async-start(bf16[64,4,512]{2,1,0:T(4,128)(2,1)} %shard_map.109), calls=%async_computation.3 | async-start | bytes 524288 | tf_op jit(solution)/shard_map/all_to_all | solution.py:17
  117.8 17.5 %all-to-all-done.3 = bf16[64,4,512]{2,1,0:T(4,128)(2,1)S(1)} async-done(((bf16[64,4,512]{2,1,0:T(4,128)(2,1)}), bf16[64,4,512]{2,1,0:T(4,128)(2,1)S(1)}, u32[]{:S(2)}, u32[]{:S(2)}) %all-to-all-start.3) | async-done | bytes 262176 | tf_op jit(solution)/shard_map/all_to_all | solution.py:17
  135.7 1.8 %copy-done.1 = bf16[16,3,224,128]{3,2,1,0:T(8,128)(2,1)S(1)} copy-done((bf16[16,3,224,128]{3,2,1,0:T(8,128)(2,1)S(1)}, bf16[16,3,224,128]{3,2,1,0:T(8,128)(2,1)}, u32[]{:S(2)}) %copy-start.1) | copy-done | bytes 2752536
  137.4 1.9 %shard_map.110 = (bf16[8,16,224]{2,1,0:T(8,128)(2,1)S(1)}, bf16[8,16,224]{2,1,0:T(8,128)(2,1)S(1)}) custom-call(s32[2]{0:T(128)S(1)} %pad_add_fusion.where, bf16[16,16,224]{2,1,0:T(8,128)(2,1)S(1)} %reshape.62.turned, bf16[16,3,224,128]{3,2,1,0:T(8,128)(2,1)S(1)} %copy-done.1, bf16[2,16,128]{2,1,0:T(8,128)(2,1)S(1)} %copy-done.8), custom_call_target="tpu_custom_call" | custom-call | tf_op jit(solution)/shard_map/pallas_call | solution.py:281
  139.4 5.3 %collective-permute-start.6 = (bf16[8,16,224]{2,1,0:T(8,128)(2,1)S(1)}, bf16[8,16,224]{2,1,0:T(8,128)(2,1)S(1)}, u32[]{:S(2)}, u32[]{:S(2)}) collective-permute-start(bf16[8,16,224]{2,1,0:T(8,128)(2,1)S(1)} %get-tuple-element.17), channel_id=1, source_target_pairs={{0,1},{1,0},{2,3},{3,2},{4,5},{5,4},{6,7},{7,6},{8,9},{9,8},{10,11... | collective-permute-start | bytes 172040 | tf_op jit(solution)/shard_map/ppermute | solution.py:290
  146.4 2.2 %collective-permute-start.7 = (bf16[16,448]{1,0:T(8,128)(2,1)S(1)}, bf16[16,448]{1,0:T(8,128)(2,1)S(1)}, u32[]{:S(2)}, u32[]{:S(2)}) collective-permute-start(bf16[16,448]{1,0:T(8,128)(2,1)S(1)} %get-tuple-element.19), channel_id=1, source_target_pairs={{0,2},{2,4},{4,6},{6,0},{1,3},{3,5},{5,7},{7,1},{8,10},{10,12},{12... | collective-permute-start | bytes 43016 | tf_op jit(solution)/shard_map/ppermute | solution.py:299
  148.6 3.7 %collective-permute-start.8 = (bf16[16,448]{1,0:T(8,128)(2,1)S(1)}, bf16[16,448]{1,0:T(8,128)(2,1)S(1)}, u32[]{:S(2)}, u32[]{:S(2)}) collective-permute-start(bf16[16,448]{1,0:T(8,128)(2,1)S(1)} %get-tuple-element.20), channel_id=1, source_target_pairs={{0,4},{2,6},{4,0},{6,2},{1,5},{3,7},{5,1},{7,3},{8,12},{10,14},{12... | collective-permute-start | bytes 43016 | tf_op jit(solution)/shard_map/ppermute | solution.py:299
  152.3 2.9 %collective-permute-start.9 = (bf16[16,448]{1,0:T(8,128)(2,1)S(1)}, bf16[16,448]{1,0:T(8,128)(2,1)S(1)}, u32[]{:S(2)}, u32[]{:S(2)}) collective-permute-start(bf16[16,448]{1,0:T(8,128)(2,1)S(1)} %get-tuple-element.21), channel_id=1, source_target_pairs={{0,6},{2,0},{4,2},{6,4},{1,7},{3,1},{5,3},{7,5},{8,14},{10,8},{12,... | collective-permute-start | bytes 43016 | tf_op jit(solution)/shard_map/ppermute | solution.py:299
  (51 shorter events, 12.5 us)
Async XLA Ops:
  7.2 31.4 %copy-start = (bf16[1,2,3584,128]{3,2,1,0:T(8,128)(2,1)S(1)}, bf16[1,2,3584,128]{3,2,1,0:T(8,128)(2,1)}, u32[]{:S(2)}) copy-start(bf16[1,2,3584,128]{3,2,1,0:T(8,128)(2,1)} %param.12) | copy-start | bytes 5505028
  7.2 128.5 %all-gather.2.cloned.1.call-start = ((), (), s32[]{:S(2)}) async-start(), calls=%async_computation.5 | async-start | bytes 2924544 | tf_op jit(solution)/shard_map/all_gather | solution.py:216
  8.1 35.7 %copy-start.2 = (bf16[1,128,3584]{2,1,0:T(8,128)(2,1)S(1)}, bf16[1,128,3584]{2,1,0:T(8,128)(2,1)}, u32[]{:S(2)}) copy-start(bf16[1,128,3584]{2,1,0:T(8,128)(2,1)} %param.13) | copy-start | bytes 2752516
  18.7 0.9 copy-start.3
  19.6 0.7 copy-start.6
  22.0 37.3 %all-to-all-start = ((bf16[64,4,448]{2,1,0:T(4,128)(2,1)}), bf16[64,4,448]{2,1,0:T(4,128)(2,1)S(1)}, u32[]{:S(2)}, u32[]{:S(2)}) async-start(bf16[64,4,448]{2,1,0:T(4,128)(2,1)} %shard_map.104), calls=%async_computation | async-start | bytes 524288 | tf_op jit(solution)/shard_map/all_to_all | solution.py:17
  39.6 38.5 %copy-start.5 = (bf16[1,2,256,128]{3,2,1,0:T(8,128)(2,1)S(1)}, bf16[1,2,256,128]{3,2,1,0:T(8,128)(2,1)}, u32[]{:S(2)}) copy-start(bf16[1,2,256,128]{3,2,1,0:T(8,128)(2,1)} %param.14) | copy-start | bytes 393220
  39.6 42.9 %collective-permute-start.5 = (bf16[2,4,448,128]{3,2,1,0:T(8,128)(2,1)}, bf16[2,4,448,128]{3,2,1,0:T(8,128)(2,1)}, u32[]{:S(2)}, u32[]{:S(2)}) collective-permute-start(bf16[2,4,448,128]{3,2,1,0:T(8,128)(2,1)} %dynamic-slice_bitcast_fusion), channel_id=1, source_target_pairs={{0,1},{1,0},{2,3},{3,2},{4,5},{5,4},{6,7},{7,6},{8,9},{9,8},{10,11... | collective-permute-start | bytes 2752520 | tf_op jit(solution)/shard_map/ppermute | solution.py:256
  45.5 20.2 %collective-permute-start.1 = (bf16[2,128,448]{2,1,0:T(8,128)(2,1)}, bf16[2,128,448]{2,1,0:T(8,128)(2,1)S(1)}, u32[]{:S(2)}, u32[]{:S(2)}) collective-permute-start(bf16[2,128,448]{2,1,0:T(8,128)(2,1)} %get-tuple-element.13), channel_id=1, source_target_pairs={{0,2},{2,4},{4,6},{6,0},{1,3},{3,5},{5,7},{7,1},{8,10},{10,12},{12... | collective-permute-start | bytes 688136 | tf_op jit(solution)/shard_map/ppermute | solution.py:234
  48.7 17.0 %collective-permute-start.2 = (bf16[2,128,448]{2,1,0:T(8,128)(2,1)}, bf16[2,128,448]{2,1,0:T(8,128)(2,1)S(1)}, u32[]{:S(2)}, u32[]{:S(2)}) collective-permute-start(bf16[2,128,448]{2,1,0:T(8,128)(2,1)} %get-tuple-element.14), channel_id=1, source_target_pairs={{0,4},{2,6},{4,0},{6,2},{1,5},{3,7},{5,1},{7,3},{8,12},{10,14},{12... | collective-permute-start | bytes 688136 | tf_op jit(solution)/shard_map/ppermute | solution.py:234
  53.2 12.4 %collective-permute-start.3 = (bf16[2,128,448]{2,1,0:T(8,128)(2,1)}, bf16[2,128,448]{2,1,0:T(8,128)(2,1)S(1)}, u32[]{:S(2)}, u32[]{:S(2)}) collective-permute-start(bf16[2,128,448]{2,1,0:T(8,128)(2,1)} %get-tuple-element.15), channel_id=1, source_target_pairs={{0,6},{2,0},{4,2},{6,4},{1,7},{3,1},{5,3},{7,5},{8,14},{10,8},{12,... | collective-permute-start | bytes 688136 | tf_op jit(solution)/shard_map/ppermute | solution.py:234
  59.3 7.5 %collective-permute-start = (bf16[64,4,448]{2,1,0:T(4,128)(2,1)S(1)}, bf16[64,4,448]{2,1,0:T(4,128)(2,1)S(1)}, u32[]{:S(2)}, u32[]{:S(2)}) collective-permute-start(bf16[64,4,448]{2,1,0:T(4,128)(2,1)S(1)} %all-to-all-done.own), channel_id=1, source_target_pairs={{0,1},{1,0},{2,3},{3,2},{4,5},{5,4},{6,7},{7,6},{8,9},{9,8},{10,11... | collective-permute-start | bytes 688136 | tf_op jit(solution)/shard_map/ppermute | solution.py:237
  78.8 4.7 %collective-permute-start.4 = (bf16[256,384]{1,0:T(8,128)(2,1)S(1)}, bf16[256,384]{1,0:T(8,128)(2,1)S(1)}, u32[]{:S(2)}, u32[]{:S(2)}) collective-permute-start(bf16[256,384]{1,0:T(8,128)(2,1)S(1)} %shard_map.107.mine), channel_id=1, source_target_pairs={{0,1},{1,0},{2,3},{3,2},{4,5},{5,4},{6,7},{7,6},{8,9},{9,8},{10,11... | collective-permute-start | bytes 589832 | tf_op jit(solution)/shard_map/ppermute | solution.py:259
  86.0 30.7 %copy-start.4 = (bf16[16,3584]{1,0:T(8,128)(2,1)S(1)}, bf16[16,3584]{1,0:T(8,128)(2,1)}, u32[]{:S(2)}) copy-start(bf16[16,3584]{1,0:T(8,128)(2,1)} %tokens.1) | copy-start | bytes 344068
  102.3 15.3 %copy-start.7 = (s32[16,8]{0,1:T(8,128)S(1)}, s32[16,8]{0,1:T(8,128)}, u32[]{:S(2)}) copy-start(s32[16,8]{0,1:T(8,128)} %param.10) | copy-start | bytes 1540
  102.3 33.4 %copy-start.8 = (bf16[2,16,128]{2,1,0:T(8,128)(2,1)S(1)}, bf16[2,16,128]{2,1,0:T(8,128)(2,1)}, u32[]{:S(2)}) copy-start(bf16[2,16,128]{2,1,0:T(8,128)(2,1)} %saved.1) | copy-start | bytes 24580
  103.8 31.5 %all-to-all-start.3 = ((bf16[64,4,512]{2,1,0:T(4,128)(2,1)}), bf16[64,4,512]{2,1,0:T(4,128)(2,1)S(1)}, u32[]{:S(2)}, u32[]{:S(2)}) async-start(bf16[64,4,512]{2,1,0:T(4,128)(2,1)} %shard_map.109), calls=%async_computation.3 | async-start | bytes 524288 | tf_op jit(solution)/shard_map/all_to_all | solution.py:17
  135.4 9.3 %copy-start.9 = (f32[16,8]{0,1:T(8,128)S(1)}, f32[16,8]{0,1:T(8,128)}, u32[]{:S(2)}) copy-start(f32[16,8]{0,1:T(8,128)} %param.11) | copy-start | bytes 1540
  135.7 1.8 %copy-start.1 = (bf16[16,3,224,128]{3,2,1,0:T(8,128)(2,1)S(1)}, bf16[16,3,224,128]{3,2,1,0:T(8,128)(2,1)}, u32[]{:S(2)}) copy-start(bf16[16,3,224,128]{3,2,1,0:T(8,128)(2,1)} %all-gather.2.cloned.1.call-done.pieces) | copy-start | bytes 8257540
  139.4 6.1 %collective-permute-start.6 = (bf16[8,16,224]{2,1,0:T(8,128)(2,1)S(1)}, bf16[8,16,224]{2,1,0:T(8,128)(2,1)S(1)}, u32[]{:S(2)}, u32[]{:S(2)}) collective-permute-start(bf16[8,16,224]{2,1,0:T(8,128)(2,1)S(1)} %get-tuple-element.17), channel_id=1, source_target_pairs={{0,1},{1,0},{2,3},{3,2},{4,5},{5,4},{6,7},{7,6},{8,9},{9,8},{10,11... | collective-permute-start | bytes 172040 | tf_op jit(solution)/shard_map/ppermute | solution.py:290
  146.4 9.6 %collective-permute-start.7 = (bf16[16,448]{1,0:T(8,128)(2,1)S(1)}, bf16[16,448]{1,0:T(8,128)(2,1)S(1)}, u32[]{:S(2)}, u32[]{:S(2)}) collective-permute-start(bf16[16,448]{1,0:T(8,128)(2,1)S(1)} %get-tuple-element.19), channel_id=1, source_target_pairs={{0,2},{2,4},{4,6},{6,0},{1,3},{3,5},{5,7},{7,1},{8,10},{10,12},{12... | collective-permute-start | bytes 43016 | tf_op jit(solution)/shard_map/ppermute | solution.py:299
  148.6 7.4 %collective-permute-start.8 = (bf16[16,448]{1,0:T(8,128)(2,1)S(1)}, bf16[16,448]{1,0:T(8,128)(2,1)S(1)}, u32[]{:S(2)}, u32[]{:S(2)}) collective-permute-start(bf16[16,448]{1,0:T(8,128)(2,1)S(1)} %get-tuple-element.20), channel_id=1, source_target_pairs={{0,4},{2,6},{4,0},{6,2},{1,5},{3,7},{5,1},{7,3},{8,12},{10,14},{12... | collective-permute-start | bytes 43016 | tf_op jit(solution)/shard_map/ppermute | solution.py:299
  152.3 4.5 %collective-permute-start.9 = (bf16[16,448]{1,0:T(8,128)(2,1)S(1)}, bf16[16,448]{1,0:T(8,128)(2,1)S(1)}, u32[]{:S(2)}, u32[]{:S(2)}) collective-permute-start(bf16[16,448]{1,0:T(8,128)(2,1)S(1)} %get-tuple-element.21), channel_id=1, source_target_pairs={{0,6},{2,0},{4,2},{6,4},{1,7},{3,1},{5,3},{7,5},{8,14},{10,8},{12,... | collective-permute-start | bytes 43016 | tf_op jit(solution)/shard_map/ppermute | solution.py:299
Sparse Core Ops, SparseCore 0:
  18.8 77.9 all-gather.1

commit v7 on v6

--- a/solution.py
+++ b/solution.py
@@ -111,9 +111,14 @@
     core, y = where[0], where[1]
     mine = own[...].reshape(out.shape[1], own.shape[2])
     theirs = other[...].reshape(mine.shape)
-    for r, weight in enumerate(weights):
-        part = contract_last(mine, weight[core]) + contract_last(theirs, weight[1 - core])
-        out[(y + len(weights) - r) % len(weights)] = part.astype(BF16)
+    count, hidden = len(weights), out.shape[2]
+    for r in range(0, count, 2):
+        pair = weights[r : r + 2]
+        part = contract_last(mine, jnp.concatenate([w[core] for w in pair], axis=0))
+        part += contract_last(theirs, jnp.concatenate([w[1 - core] for w in pair], axis=0))
+        for i in range(2):
+            block = part[:, i * hidden : (i + 1) * hidden]
+            out[(y + count - r - i) % count] = block.astype(BF16)
 
 
 def gate_kernel(where, parts, saved, out):

time: 166 us -> 165 us (level)
  transfers between devices with their start and end apart: 13 -> 13, of which waited for: 6 -> 6; matrix products, arithmetic and copies ran while one was open for 2% -> 2% of each run, Pallas kernels for 6% -> 5%
where the time goes in v7:
time: 165 us; the launch traced here: 164 us
  starting transfers between devices  68.7 us (42%)
  blocking collectives  36 us (22%)
  waiting for transfers between devices  24.3 us (15%)
  between operations  14.4 us (9%)
  Pallas kernels  11.8 us (7%)
  local copies, waits for them, and re-layouts  5.93 us (4%)
  other arithmetic  2.53 us (2%)
    all_to_all x3, blocking collectives, exchange(): return lax.all_to_all(array, axis, 0, 0, tiled=True)  36 us
    all_to_all x2, starting transfers between devices, exchange(): return lax.all_to_all(array, axis, 0, 0, tiled=True)  29.6 us
    all_to_all x2, waiting for transfers between devices, exchange(): return lax.all_to_all(array, axis, 0, 0, tiled=True)  20.5 us
    ppermute x3, starting transfers between devices, per_device(): lax.ppermute(downs[r], 'y', [(i, (i + r) % ys) for i in range(ys)])  10.7 us
    pallas_call x7, Pallas kernels, kernel_call(): pl.pallas_call(body, out_shape=out_shape, in_specs=[smem] + [vmem] * len(...  9.88 us
    ppermute x3, starting transfers between devices, per_device(): lax.ppermute(folded[r], 'y', [(i, (i + r) % ys) for i in range(ys)])  8.78 us
    ppermute x1, starting transfers between devices, per_device(): other_rows = lax.ppermute(own_rows, 'core', swap)  6.38 us
    ppermute x1, starting transfers between devices, per_device(): shared_taken = lax.ppermute(shared_theirs, 'core', swap)  5.26 us
  transfers between devices with their start and end apart: 13, of which 6 were waited for; matrix products, arithmetic and copies ran while one was open for 2% of the time, Pallas kernels for 5%

profile of v7, /device:TPU:1, one launch (start us, length us, event | category | flops | bytes accessed | tf_op | source)
XLA Modules:
  0.0 164.0 jit_solution(7304825190075510203)
XLA Ops:
  8.2 9.8 %all_to_all.25 = bf16[4,3,56,128]{3,2,1,0:T(8,128)(2,1)S(1)} all-to-all(bf16[4,3,56,128]{3,2,1,0:T(8,128)(2,1)S(1)} %broadcast_in_dim.5), channel_id=1, replica_groups=mesh['x'=4,'z'=16,'y'=4,'core'=2] {'x'}, dimensions={0} | all-to-all | bytes 344064 | tf_op jit(solution)/shard_map/all_to_all | solution.py:17
  20.3 1.6 shard_map.104
  22.0 16.6 %all-to-all-start = ((bf16[64,4,448]{2,1,0:T(4,128)(2,1)}), bf16[64,4,448]{2,1,0:T(4,128)(2,1)S(1)}, u32[]{:S(2)}, u32[]{:S(2)}) async-start(bf16[64,4,448]{2,1,0:T(4,128)(2,1)} %shard_map.104), calls=%async_computation | async-start | bytes 524288 | tf_op jit(solution)/shard_map/all_to_all | solution.py:17
  39.6 4.2 %collective-permute-start.5 = (bf16[2,4,448,128]{3,2,1,0:T(8,128)(2,1)}, bf16[2,4,448,128]{3,2,1,0:T(8,128)(2,1)}, u32[]{:S(2)}, u32[]{:S(2)}) collective-permute-start(bf16[2,4,448,128]{3,2,1,0:T(8,128)(2,1)} %dynamic-slice_bitcast_fusion), channel_id=1, source_target_pairs={{0,1},{1,0},{2,3},{3,2},{4,5},{5,4},{6,7},{7,6},{8,9},{9,8},{10,11... | collective-permute-start | bytes 2752520 | tf_op jit(solution)/shard_map/ppermute | solution.py:261
  43.8 1.7 %shard_map.105 = (bf16[2,128,448]{2,1,0:T(8,128)(2,1)S(1)}, bf16[2,128,448]{2,1,0:T(8,128)(2,1)}, bf16[2,128,448]{2,1,0:T(8,128)(2,1)}, bf16[2,128,448]{2,1,0:T(8,128)(2,1)}) custom-call(s32[2]{0:T(128)S(1)} %pad_add_fusion.where, bf16[128,3584]{1,0:T(8,128)(2,1)S(1)} %bitcast.28), custom_call_target="tpu_custom_call" | custom-call | tf_op jit(solution)/shard_map/pallas_call | solution.py:36
  45.5 3.2 %collective-permute-start.1 = (bf16[2,128,448]{2,1,0:T(8,128)(2,1)}, bf16[2,128,448]{2,1,0:T(8,128)(2,1)S(1)}, u32[]{:S(2)}, u32[]{:S(2)}) collective-permute-start(bf16[2,128,448]{2,1,0:T(8,128)(2,1)} %get-tuple-element.13), channel_id=1, source_target_pairs={{0,2},{2,4},{4,6},{6,0},{1,3},{3,5},{5,7},{7,1},{8,10},{10,12},{12... | collective-permute-start | bytes 688136 | tf_op jit(solution)/shard_map/ppermute | solution.py:239
  48.7 4.5 %collective-permute-start.2 = (bf16[2,128,448]{2,1,0:T(8,128)(2,1)}, bf16[2,128,448]{2,1,0:T(8,128)(2,1)S(1)}, u32[]{:S(2)}, u32[]{:S(2)}) collective-permute-start(bf16[2,128,448]{2,1,0:T(8,128)(2,1)} %get-tuple-element.14), channel_id=1, source_target_pairs={{0,4},{2,6},{4,0},{6,2},{1,5},{3,7},{5,1},{7,3},{8,12},{10,14},{12... | collective-permute-start | bytes 688136 | tf_op jit(solution)/shard_map/ppermute | solution.py:239
  53.2 3.0 %collective-permute-start.3 = (bf16[2,128,448]{2,1,0:T(8,128)(2,1)}, bf16[2,128,448]{2,1,0:T(8,128)(2,1)S(1)}, u32[]{:S(2)}, u32[]{:S(2)}) collective-permute-start(bf16[2,128,448]{2,1,0:T(8,128)(2,1)} %get-tuple-element.15), channel_id=1, source_target_pairs={{0,6},{2,0},{4,2},{6,4},{1,7},{3,1},{5,3},{7,5},{8,14},{10,8},{12,... | collective-permute-start | bytes 688136 | tf_op jit(solution)/shard_map/ppermute | solution.py:239
  56.2 3.0 %all-to-all-done.own = bf16[64,4,448]{2,1,0:T(4,128)(2,1)S(1)} async-done(((bf16[64,4,448]{2,1,0:T(4,128)(2,1)}), bf16[64,4,448]{2,1,0:T(4,128)(2,1)S(1)}, u32[]{:S(2)}, u32[]{:S(2)}) %all-to-all-start) | async-done | bytes 229408 | tf_op jit(solution)/shard_map/all_to_all | solution.py:17
  59.3 6.4 %collective-permute-start = (bf16[64,4,448]{2,1,0:T(4,128)(2,1)S(1)}, bf16[64,4,448]{2,1,0:T(4,128)(2,1)S(1)}, u32[]{:S(2)}, u32[]{:S(2)}) collective-permute-start(bf16[64,4,448]{2,1,0:T(4,128)(2,1)S(1)} %all-to-all-done.own), channel_id=1, source_target_pairs={{0,1},{1,0},{2,3},{3,2},{4,5},{5,4},{6,7},{7,6},{8,9},{9,8},{10,11... | collective-permute-start | bytes 688136 | tf_op jit(solution)/shard_map/ppermute | solution.py:242
  65.7 1.1 collective-permute-done.other
  67.8 9.9 %all_to_all.26.parts = bf16[4,256,128]{2,1,0:T(8,128)(2,1)S(1)} all-to-all(bf16[4,256,128]{2,1,0:T(8,128)(2,1)S(1)} %shard_map.106), channel_id=1, replica_groups=mesh['x'=4,'z'=16,'y'=4,'core'=2] {'y'}, dimensions={0} | all-to-all | bytes 524288 | tf_op jit(solution)/shard_map/all_to_all | solution.py:17
  78.5 3.7 %collective-permute-start.4 = (bf16[256,384]{1,0:T(8,128)(2,1)S(1)}, bf16[256,384]{1,0:T(8,128)(2,1)S(1)}, u32[]{:S(2)}, u32[]{:S(2)}) collective-permute-start(bf16[256,384]{1,0:T(8,128)(2,1)S(1)} %shard_map.107.mine), channel_id=1, source_target_pairs={{0,1},{1,0},{2,3},{3,2},{4,5},{5,4},{6,7},{7,6},{8,9},{9,8},{10,11... | collective-permute-start | bytes 589832 | tf_op jit(solution)/shard_map/ppermute | solution.py:264
  83.3 2.5 %shard_map.108 = bf16[4,136,896]{2,1,0:T(8,128)(2,1)S(1)} custom-call(s32[2]{0:T(128)S(1)} %pad_add_fusion.where, bf16[256,384]{1,0:T(8,128)(2,1)S(1)} %shard_map.107.mine, bf16[256,384]{1,0:T(8,128)(2,1)S(1)} %collective-permute-done.4.theirs, bf16[2,3584,128]{2,1,0:T(8,128)(2,1)S(1)} %bitcast.27, bf16[2,4,448,128]{3,2,1,0:T(8,128)(2,1)} %collective-permute-done.5.other), custom_call_target="tpu_custom_call" | custom-call | tf_op jit(solution)/shard_map/pallas_call | solution.py:36
  85.8 16.3 %all_to_all.27.parts = bf16[4,136,896]{2,1,0:T(8,128)(2,1)S(1)} all-to-all(bf16[4,136,896]{2,1,0:T(8,128)(2,1)S(1)} %shard_map.108), channel_id=1, replica_groups=mesh['x'=4,'z'=16,'y'=4,'core'=2] {'y'}, dimensions={0} | all-to-all | bytes 1949696 | tf_op jit(solution)/shard_map/all_to_all | solution.py:17
  102.0 1.5 shard_map.109
  103.5 12.9 %all-to-all-start.3 = ((bf16[64,4,512]{2,1,0:T(4,128)(2,1)}), bf16[64,4,512]{2,1,0:T(4,128)(2,1)S(1)}, u32[]{:S(2)}, u32[]{:S(2)}) async-start(bf16[64,4,512]{2,1,0:T(4,128)(2,1)} %shard_map.109), calls=%async_computation.3 | async-start | bytes 524288 | tf_op jit(solution)/shard_map/all_to_all | solution.py:17
  117.6 17.5 %all-to-all-done.3 = bf16[64,4,512]{2,1,0:T(4,128)(2,1)S(1)} async-done(((bf16[64,4,512]{2,1,0:T(4,128)(2,1)}), bf16[64,4,512]{2,1,0:T(4,128)(2,1)S(1)}, u32[]{:S(2)}, u32[]{:S(2)}) %all-to-all-start.3) | async-done | bytes 262176 | tf_op jit(solution)/shard_map/all_to_all | solution.py:17
  135.4 1.8 %copy-done.1 = bf16[16,3,224,128]{3,2,1,0:T(8,128)(2,1)S(1)} copy-done((bf16[16,3,224,128]{3,2,1,0:T(8,128)(2,1)S(1)}, bf16[16,3,224,128]{3,2,1,0:T(8,128)(2,1)}, u32[]{:S(2)}) %copy-start.1) | copy-done | bytes 2752536
  137.2 1.9 %shard_map.110 = (bf16[8,16,224]{2,1,0:T(8,128)(2,1)S(1)}, bf16[8,16,224]{2,1,0:T(8,128)(2,1)S(1)}) custom-call(s32[2]{0:T(128)S(1)} %pad_add_fusion.where, bf16[16,16,224]{2,1,0:T(8,128)(2,1)S(1)} %reshape.62.turned, bf16[16,3,224,128]{3,2,1,0:T(8,128)(2,1)S(1)} %copy-done.1, bf16[2,16,128]{2,1,0:T(8,128)(2,1)S(1)} %copy-done.8), custom_call_target="tpu_custom_call" | custom-call | tf_op jit(solution)/shard_map/pallas_call | solution.py:286
  139.1 5.3 %collective-permute-start.6 = (bf16[8,16,224]{2,1,0:T(8,128)(2,1)S(1)}, bf16[8,16,224]{2,1,0:T(8,128)(2,1)S(1)}, u32[]{:S(2)}, u32[]{:S(2)}) collective-permute-start(bf16[8,16,224]{2,1,0:T(8,128)(2,1)S(1)} %get-tuple-element.17), channel_id=1, source_target_pairs={{0,1},{1,0},{2,3},{3,2},{4,5},{5,4},{6,7},{7,6},{8,9},{9,8},{10,11... | collective-permute-start | bytes 172040 | tf_op jit(solution)/shard_map/ppermute | solution.py:295
  146.2 2.2 %collective-permute-start.7 = (bf16[16,448]{1,0:T(8,128)(2,1)S(1)}, bf16[16,448]{1,0:T(8,128)(2,1)S(1)}, u32[]{:S(2)}, u32[]{:S(2)}) collective-permute-start(bf16[16,448]{1,0:T(8,128)(2,1)S(1)} %get-tuple-element.19), channel_id=1, source_target_pairs={{0,2},{2,4},{4,6},{6,0},{1,3},{3,5},{5,7},{7,1},{8,10},{10,12},{12... | collective-permute-start | bytes 43016 | tf_op jit(solution)/shard_map/ppermute | solution.py:304
  148.4 3.7 %collective-permute-start.8 = (bf16[16,448]{1,0:T(8,128)(2,1)S(1)}, bf16[16,448]{1,0:T(8,128)(2,1)S(1)}, u32[]{:S(2)}, u32[]{:S(2)}) collective-permute-start(bf16[16,448]{1,0:T(8,128)(2,1)S(1)} %get-tuple-element.20), channel_id=1, source_target_pairs={{0,4},{2,6},{4,0},{6,2},{1,5},{3,7},{5,1},{7,3},{8,12},{10,14},{12... | collective-permute-start | bytes 43016 | tf_op jit(solution)/shard_map/ppermute | solution.py:304
  152.1 2.9 %collective-permute-start.9 = (bf16[16,448]{1,0:T(8,128)(2,1)S(1)}, bf16[16,448]{1,0:T(8,128)(2,1)S(1)}, u32[]{:S(2)}, u32[]{:S(2)}) collective-permute-start(bf16[16,448]{1,0:T(8,128)(2,1)S(1)} %get-tuple-element.21), channel_id=1, source_target_pairs={{0,6},{2,0},{4,2},{6,4},{1,7},{3,1},{5,3},{7,5},{8,14},{10,8},{12,... | collective-permute-start | bytes 43016 | tf_op jit(solution)/shard_map/ppermute | solution.py:304
  (51 shorter events, 12.4 us)
Async XLA Ops:
  7.2 31.4 %copy-start = (bf16[1,2,3584,128]{3,2,1,0:T(8,128)(2,1)S(1)}, bf16[1,2,3584,128]{3,2,1,0:T(8,128)(2,1)}, u32[]{:S(2)}) copy-start(bf16[1,2,3584,128]{3,2,1,0:T(8,128)(2,1)} %param.12) | copy-start | bytes 5505028
  7.2 128.2 %all-gather.2.cloned.1.call-start = ((), (), s32[]{:S(2)}) async-start(), calls=%async_computation.5 | async-start | bytes 2924544 | tf_op jit(solution)/shard_map/all_gather | solution.py:221
  8.1 35.7 %copy-start.2 = (bf16[1,128,3584]{2,1,0:T(8,128)(2,1)S(1)}, bf16[1,128,3584]{2,1,0:T(8,128)(2,1)}, u32[]{:S(2)}) copy-start(bf16[1,128,3584]{2,1,0:T(8,128)(2,1)} %param.13) | copy-start | bytes 2752516
  18.7 0.9 copy-start.3
  19.6 0.7 copy-start.6
  22.0 37.3 %all-to-all-start = ((bf16[64,4,448]{2,1,0:T(4,128)(2,1)}), bf16[64,4,448]{2,1,0:T(4,128)(2,1)S(1)}, u32[]{:S(2)}, u32[]{:S(2)}) async-start(bf16[64,4,448]{2,1,0:T(4,128)(2,1)} %shard_map.104), calls=%async_computation | async-start | bytes 524288 | tf_op jit(solution)/shard_map/all_to_all | solution.py:17
  39.6 38.2 %copy-start.5 = (bf16[1,2,256,128]{3,2,1,0:T(8,128)(2,1)S(1)}, bf16[1,2,256,128]{3,2,1,0:T(8,128)(2,1)}, u32[]{:S(2)}) copy-start(bf16[1,2,256,128]{3,2,1,0:T(8,128)(2,1)} %param.14) | copy-start | bytes 393220
  39.6 42.6 %collective-permute-start.5 = (bf16[2,4,448,128]{3,2,1,0:T(8,128)(2,1)}, bf16[2,4,448,128]{3,2,1,0:T(8,128)(2,1)}, u32[]{:S(2)}, u32[]{:S(2)}) collective-permute-start(bf16[2,4,448,128]{3,2,1,0:T(8,128)(2,1)} %dynamic-slice_bitcast_fusion), channel_id=1, source_target_pairs={{0,1},{1,0},{2,3},{3,2},{4,5},{5,4},{6,7},{7,6},{8,9},{9,8},{10,11... | collective-permute-start | bytes 2752520 | tf_op jit(solution)/shard_map/ppermute | solution.py:261
  45.5 20.2 %collective-permute-start.1 = (bf16[2,128,448]{2,1,0:T(8,128)(2,1)}, bf16[2,128,448]{2,1,0:T(8,128)(2,1)S(1)}, u32[]{:S(2)}, u32[]{:S(2)}) collective-permute-start(bf16[2,128,448]{2,1,0:T(8,128)(2,1)} %get-tuple-element.13), channel_id=1, source_target_pairs={{0,2},{2,4},{4,6},{6,0},{1,3},{3,5},{5,7},{7,1},{8,10},{10,12},{12... | collective-permute-start | bytes 688136 | tf_op jit(solution)/shard_map/ppermute | solution.py:239
  48.7 17.0 %collective-permute-start.2 = (bf16[2,128,448]{2,1,0:T(8,128)(2,1)}, bf16[2,128,448]{2,1,0:T(8,128)(2,1)S(1)}, u32[]{:S(2)}, u32[]{:S(2)}) collective-permute-start(bf16[2,128,448]{2,1,0:T(8,128)(2,1)} %get-tuple-element.14), channel_id=1, source_target_pairs={{0,4},{2,6},{4,0},{6,2},{1,5},{3,7},{5,1},{7,3},{8,12},{10,14},{12... | collective-permute-start | bytes 688136 | tf_op jit(solution)/shard_map/ppermute | solution.py:239
  53.2 12.4 %collective-permute-start.3 = (bf16[2,128,448]{2,1,0:T(8,128)(2,1)}, bf16[2,128,448]{2,1,0:T(8,128)(2,1)S(1)}, u32[]{:S(2)}, u32[]{:S(2)}) collective-permute-start(bf16[2,128,448]{2,1,0:T(8,128)(2,1)} %get-tuple-element.15), channel_id=1, source_target_pairs={{0,6},{2,0},{4,2},{6,4},{1,7},{3,1},{5,3},{7,5},{8,14},{10,8},{12,... | collective-permute-start | bytes 688136 | tf_op jit(solution)/shard_map/ppermute | solution.py:239
  59.3 7.5 %collective-permute-start = (bf16[64,4,448]{2,1,0:T(4,128)(2,1)S(1)}, bf16[64,4,448]{2,1,0:T(4,128)(2,1)S(1)}, u32[]{:S(2)}, u32[]{:S(2)}) collective-permute-start(bf16[64,4,448]{2,1,0:T(4,128)(2,1)S(1)} %all-to-all-done.own), channel_id=1, source_target_pairs={{0,1},{1,0},{2,3},{3,2},{4,5},{5,4},{6,7},{7,6},{8,9},{9,8},{10,11... | collective-permute-start | bytes 688136 | tf_op jit(solution)/shard_map/ppermute | solution.py:242
  78.5 4.8 %collective-permute-start.4 = (bf16[256,384]{1,0:T(8,128)(2,1)S(1)}, bf16[256,384]{1,0:T(8,128)(2,1)S(1)}, u32[]{:S(2)}, u32[]{:S(2)}) collective-permute-start(bf16[256,384]{1,0:T(8,128)(2,1)S(1)} %shard_map.107.mine), channel_id=1, source_target_pairs={{0,1},{1,0},{2,3},{3,2},{4,5},{5,4},{6,7},{7,6},{8,9},{9,8},{10,11... | collective-permute-start | bytes 589832 | tf_op jit(solution)/shard_map/ppermute | solution.py:264
  85.7 30.7 %copy-start.4 = (bf16[16,3584]{1,0:T(8,128)(2,1)S(1)}, bf16[16,3584]{1,0:T(8,128)(2,1)}, u32[]{:S(2)}) copy-start(bf16[16,3584]{1,0:T(8,128)(2,1)} %tokens.1) | copy-start | bytes 344068
  102.0 15.3 %copy-start.7 = (s32[16,8]{0,1:T(8,128)S(1)}, s32[16,8]{0,1:T(8,128)}, u32[]{:S(2)}) copy-start(s32[16,8]{0,1:T(8,128)} %param.10) | copy-start | bytes 1540
  102.0 33.4 %copy-start.8 = (bf16[2,16,128]{2,1,0:T(8,128)(2,1)S(1)}, bf16[2,16,128]{2,1,0:T(8,128)(2,1)}, u32[]{:S(2)}) copy-start(bf16[2,16,128]{2,1,0:T(8,128)(2,1)} %saved.1) | copy-start | bytes 24580
  103.5 31.6 %all-to-all-start.3 = ((bf16[64,4,512]{2,1,0:T(4,128)(2,1)}), bf16[64,4,512]{2,1,0:T(4,128)(2,1)S(1)}, u32[]{:S(2)}, u32[]{:S(2)}) async-start(bf16[64,4,512]{2,1,0:T(4,128)(2,1)} %shard_map.109), calls=%async_computation.3 | async-start | bytes 524288 | tf_op jit(solution)/shard_map/all_to_all | solution.py:17
  135.1 9.3 %copy-start.9 = (f32[16,8]{0,1:T(8,128)S(1)}, f32[16,8]{0,1:T(8,128)}, u32[]{:S(2)}) copy-start(f32[16,8]{0,1:T(8,128)} %param.11) | copy-start | bytes 1540
  135.4 1.8 %copy-start.1 = (bf16[16,3,224,128]{3,2,1,0:T(8,128)(2,1)S(1)}, bf16[16,3,224,128]{3,2,1,0:T(8,128)(2,1)}, u32[]{:S(2)}) copy-start(bf16[16,3,224,128]{3,2,1,0:T(8,128)(2,1)} %all-gather.2.cloned.1.call-done.pieces) | copy-start | bytes 8257540
  139.1 6.1 %collective-permute-start.6 = (bf16[8,16,224]{2,1,0:T(8,128)(2,1)S(1)}, bf16[8,16,224]{2,1,0:T(8,128)(2,1)S(1)}, u32[]{:S(2)}, u32[]{:S(2)}) collective-permute-start(bf16[8,16,224]{2,1,0:T(8,128)(2,1)S(1)} %get-tuple-element.17), channel_id=1, source_target_pairs={{0,1},{1,0},{2,3},{3,2},{4,5},{5,4},{6,7},{7,6},{8,9},{9,8},{10,11... | collective-permute-start | bytes 172040 | tf_op jit(solution)/shard_map/ppermute | solution.py:295
  146.2 9.6 %collective-permute-start.7 = (bf16[16,448]{1,0:T(8,128)(2,1)S(1)}, bf16[16,448]{1,0:T(8,128)(2,1)S(1)}, u32[]{:S(2)}, u32[]{:S(2)}) collective-permute-start(bf16[16,448]{1,0:T(8,128)(2,1)S(1)} %get-tuple-element.19), channel_id=1, source_target_pairs={{0,2},{2,4},{4,6},{6,0},{1,3},{3,5},{5,7},{7,1},{8,10},{10,12},{12... | collective-permute-start | bytes 43016 | tf_op jit(solution)/shard_map/ppermute | solution.py:304
  148.4 7.4 %collective-permute-start.8 = (bf16[16,448]{1,0:T(8,128)(2,1)S(1)}, bf16[16,448]{1,0:T(8,128)(2,1)S(1)}, u32[]{:S(2)}, u32[]{:S(2)}) collective-permute-start(bf16[16,448]{1,0:T(8,128)(2,1)S(1)} %get-tuple-element.20), channel_id=1, source_target_pairs={{0,4},{2,6},{4,0},{6,2},{1,5},{3,7},{5,1},{7,3},{8,12},{10,14},{12... | collective-permute-start | bytes 43016 | tf_op jit(solution)/shard_map/ppermute | solution.py:304
  152.1 4.5 %collective-permute-start.9 = (bf16[16,448]{1,0:T(8,128)(2,1)S(1)}, bf16[16,448]{1,0:T(8,128)(2,1)S(1)}, u32[]{:S(2)}, u32[]{:S(2)}) collective-permute-start(bf16[16,448]{1,0:T(8,128)(2,1)S(1)} %get-tuple-element.21), channel_id=1, source_target_pairs={{0,6},{2,0},{4,2},{6,4},{1,7},{3,1},{5,3},{7,5},{8,14},{10,8},{12,... | collective-permute-start | bytes 43016 | tf_op jit(solution)/shard_map/ppermute | solution.py:304
Sparse Core Ops, SparseCore 0:
  18.8 78.0 all-gather.1
